TPU v7x, 8 devices: a whole 2x2x1 slice. The times are simulated.
8 devices in a mesh: datb: 2 (over z, y), model: 2 (over x), data: 2 (over core).
Axes of the slice: x: 2, y: 2, z: 1, core: 2. Of those that a mesh axis runs over, the one named last changes fastest.
Arguments:
- tokens: bfloat16 [4096, 2048], P(('datb', 'data', 'model'))
- w_gate: bfloat16 [2048, 8192], P(('datb', 'data'), 'model')
- w_up: bfloat16 [2048, 8192], P(('datb', 'data'), 'model')
- w_down: bfloat16 [8192, 2048], P('model', ('datb', 'data'))
- grad_out: bfloat16 [4096, 2048], P(('datb', 'data', 'model'))
Outputs:
- output 1: bfloat16 [4096, 2048], P(('datb', 'data', 'model'))
- output 2: bfloat16 [4096, 2048], P(('datb', 'data', 'model'))
- output 3: float32 [2048, 8192], P(('datb', 'data'), 'model')
- output 4: float32 [2048, 8192], P(('datb', 'data'), 'model')
- output 5: float32 [8192, 2048], P('model', ('datb', 'data'))
All inputs are finite; a program needn't handle non-finite values.
Results may differ from a plain program's by a relative error of at most 0.0160102.
Values are sent between devices in bfloat16 or wider.
A program may use at most 1 GiB of HBM per device.

v0:
```python
import jax
import jax.numpy as jnp
from jax import lax
from jax.sharding import PartitionSpec as P

ROW_SPEC = P(("datb", "data", "model"), None)
GATE_SPEC = P(("datb", "data"), "model")
DOWN_SPEC = P("model", ("datb", "data"))


def solution(mesh):
    datb_size = mesh.shape["datb"]
    data_size = mesh.shape["data"]
    model_size = mesh.shape["model"]

    def local_step(tok_loc, wg_loc, wu_loc, wd_loc, grad_loc):
        rows_dev, d_model = tok_loc.shape
        d_part = wg_loc.shape[0]
        shard_rows = rows_dev * model_size

        def to_rows(part_out):
            per_model = lax.psum_scatter(part_out.reshape(data_size, model_size, rows_dev, datb_size, d_part), "model", scatter_dimension=1)
            moved_rows = lax.all_to_all(per_model[:, :, :, None, :], "data", 0, 3, tiled=True)
            return moved_rows.reshape(rows_dev, d_model)

        gate_w = lax.all_gather(wg_loc, "datb", axis=0)
        up_w = lax.all_gather(wu_loc, "datb", axis=0)
        down_w = lax.all_gather(wd_loc, "datb", axis=1)

        tok_full = lax.all_gather(tok_loc, "model", axis=0, tiled=True)
        tok_split = lax.all_to_all(tok_full.reshape(shard_rows, datb_size, data_size, d_part), "data", 2, 2, tiled=True)
        gate_part = jnp.einsum("tbae,bef->taf", tok_split, gate_w, preferred_element_type=jnp.float32).astype(jnp.bfloat16)
        up_part = jnp.einsum("tbae,bef->taf", tok_split, up_w, preferred_element_type=jnp.float32).astype(jnp.bfloat16)
        gate_pre = lax.psum_scatter(gate_part, "data", scatter_dimension=1).astype(jnp.float32)
        up_pre = lax.psum_scatter(up_part, "data", scatter_dimension=1).astype(jnp.float32)
        gate_sig = jax.nn.sigmoid(gate_pre)
        silu_gate = gate_pre * gate_sig
        hidden = (silu_gate * up_pre).astype(jnp.bfloat16)
        hid_all = lax.all_gather(hidden, "data", axis=0)
        down_part = jnp.einsum("atf,fbe->atbe", hid_all, down_w, preferred_element_type=jnp.float32).astype(jnp.bfloat16)
        out = (tok_loc.astype(jnp.float32) + to_rows(down_part).astype(jnp.float32)).astype(jnp.bfloat16)

        grad_full = lax.all_gather(grad_loc, "model", axis=0, tiled=True)
        grad_split = lax.all_to_all(grad_full.reshape(shard_rows, datb_size, data_size, d_part), "data", 2, 2, tiled=True)
        grad_hid_part = jnp.einsum("tbae,fbe->taf", grad_split, down_w, preferred_element_type=jnp.float32).astype(jnp.bfloat16)
        grad_hidden = lax.psum_scatter(grad_hid_part, "data", scatter_dimension=1).astype(jnp.float32)
        grad_gate_pre = (grad_hidden * up_pre * gate_sig * (1.0 + gate_pre * (1.0 - gate_sig))).astype(jnp.bfloat16)
        grad_up_pre = (grad_hidden * silu_gate).astype(jnp.bfloat16)
        dgate_all = lax.all_gather(grad_gate_pre, "data", axis=0)
        dup_all = lax.all_gather(grad_up_pre, "data", axis=0)
        back_part = (jnp.einsum("atf,bef->atbe", dgate_all, gate_w, preferred_element_type=jnp.float32) + jnp.einsum("atf,bef->atbe", dup_all, up_w, preferred_element_type=jnp.float32)).astype(jnp.bfloat16)
        grad_in = (grad_loc.astype(jnp.float32) + to_rows(back_part).astype(jnp.float32)).astype(jnp.bfloat16)

        grad_down = lax.psum_scatter(jnp.einsum("atf,tbae->fbe", hid_all, grad_split, preferred_element_type=jnp.float32), "datb", scatter_dimension=1)
        grad_gate = lax.psum_scatter(jnp.einsum("tbae,atf->bef", tok_split, dgate_all, preferred_element_type=jnp.float32), "datb", scatter_dimension=0)
        grad_up = lax.psum_scatter(jnp.einsum("tbae,atf->bef", tok_split, dup_all, preferred_element_type=jnp.float32), "datb", scatter_dimension=0)
        return out, grad_in, grad_gate, grad_up, grad_down

    return jax.shard_map(local_step, mesh=mesh, in_specs=(ROW_SPEC, GATE_SPEC, GATE_SPEC, DOWN_SPEC, ROW_SPEC), out_specs=(ROW_SPEC, ROW_SPEC, GATE_SPEC, GATE_SPEC, DOWN_SPEC), check_vma=False)
```

profile of v0, /device:TPU:0, one launch (start us, length us, event | category | flops | bytes accessed | tf_op | source)
XLA Modules:
  0.0 1417.7 jit_solution(10309116060381693815)
XLA Ops:
  7.2 4.1 copy.54
  11.4 0.7 all-gather.22.cloned.1.call-update
  12.1 0.7 all-gather.24.cloned.1.call-update
  12.9 2.5 copy.61
  15.4 6.3 copy.57
  21.8 46.6 %all-gather.12.cloned.1.call-done = bf16[1024,2048]{0,1:T(8,128)(2,1)} async-done(((bf16[512,2048]{0,1:T(8,128)(2,1)}), bf16[1024,2048]{0,1:T(8,128)(2,1)}) %all-gather.12.cloned.1.call-update) | async-done | bytes 4194320 | tf_op jit(solution)/shard_map/all_gather | solution.py:30
  68.5 6.2 copy.56
  74.7 11.5 all_to_all.28
  86.2 86.1 %all-gather.22.cloned.1.call-done = bf16[1024,4096]{1,0:T(8,128)(2,1)} async-done(((bf16[512,4096]{1,0:T(8,128)(2,1)}), bf16[1024,4096]{1,0:T(8,128)(2,1)}) %all-gather.22.cloned.1.call-update) | async-done | bytes 8388624 | tf_op jit(solution)/shard_map/all_gather | solution.py:26
  172.3 24.2 %bitcast_convert_fusion.2 = bf16[1024,2,4096]{2,0,1:T(8,128)(2,1)} fusion(bf16[1024,2,2,512]{3,0,1,2:T(8,128)(2,1)} %all_to_all.28, bf16[2,512,4096,1]{2,1,0,3:T(8,128)(2,1)} %bitcast.162), kind=kOutput, calls=%fused_computation.2 | convolution fusion | flops 17188257792 | bytes 29360128 | tf_op jit(solution)/shard_map/tbae,bef->taf/dot_general | solution.py:32
  196.6 79.5 %all-gather.24.cloned.1.call-done = bf16[1024,4096]{1,0:T(8,128)(2,1)} async-done(((bf16[512,4096]{1,0:T(8,128)(2,1)}), bf16[1024,4096]{1,0:T(8,128)(2,1)}) %all-gather.24.cloned.1.call-update) | async-done | bytes 8388624 | tf_op jit(solution)/shard_map/all_gather | solution.py:27
  276.1 24.2 %bitcast_convert_fusion.1 = bf16[1024,2,4096]{2,0,1:T(8,128)(2,1)} fusion(bf16[1024,2,2,512]{3,0,1,2:T(8,128)(2,1)} %all_to_all.28, bf16[2,512,4096,1]{2,1,0,3:T(8,128)(2,1)} %bitcast.164), kind=kOutput, calls=%fused_computation.1 | convolution fusion | flops 17188257792 | bytes 29360128 | tf_op jit(solution)/shard_map/tbae,bef->taf/dot_general | solution.py:33
  300.4 31.9 %all-gather.16.cloned.1.call-done = bf16[1024,2048]{0,1:T(8,128)(2,1)} async-done(((bf16[512,2048]{0,1:T(8,128)(2,1)}), bf16[1024,2048]{0,1:T(8,128)(2,1)}) %all-gather.16.cloned.1.call-update) | async-done | bytes 4194320 | tf_op jit(solution)/shard_map/all_gather | solution.py:43
  332.3 6.2 copy.63
  338.5 12.0 all_to_all.29
  350.5 86.0 %all-gather.26.cloned.1.call-done = bf16[4096,1024]{0,1:T(8,128)(2,1)} async-done(((bf16[4096,512]{0,1:T(8,128)(2,1)}), bf16[4096,1024]{0,1:T(8,128)(2,1)}) %all-gather.26.cloned.1.call-update) | async-done | bytes 8388624 | tf_op jit(solution)/shard_map/all_gather | solution.py:28
  436.5 24.2 %bitcast_convert_fusion = bf16[1024,2,4096]{2,0,1:T(8,128)(2,1)} fusion(bf16[1024,2,2,512]{3,0,1,2:T(8,128)(2,1)} %all_to_all.29, bf16[4096,2,512,1]{0,2,1,3:T(8,128)(2,1)} %bitcast.166), kind=kOutput, calls=%fused_computation | convolution fusion | flops 17188257792 | bytes 29360128 | tf_op jit(solution)/shard_map/tbae,fbe->taf/dot_general | solution.py:45
  460.8 24.9 %reduce-scatter.15.cloned.1.call-done = bf16[1024,1,4096]{2,0,1:T(8,128)(2,1)} async-done(((bf16[1024,2,4096]{2,0,1:T(8,128)(2,1)}), bf16[1024,1,4096]{2,0,1:T(8,128)(2,1)}) %reduce-scatter.15.cloned.1.call-update) | async-done | bytes 8388624 | tf_op jit(solution)/shard_map/reduce_scatter | solution.py:35
  485.7 25.3 %reduce-scatter.17.cloned.1.call-done = bf16[1024,1,4096]{2,0,1:T(8,128)(2,1)} async-done(((bf16[1024,2,4096]{2,0,1:T(8,128)(2,1)}), bf16[1024,1,4096]{2,0,1:T(8,128)(2,1)}) %reduce-scatter.17.cloned.1.call-update) | async-done | bytes 8388624 | tf_op jit(solution)/shard_map/reduce_scatter | solution.py:46
  511.0 24.1 %fusion.3 = (bf16[1,1024,4096]{2,1,0:T(8,128)(2,1)}, bf16[1,1024,4096]{2,1,0:T(8,128)(2,1)}, bf16[1,1024,4096]{2,1,0:T(8,128)(2,1)}) fusion(bf16[1024,1,4096]{2,0,1:T(8,128)(2,1)} %reduce-scatter.17.cloned.1.call-done, bf16[1024,1,4096]{2,0,1:T(8,128)(2,1)} %reduce-scatter.15.cloned.1.call-done, bf16[1024,1,4096]{2,0,1:T(8,128)(2,1)} %reduce-scatter.13.cloned.1.call-done), kind=kLoop, calls=%fused_computation.12 | loop fusion | flops 75497472 | bytes 50331648 | tf_op jit(solution)/shard_map/convert_element_type | solution.py:47
  535.7 0.7 all-gather.18.cloned.1.call-update
  536.6 27.6 %all-gather.20.cloned.1.call-done = bf16[2,1024,4096]{2,1,0:T(8,128)(2,1)} async-done(((bf16[1,1024,4096]{2,1,0:T(8,128)(2,1)}), bf16[2,1024,4096]{2,1,0:T(8,128)(2,1)}) %all-gather.20.cloned.1.call-update) | async-done | bytes 16777232 | tf_op jit(solution)/shard_map/all_gather | solution.py:50
  564.1 24.1 %fusion.11 = f32[2,1024,2,512]{3,1,2,0:T(8,128)} fusion(bf16[2,512,4096,1]{2,1,0,3:T(8,128)(2,1)} %bitcast.165, bf16[2,1024,4096]{2,1,0:T(8,128)(2,1)} %all-gather.20.cloned.1.call-done), kind=kOutput, calls=%fused_computation.20 | convolution fusion | flops 17179869184 | bytes 33554432 | tf_op jit(solution)/shard_map/atf,bef->atbe/dot_general | solution.py:51
  588.3 6.8 all-gather.14.cloned.1.call-done
  595.1 23.8 %fusion.34 = bf16[2,1024,2,512]{3,1,2,0:T(8,128)(2,1)} fusion(bf16[4096,2,512,1]{0,2,1,3:T(8,128)(2,1)} %bitcast.167, bf16[2,1024,4096]{2,1,0:T(8,128)(2,1)} %all-gather.14.cloned.1.call-done), kind=kOutput, calls=%fused_computation.38 | convolution fusion | flops 17181966336 | bytes 29360128 | tf_op jit(solution)/shard_map/atf,fbe->atbe/dot_general | solution.py:40
  618.9 7.3 all-gather.18.cloned.1.call-done
  626.2 24.4 %add_convert_fusion = bf16[2,1024,2,512]{3,1,2,0:T(8,128)(2,1)} fusion(f32[2,1024,2,512]{3,1,2,0:T(8,128)} %fusion.11, bf16[2,512,4096,1]{2,1,0,3:T(8,128)(2,1)} %bitcast.163, bf16[2,1024,4096]{2,1,0:T(8,128)(2,1)} %all-gather.18.cloned.1.call-done), kind=kOutput, calls=%fused_computation.33 | convolution fusion | flops 17184063488 | bytes 37748736 | tf_op jit(solution)/shard_map/atf,bef->atbe/dot_general | solution.py:51
  650.9 23.8 %fusion.24 = f32[2,512,4096]{1,2,0:T(8,128)} fusion(bf16[1024,2,2,512]{3,0,1,2:T(8,128)(2,1)} %all_to_all.28, bf16[2,1024,4096]{2,1,0:T(8,128)(2,1)} %all-gather.18.cloned.1.call-done), kind=kOutput, calls=%fused_computation.31 | convolution fusion | flops 17179869184 | bytes 37748736 | tf_op jit(solution)/shard_map/tbae,atf->bef/dot_general | solution.py:55
  674.8 23.8 %fusion.27 = f32[2,512,4096]{1,2,0:T(8,128)} fusion(bf16[1024,2,2,512]{3,0,1,2:T(8,128)(2,1)} %all_to_all.28, bf16[2,1024,4096]{2,1,0:T(8,128)(2,1)} %all-gather.20.cloned.1.call-done), kind=kOutput, calls=%fused_computation.32 | convolution fusion | flops 17179869184 | bytes 37748736 | tf_op jit(solution)/shard_map/tbae,atf->bef/dot_general | solution.py:56
  698.9 23.8 %fusion.21 = f32[4096,2,512]{2,0,1:T(8,128)} fusion(bf16[1024,2,2,512]{3,0,1,2:T(8,128)(2,1)} %all_to_all.29, bf16[2,1024,4096]{2,1,0:T(8,128)(2,1)} %all-gather.14.cloned.1.call-done), kind=kOutput, calls=%fused_computation.30 | convolution fusion | flops 17179869184 | bytes 37748736 | tf_op jit(solution)/shard_map/atf,tbae->fbe/dot_general | solution.py:54
  723.9 120.3 %all-reduce.5.cloned.1.call-done = (bf16[2,2,512,2,512]{4,2,1,3,0:T(8,128)(2,1)}, bf16[2,2,512,2,512]{4,2,1,3,0:T(8,128)(2,1)}) async-done(((bf16[2,2,512,2,512]{4,2,1,3,0:T(8,128)(2,1)}, bf16[2,2,512,2,512]{4,2,1,3,0:T(8,128)(2,1)}), (bf16[2,2,512,2,512]{4,2,1,3,0:T(8,128)(2,1)}, bf16[2,2,512,2,512]{4,2,1,3,0:T(8,128)(2,1)})) %all-reduce.5.cloned.1.call-update) | async-done | bytes 8388624
  844.2 2.4 dynamic-slice_bitcast_fusion
  846.6 6.3 all_to_all.30
  852.9 4.1 copy.66
  857.0 2.2 bitcast_convert_fusion.3
  859.2 2.2 fusion.30
  861.4 3.9 copy.74
  865.3 2.4 dynamic-slice_bitcast_fusion.1
  867.7 6.3 all_to_all.31
  873.9 4.1 copy.60
  878.1 2.2 bitcast_convert_fusion.4
  880.3 2.2 fusion.31
  882.5 3.9 copy.73
  886.4 146.8 %reduce-scatter.19.cloned.1.call-done = f32[1,512,4096]{1,2,0:T(8,128)} async-done(((f32[2,512,4096]{1,2,0:T(8,128)}), f32[1,512,4096]{1,2,0:T(8,128)}) %reduce-scatter.19.cloned.1.call-update) | async-done | bytes 8388624 | tf_op jit(solution)/shard_map/reduce_scatter | solution.py:55
  1033.2 8.9 copy.75
  1042.1 179.6 %reduce-scatter.21.cloned.1.call-done = f32[1,512,4096]{1,2,0:T(8,128)} async-done(((f32[2,512,4096]{1,2,0:T(8,128)}), f32[1,512,4096]{1,2,0:T(8,128)}) %reduce-scatter.21.cloned.1.call-update) | async-done | bytes 8388624 | tf_op jit(solution)/shard_map/reduce_scatter | solution.py:56
  1221.6 8.9 copy.76
  1230.5 180.2 %reduce-scatter.23.cloned.1.call-done = f32[4096,1,512]{2,0,1:T(8,128)} async-done(((f32[4096,2,512]{2,0,1:T(8,128)}), f32[4096,1,512]{2,0,1:T(8,128)}) %reduce-scatter.23.cloned.1.call-update) | async-done | bytes 8388624 | tf_op jit(solution)/shard_map/reduce_scatter | solution.py:54
  (37 shorter events, 3.2 us)
Async XLA Ops:
  7.2 5.7 copy-start.2
  7.2 61.3 %all-gather.12.cloned.1.call-start = ((), (), s32[]{:S(2)}) async-start(), calls=%async_computation.10 | async-start | bytes 6291456 | tf_op jit(solution)/shard_map/all_gather | solution.py:30
  11.3 161.0 %all-gather.22.cloned.1.call-start = ((), (), s32[]{:S(2)}) async-start(), calls=%async_computation.21 | async-start | bytes 12582912 | tf_op jit(solution)/shard_map/all_gather | solution.py:26
  12.1 264.0 %all-gather.24.cloned.1.call-start = ((), (), s32[]{:S(2)}) async-start(), calls=%async_computation.22 | async-start | bytes 12582912 | tf_op jit(solution)/shard_map/all_gather | solution.py:27
  12.8 319.5 %all-gather.16.cloned.1.call-start = ((), (), s32[]{:S(2)}) async-start(), calls=%async_computation.14 | async-start | bytes 6291456 | tf_op jit(solution)/shard_map/all_gather | solution.py:43
  15.4 421.1 %all-gather.26.cloned.1.call-start = ((), (), s32[]{:S(2)}) async-start(), calls=%async_computation.23 | async-start | bytes 12582912 | tf_op jit(solution)/shard_map/all_gather | solution.py:28
  21.8 439.0 %reduce-scatter.13.cloned.1.call-start = ((), (), s32[]{:S(2)}) async-start(), calls=%async_computation.11 | async-start | bytes 25165824 | tf_op jit(solution)/shard_map/reduce_scatter | solution.py:34
  196.5 289.2 %reduce-scatter.15.cloned.1.call-start = ((), (), s32[]{:S(2)}) async-start(), calls=%async_computation.12 | async-start | bytes 25165824 | tf_op jit(solution)/shard_map/reduce_scatter | solution.py:35
  300.3 210.6 %reduce-scatter.17.cloned.1.call-start = ((), (), s32[]{:S(2)}) async-start(), calls=%async_computation.15 | async-start | bytes 25165824 | tf_op jit(solution)/shard_map/reduce_scatter | solution.py:46
  460.7 103.4 %all-gather.20.cloned.1.call-start = ((), (), s32[]{:S(2)}) async-start(), calls=%async_computation.17 | async-start | bytes 25165824 | tf_op jit(solution)/shard_map/all_gather | solution.py:50
  535.0 60.1 %all-gather.14.cloned.1.call-start = ((), (), s32[]{:S(2)}) async-start(), calls=%async_computation.13 | async-start | bytes 25165824 | tf_op jit(solution)/shard_map/all_gather | solution.py:39
  535.6 90.6 %all-gather.18.cloned.1.call-start = ((), (), s32[]{:S(2)}) async-start(), calls=%async_computation.16 | async-start | bytes 25165824 | tf_op jit(solution)/shard_map/all_gather | solution.py:49
  536.4 307.9 %all-reduce.5.cloned.1.call-start = ((), (), s32[]{:S(2)}) async-start(), calls=%async_computation.24 | async-start | bytes 16777216
  650.7 382.5 %reduce-scatter.19.cloned.1.call-start = ((), (), s32[]{:S(2)}) async-start(), calls=%async_computation.18 | async-start | bytes 25165824 | tf_op jit(solution)/shard_map/reduce_scatter | solution.py:55
  674.7 546.9 %reduce-scatter.21.cloned.1.call-start = ((), (), s32[]{:S(2)}) async-start(), calls=%async_computation.19 | async-start | bytes 25165824 | tf_op jit(solution)/shard_map/reduce_scatter | solution.py:56
  698.6 712.1 %reduce-scatter.23.cloned.1.call-start = ((), (), s32[]{:S(2)}) async-start(), calls=%async_computation.20 | async-start | bytes 25165824 | tf_op jit(solution)/shard_map/reduce_scatter | solution.py:54
  722.6 0.7 copy-start.3
  846.6 12.6 copy-start.1
  867.7 12.6 copy-start
Sparse Core Ops, SparseCore 0:
  11.4 57.0 all-gather.11
  70.0 102.2 all-gather.21
  173.8 102.2 all-gather.23
  278.0 54.1 all-gather.15
  334.2 102.2 all-gather.25
  438.6 21.7 reduce-scatter.12
  462.7 22.9 reduce-scatter.14
  488.0 22.9 reduce-scatter.16
  535.2 28.9 all-gather.19
  566.1 28.9 all-gather.13
  597.2 28.9 all-gather.17
  650.8 193.3 all-reduce.4
  846.5 186.6 reduce-scatter.18
  1035.3 186.2 reduce-scatter.20
  1224.3 186.3 reduce-scatter.22
where the time goes:
time: 1430 us; the launch traced here: 1420 us
  waiting for transfers between devices  1050 us (73%)
  matrix products  216 us (15%)
  local copies, waits for them, and re-layouts  65.2 us (5%)
  blocking collectives  36 us (3%)
  other arithmetic  32.8 us (2%)
  between operations  14.5 us (1%)
    reduce_scatter x1, waiting for transfers between devices, local_step(): lax.psum_scatter(jnp.einsum('atf,tbae->fbe', hid_all, grad_split, preferr...  180 us
    reduce_scatter x1, waiting for transfers between devices, local_step(): lax.psum_scatter(jnp.einsum('tbae,atf->bef', tok_split, dup_all, preferre...  180 us
    reduce_scatter x1, waiting for transfers between devices, local_step(): lax.psum_scatter(jnp.einsum('tbae,atf->bef', tok_split, dgate_all, prefer...  147 us
    unnamed x16, waiting for transfers between devices  123 us
    all_gather x1, waiting for transfers between devices, local_step(): gate_w = lax.all_gather(wg_loc, 'datb', axis=0)  86.1 us
    all_gather x1, waiting for transfers between devices, local_step(): down_w = lax.all_gather(wd_loc, 'datb', axis=1)  86 us
    all_gather x1, waiting for transfers between devices, local_step(): up_w = lax.all_gather(wu_loc, 'datb', axis=0)  79.5 us
    all_gather x1, waiting for transfers between devices, local_step(): tok_full = lax.all_gather(tok_loc, 'model', axis=0, tiled=True)  46.6 us
  transfers between devices with their start and end apart: 15, of which 14 were waited for; matrix products, arithmetic and copies ran while one was open for 18% of the time, Pallas kernels for 0%

commit v1 on v0

v1 whole, which is shorter than its diff:
```python
import functools

import jax
import jax.numpy as jnp
from jax import lax
from jax.experimental import pallas as pl
from jax.experimental.pallas import tpu as pltpu
from jax.sharding import PartitionSpec as P


ROW_SPEC = P(("datb", "data", "model"), None)
GATE_SPEC = P(("datb", "data"), "model")
DOWN_SPEC = P("model", ("datb", "data"))
AXES = ("datb", "model", "data")
CHUNKS = 4
OWN_TILE = 256
LIMIT = 62 * 1024 * 1024
bf16, f32 = jnp.bfloat16, jnp.float32
ANY = pl.BlockSpec(memory_space=pl.ANY)


def mm(a, b, ca=1, cb=0):
    return lax.dot_general(a, b, (((ca,), (cb,)), ((), ())), preferred_element_type=f32)


def activations(x, dy, wg, wu, wd):
    a = mm(x, wg).astype(bf16).astype(f32)
    b = mm(x, wu).astype(bf16).astype(f32)
    g = mm(dy, wd, 1, 1).astype(bf16).astype(f32)
    sig = jax.nn.sigmoid(a)
    silu = a * sig
    h = (silu * b).astype(bf16)
    da = (g * b * sig * (1.0 + a * (1.0 - sig))).astype(bf16)
    db = (g * silu).astype(bf16)
    return h, da, db


def own_kernel(first, last, half, *refs):
    x_ref, dy_ref, *refs = refs
    pieces, refs = refs[:4], refs[4:]
    if not first:
        (y_in, dx_in), refs = refs[:2], refs[8:]
    sums, (wg, wu, wd, dg, du, dd) = refs[:-6], refs[-6:]
    part = pieces[0].shape[1]
    r = pl.program_id(0)

    @pl.when(r == 0)
    def _():
        for i, piece in enumerate(pieces):
            wg[0, i * part:(i + 1) * part, :] = piece[0]
            wu[0, i * part:(i + 1) * part, :] = piece[1]
            wd[0, :, i * part:(i + 1) * part] = piece[2]
        dg[...] = jnp.zeros_like(dg)
        du[...] = jnp.zeros_like(du)
        dd[...] = jnp.zeros_like(dd)

    x, dy = x_ref[...], dy_ref[...]
    h, da, db = activations(x, dy, wg[0], wu[0], wd[0])
    y = mm(h, wd[0])
    dx = mm(da, wg[0], 1, 1) + mm(db, wu[0], 1, 1)
    if not first:
        y, dx = y + y_in[...], dx + dx_in[...]
    if last:
        y_keep, dx_keep, y_send, dx_send = sums
        keep = pl.num_programs(0) // 2

        @pl.when(r < keep)
        def _():
            y_keep[...] = y
            dx_keep[...] = dx

        @pl.when(r >= keep)
        def _():
            y_send[...] = y.astype(bf16)
            dx_send[...] = dx.astype(bf16)
    else:
        y_out, dx_out = sums
        y_out[...] = y
        dx_out[...] = dx
    dg[...] += mm(x[:, :half], da, 0, 0)
    du[...] += mm(x[:, :half], db, 0, 0)
    dd[...] += mm(h, dy[:, :half], 0, 0)


def grad_kernel(half, x_ref, dy_ref, wg, wu, wd, dg_in, du_in, dd_in, dg, du, dd):
    @pl.when(pl.program_id(1) == 0)
    def _():
        dg[...] = dg_in[...]
        du[...] = du_in[...]
        dd[...] = dd_in[...]

    x, dy = x_ref[...], dy_ref[...]
    h, da, db = activations(x, dy, wg[0], wu[0], wd[0])
    dg[...] += mm(x[:, :half], da, 0, 0)
    du[...] += mm(x[:, :half], db, 0, 0)
    dd[...] += mm(h, dy[:, :half], 0, 0)


def last_kernel(half, fresh, core, x_ref, dy_ref, wg, wu, wd, dg_in, du_in, dd_in, *refs):
    refs = refs if fresh else refs[3:]
    gate, up, down, gate_send, up_send, down_send = refs
    part = half // 2
    x, dy = x_ref[...], dy_ref[...]
    h, da, db = activations(x, dy, wg[0], wu[0], wd[0])
    dg = dg_in[...] + mm(x[:, :half], da, 0, 0)
    gate[...] = dg[:part]
    gate_send[...] = dg[part:]
    du = du_in[...] + mm(x[:, :half], db, 0, 0)
    up[...] = du[:part]
    up_send[...] = du[part:]
    dd = dd_in[...] + mm(h, dy[:, :half], 0, 0)
    down[...] = dd[:, :part]
    down_send[...] = dd[:, part:]


def gather_kernel(masks, *refs):
    *srcs, out = refs
    part = out.shape[2] // 4
    for n, (src, mask) in enumerate(zip(srcs, masks)):
        for i in range(4):
            out[n, :, (i ^ mask) * part:((i ^ mask) + 1) * part] = src[:, i * part:(i + 1) * part]


def gather_rows(blocks, masks):
    count, (rows, cols) = len(blocks), blocks[0].shape
    tile = 64
    out = pl.pallas_call(
        functools.partial(gather_kernel, masks),
        grid=(rows // tile,),
        in_specs=[pl.BlockSpec((tile, cols), lambda t: (t, 0))] * count,
        out_specs=pl.BlockSpec((count, tile, cols), lambda t: (0, t, 0)),
        out_shape=jax.ShapeDtypeStruct((count, rows, cols), blocks[0].dtype),
        cost_estimate=pl.CostEstimate(flops=1000000, bytes_accessed=2 * count * rows * cols * 2, transcendentals=0),
    )(*blocks)
    return out.reshape(count * rows, cols)


def solution(mesh):
    def flip(value, names):
        mask = sum(4 >> AXES.index(name) for name in names)
        return lax.ppermute(value, AXES, [(i, i ^ mask) for i in range(8)])

    def quarters(value, order):
        part = value.shape[1] // 4
        return jnp.concatenate([value[:, i * part:(i + 1) * part] for i in order], axis=1)

    def local_step(tok, wg, wu, wd, dy):
        rows, d_model = tok.shape
        part = d_model // 4
        half = d_model // 2
        ff = wg.shape[1] // 2
        width = ff // CHUNKS
        core = lax.axis_index("data")
        place = 2 * lax.axis_index("datb") + core
        once = pl.Buffered(1)

        def relative(value):
            return jnp.concatenate([lax.dynamic_slice(value, (0, (place ^ i) * part), (value.shape[0], part)) for i in range(4)], axis=1)

        def pieces(which, j):
            start = which * ff + j * width
            gate = lax.dynamic_slice(wg, (0, start), (part, width))
            up = lax.dynamic_slice(wu, (0, start), (part, width))
            down = lax.dynamic_slice(wd, (start, 0), (width, part))
            return lax.optimization_barrier(jnp.stack([gate, up, down]))

        tok_r, dy_r = lax.optimization_barrier((relative(tok), relative(dy)))
        weights = []
        for j in range(CHUNKS):
            same, other = pieces(core, j), pieces(1 - core, j)
            weights.append((same, flip(other, ["data"]), flip(same, ["datb"]), flip(other, ["datb", "data"])))
        tok_x = flip(tok_r, ["model"])
        dy_x = flip(dy_r, ["model"])
        x_own = gather_rows([tok_r, tok_x, flip(tok_r, ["data"]), flip(tok_x, ["data"])], (0, 0, 1, 1))
        dy_own = gather_rows([dy_r, dy_x, flip(dy_r, ["data"]), flip(dy_x, ["data"])], (0, 0, 1, 1))

        early = rows // 2

        def near_far(direct, crossed):
            blocks, masks = [], []
            for block in (direct, crossed):
                if block is not None:
                    blocks += [block, flip(block, ["data"])]
                    masks += [2, 3]
            return gather_rows(blocks, tuple(masks))

        tok_y = flip(tok_r[:early], ["datb"])
        dy_y = flip(dy_r[:early], ["datb"])
        x_ext = near_far(tok_y, flip(tok_y, ["model"]))
        dy_ext = near_far(dy_y, flip(dy_y, ["model"]))
        late_tok = flip(tok_r[early:], ["datb"])
        late_dy = flip(dy_r[early:], ["datb"])
        late_tok_x = flip(tok_x[early:], ["datb"])
        late_dy_x = flip(dy_x[early:], ["datb"])

        w_shapes = [jax.ShapeDtypeStruct((CHUNKS, d_model, width), bf16)] * 2 + [jax.ShapeDtypeStruct((CHUNKS, width, d_model), bf16)]
        d_shapes = [jax.ShapeDtypeStruct((half, ff), f32)] * 2 + [jax.ShapeDtypeStruct((ff, half), f32)]
        params = pltpu.CompilerParams(vmem_limit_bytes=LIMIT)

        def grow(x_rows, dy_rows, carry, chunks):
            start, tile = chunks[0], 512
            row_block = pl.BlockSpec((tile, d_model), lambda j, r: (r, 0))
            specs = [pl.BlockSpec((1, d_model, width), lambda j, r: (start + j, 0, 0))] * 2 + [pl.BlockSpec((1, width, d_model), lambda j, r: (start + j, 0, 0))]
            d_specs = [pl.BlockSpec((half, width), lambda j, r: (0, start + j))] * 2 + [pl.BlockSpec((width, half), lambda j, r: (start + j, 0))]
            grads = pl.pallas_call(
                functools.partial(grad_kernel, half),
                grid=(len(chunks), x_rows.shape[0] // tile),
                in_specs=[row_block] * 2 + specs + d_specs,
                out_specs=d_specs,
                out_shape=d_shapes,
                input_output_aliases={5 + i: i for i in range(3)},
                compiler_params=params,
                cost_estimate=pl.CostEstimate(flops=9 * x_rows.shape[0] * d_model * width * len(chunks), bytes_accessed=50 << 20, transcendentals=0),
            )(x_rows, dy_rows, *carry)
            return [*carry[:3], *grads]

        own_count = 4 * rows
        keep = own_count // OWN_TILE // 2
        for j in range(CHUNKS):
            first, last = j == 0, j == CHUNKS - 1
            row_block = pl.BlockSpec((OWN_TILE, d_model), lambda r: (r, 0))
            piece_block = pl.BlockSpec((3, part, width), lambda r: (0, 0, 0), pipeline_mode=once)
            carry_specs = [pl.BlockSpec((1, d_model, width), lambda r, j=j: (j, 0, 0), pipeline_mode=once)] * 2 + [pl.BlockSpec((1, width, d_model), lambda r, j=j: (j, 0, 0), pipeline_mode=once)] + [pl.BlockSpec((half, width), lambda r, j=j: (0, j), pipeline_mode=once)] * 2 + [pl.BlockSpec((width, half), lambda r, j=j: (j, 0), pipeline_mode=once)]
            if last:
                sum_specs = [pl.BlockSpec((OWN_TILE, d_model), lambda r: (jnp.minimum(r, keep - 1), 0))] * 2 + [pl.BlockSpec((OWN_TILE, d_model), lambda r: (jnp.maximum(r - keep, 0), 0))] * 2
                sum_shapes = [jax.ShapeDtypeStruct((own_count // 2, d_model), f32)] * 2 + [jax.ShapeDtypeStruct((own_count // 2, d_model), bf16)] * 2
            else:
                sum_specs = [row_block] * 2
                sum_shapes = [jax.ShapeDtypeStruct((own_count, d_model), f32)] * 2
            aliases = {} if first else {8 + i: len(sum_specs) + i for i in range(6)}
            if not first and not last:
                aliases |= {6: 0, 7: 1}
            outs = pl.pallas_call(
                functools.partial(own_kernel, first, last, half),
                grid=(own_count // OWN_TILE,),
                in_specs=[row_block] * 2 + [piece_block] * 4 + ([] if first else [row_block] * 2 + [ANY] * 6),
                out_specs=sum_specs + carry_specs,
                out_shape=sum_shapes + w_shapes + d_shapes,
                input_output_aliases=aliases,
                compiler_params=params,
                cost_estimate=pl.CostEstimate(flops=15 * own_count * d_model * width, bytes_accessed=100 << 20, transcendentals=0),
            )(x_own, dy_own, *weights[j], *([] if first else [*sums, *carry]))
            sums, carry = outs[:len(sum_specs)], list(outs[len(sum_specs):])
            if 0 < j < CHUNKS - 1:
                carry = grow(x_ext, dy_ext, carry, (j - 1,))
        y_keep, dx_keep, y_send, dx_send = sums

        def scatter(kept, sent, residual):
            near = flip(sent, ["data"])
            far_part = lax.optimization_barrier((kept[rows:] + quarters(near[rows:], (1, 0, 3, 2)).astype(f32)).astype(bf16))
            far = flip(far_part, ["model"])
            return relative((residual.astype(f32) + kept[:rows] + quarters(near[:rows], (1, 0, 3, 2)).astype(f32) + far.astype(f32)).astype(bf16))

        out = scatter(y_keep, y_send, tok_r)
        grad_in = scatter(dx_keep, dx_send, dy_r)

        for j in (CHUNKS - 2, CHUNKS - 1):
            carry = grow(x_ext, dy_ext, carry, (j,))
        carry = grow(near_far(late_tok, None), near_far(late_dy, None), carry, tuple(range(CHUNKS)))

        x_rows, dy_rows = near_far(late_tok_x, None), near_far(late_dy_x, None)
        finals, sends = None, []
        group = CHUNKS // 2
        for start in range(0, CHUNKS, group):
            row_block = pl.BlockSpec((512, d_model), lambda j, c: (0, 0))
            w_specs = [pl.BlockSpec((1, d_model, width), lambda j, c, s=start: (s + j, 0, 0))] * 2 + [pl.BlockSpec((1, width, d_model), lambda j, c, s=start: (s + j, 0, 0))]
            d_specs = [pl.BlockSpec((half, width), lambda j, c, s=start: (0, s + j))] * 2 + [pl.BlockSpec((width, half), lambda j, c, s=start: (s + j, 0))]
            f_specs = [pl.BlockSpec((part, width), lambda j, c, s=start: (0, c[0] * CHUNKS + s + j))] * 2 + [pl.BlockSpec((width, part), lambda j, c, s=start: (c[0] * CHUNKS + s + j, 0))]
            s_specs = [pl.BlockSpec((part, width), lambda j, c: (0, j))] * 2 + [pl.BlockSpec((width, part), lambda j, c: (j, 0))]
            fresh = finals is None
            outs = pl.pallas_call(
                functools.partial(last_kernel, half, fresh),
                grid_spec=pltpu.PrefetchScalarGridSpec(
                    num_scalar_prefetch=1,
                    grid=(group,),
                    in_specs=[row_block] * 2 + w_specs + d_specs + ([] if fresh else [ANY] * 3),
                    out_specs=f_specs + s_specs,
                ),
                out_shape=[jax.ShapeDtypeStruct((part, 2 * ff), f32)] * 2 + [jax.ShapeDtypeStruct((2 * ff, part), f32)] + [jax.ShapeDtypeStruct((part, group * width), f32)] * 2 + [jax.ShapeDtypeStruct((group * width, part), f32)],
                input_output_aliases={} if fresh else {9 + i: i for i in range(3)},
                compiler_params=params,
                cost_estimate=pl.CostEstimate(flops=9 * 512 * d_model * width * group, bytes_accessed=50 << 20, transcendentals=0),
            )(core.reshape(1), x_rows, dy_rows, *carry, *([] if fresh else finals))
            finals = outs[:3]
            sends.append([flip(v, ["data"]) for v in outs[3:]])
        grad_gate, grad_up, grad_down = finals
        for n, (got_g, got_u, got_d) in enumerate(sends):
            at = (1 - core) * ff + n * group * width
            grad_gate = lax.dynamic_update_slice(grad_gate, got_g, (0, at))
            grad_up = lax.dynamic_update_slice(grad_up, got_u, (0, at))
            grad_down = lax.dynamic_update_slice(grad_down, got_d, (at, 0))
        return out, grad_in, grad_gate, grad_up, grad_down

    return jax.shard_map(local_step, mesh=mesh, in_specs=(ROW_SPEC, GATE_SPEC, GATE_SPEC, DOWN_SPEC, ROW_SPEC), out_specs=(ROW_SPEC, ROW_SPEC, GATE_SPEC, GATE_SPEC, DOWN_SPEC), check_vma=False)
```

time: 1430 us -> 751 us (0.53)
  waiting for transfers between devices: 1050 us -> 287 us
  Pallas kernels: 0 us -> 378 us
  matrix products: 216 us -> 0 us
  blocking collectives: 36 us -> 0 us
  local copies, waits for them, and re-layouts: 65.2 us -> 29.7 us
  starting transfers between devices: 1.24 us -> 30.4 us
    reduce_scatter x6 -> x0, waiting for transfers between devices: 557 us -> none  [the longest x1 180 us: local_step(): lax.psum_scatter(jnp.einsum('atf,tbae->fbe', hid_all, grad_split, preferr...]
    pallas_call x0 -> x19, Pallas kernels: none -> 378 us  [the longest x4 187 us: local_step(): pl.pallas_call(functools.partial(own_kernel, first, last, half), grid=(ow...]
    all_gather x8 -> x0, waiting for transfers between devices: 372 us -> none  [the longest x1 86.1 us: local_step(): gate_w = lax.all_gather(wg_loc, 'datb', axis=0)]
    ppermute x0 -> x44, waiting for transfers between devices: none -> 287 us  [flip(): return lax.ppermute(value, AXES, [(i, i ^ mask) for i in range(8)])]
    dot_general x9 -> x0, matrix products: 216 us -> none  [the longest x1 24.4 us: local_step(): jnp.einsum('atf,bef->atbe', dgate_all, gate_w, preferred_element_type=jnp...]
    unnamed x16 -> x0, waiting for transfers between devices: 123 us -> none
    unnamed x16 -> x40, local copies, waits for them, and re-layouts: 39.7 us -> 2.39 us
    all_to_all x4 -> x0, blocking collectives: 36 us -> none  [the longest x2 12.5 us: to_rows(): lax.all_to_all(per_model[:, :, :, None, :], 'data', 0, 3, tiled=True)]
  transfers between devices with their start and end apart: 15 -> 44, of which waited for: 14 -> 14; matrix products, arithmetic and copies ran while one was open for 18% -> 5% of each run, Pallas kernels for 0% -> 51%
where the time goes in v1:
time: 751 us; the launch traced here: 746 us
  Pallas kernels  378 us (50%)
  waiting for transfers between devices  287 us (38%)
  starting transfers between devices  30.4 us (4%)
  local copies, waits for them, and re-layouts  29.7 us (4%)
  other arithmetic  20.2 us (3%)
    ppermute x44, waiting for transfers between devices, flip(): return lax.ppermute(value, AXES, [(i, i ^ mask) for i in range(8)])  287 us
    pallas_call x4, Pallas kernels, local_step(): pl.pallas_call(functools.partial(own_kernel, first, last, half), grid=(ow...  187 us
    pallas_call x5, Pallas kernels, grow(): pl.pallas_call(functools.partial(grad_kernel, half), grid=(len(chunks), x...  108 us
    pallas_call x8, Pallas kernels, gather_rows(): pl.pallas_call(functools.partial(gather_kernel, masks), grid=(rows // til...  42.2 us
    pallas_call x2, Pallas kernels, local_step(): pl.pallas_call(functools.partial(last_kernel, half, fresh), grid_spec=plt...  41 us
    ppermute x44, starting transfers between devices, flip(): return lax.ppermute(value, AXES, [(i, i ^ mask) for i in range(8)])  30.4 us
  transfers between devices with their start and end apart: 44, of which 14 were waited for; matrix products, arithmetic and copies ran while one was open for 5% of the time, Pallas kernels for 51%

profile of v1, /device:TPU:0, one launch (start us, length us, event | category | flops | bytes accessed | tf_op | source)
XLA Modules:
  0.0 746.3 jit_solution(4283251742887141245)
XLA Ops:
  0.7 2.5 constant_dynamic-slice_fusion.11
  3.9 3.4 collective-permute-start.18
  7.4 2.0 collective-permute-start.3
  9.5 21.8 %collective-permute-done.18.refs_0_ = bf16[256,2048]{1,0:T(8,128)(2,1)S(1)} collective-permute-done((bf16[256,2048]{1,0:T(8,128)(2,1)S(1)}, bf16[256,2048]{1,0:T(8,128)(2,1)S(1)}, u32[]{:S(2)}, u32[]{:S(2)}) %collective-permute-start.18) | collective-permute-done | bytes 1048608 | tf_op jit(solution)/shard_map/ppermute | solution.py:141
  31.3 2.0 collective-permute-start.34
  33.3 20.4 %collective-permute-done.22.refs_0_ = bf16[256,2048]{1,0:T(8,128)(2,1)S(1)} collective-permute-done((bf16[256,2048]{1,0:T(8,128)(2,1)S(1)}, bf16[256,2048]{1,0:T(8,128)(2,1)S(1)}, u32[]{:S(2)}, u32[]{:S(2)}) %collective-permute-start.22) | collective-permute-done | bytes 1048608 | tf_op jit(solution)/shard_map/ppermute | solution.py:141
  53.7 2.0 collective-permute-start.36
  55.7 20.4 %collective-permute-done.34.refs_0_ = bf16[256,2048]{1,0:T(8,128)(2,1)S(1)} collective-permute-done((bf16[256,2048]{1,0:T(8,128)(2,1)S(1)}, bf16[256,2048]{1,0:T(8,128)(2,1)S(1)}, u32[]{:S(2)}, u32[]{:S(2)}) %collective-permute-start.34) | collective-permute-done | bytes 1048608 | tf_op jit(solution)/shard_map/ppermute | solution.py:141
  76.2 2.0 collective-permute-start.20
  78.2 19.7 %collective-permute-done.36.refs_0_ = bf16[256,2048]{1,0:T(8,128)(2,1)} collective-permute-done((bf16[256,2048]{1,0:T(8,128)(2,1)S(1)}, bf16[256,2048]{1,0:T(8,128)(2,1)}, u32[]{:S(2)}, u32[]{:S(2)}) %collective-permute-start.36) | collective-permute-done | bytes 1048608 | tf_op jit(solution)/shard_map/ppermute | solution.py:141
  97.9 1.7 collective-permute-start.24
  102.2 21.3 %collective-permute-done.20.refs_2_ = bf16[256,2048]{1,0:T(8,128)(2,1)} collective-permute-done((bf16[256,2048]{1,0:T(8,128)(2,1)S(1)}, bf16[256,2048]{1,0:T(8,128)(2,1)}, u32[]{:S(2)}, u32[]{:S(2)}) %collective-permute-start.20) | collective-permute-done | bytes 1048608 | tf_op jit(solution)/shard_map/ppermute | solution.py:141
  124.0 20.5 %collective-permute-done.24.refs_2_ = bf16[256,2048]{1,0:T(8,128)(2,1)} collective-permute-done((bf16[256,2048]{1,0:T(8,128)(2,1)S(1)}, bf16[256,2048]{1,0:T(8,128)(2,1)}, u32[]{:S(2)}, u32[]{:S(2)}) %collective-permute-start.24) | collective-permute-done | bytes 1048608 | tf_op jit(solution)/shard_map/ppermute | solution.py:141
  146.6 4.2 dynamic-slice_bitcast_fusion
  154.1 1.7 collective-permute-start.16
  165.0 2.3 slice.141
  167.4 3.9 shard_map.104
  171.3 3.8 shard_map.105
  175.1 4.7 shard_map.96
  179.7 4.7 shard_map.97
  184.4 8.8 %shard_map.93 = bf16[4,512,2048]{2,1,0:T(8,128)(2,1)} custom-call(bf16[512,2048]{1,0:T(8,128)(2,1)} %copy-done.2, bf16[512,2048]{1,0:T(8,128)(2,1)} %collective-permute-done.3.refs_1_, bf16[512,2048]{1,0:T(8,128)(2,1)} %copy-done.7, bf16[512,2048]{1,0:T(8,128)(2,1)} %collective-permute-done.5.refs_3_), custom_call_target="tpu_custom_call" | custom-call | flops 1000000 | bytes 16777216 | tf_op jit(solution)/shard_map/pallas_call | solution.py:127
  195.1 8.8 %shard_map.92 = bf16[4,512,2048]{2,1,0:T(8,128)(2,1)} custom-call(bf16[512,2048]{1,0:T(8,128)(2,1)} %copy-done, bf16[512,2048]{1,0:T(8,128)(2,1)} %copy-done.4, bf16[512,2048]{1,0:T(8,128)(2,1)} %collective-permute-done.1.refs_2_, bf16[512,2048]{1,0:T(8,128)(2,1)} %collective-permute-done.2.refs_3_), custom_call_target="tpu_custom_call" | custom-call | flops 1000000 | bytes 16777216 | tf_op jit(solution)/shard_map/pallas_call | solution.py:127
  204.4 20.2 %collective-permute-done.17.refs_5_ = bf16[3,512,512]{2,1,0:T(8,128)(2,1)} collective-permute-done((bf16[3,512,512]{2,1,0:T(8,128)(2,1)}, bf16[3,512,512]{2,1,0:T(8,128)(2,1)}, u32[]{:S(2)}, u32[]{:S(2)}) %collective-permute-start.17) | collective-permute-done | bytes 1572896 | tf_op jit(solution)/shard_map/ppermute | solution.py:141
  226.1 43.0 %shard_map.94 = (f32[2048,2048]{1,0:T(8,128)}, f32[2048,2048]{1,0:T(8,128)}, bf16[4,2048,512]{2,1,0:T(8,128)(2,1)}, bf16[4,2048,512]{2,1,0:T(8,128)(2,1)}, bf16[...) custom-call(bf16[2048,2048]{1,0:T(8,128)(2,1)} %bitcast.77, ...), custom_call_target="tpu_custom_call" | custom-call | flops 32212254720 | bytes 104857600 | tf_op jit(solution)/shard_map/pallas_call | solution.py:233
  269.6 56.9 %collective-permute-done.13.refs_4_ = bf16[3,512,512]{2,1,0:T(8,128)(2,1)} collective-permute-done((bf16[3,512,512]{2,1,0:T(8,128)(2,1)S(1)}, bf16[3,512,512]{2,1,0:T(8,128)(2,1)}, u32[]{:S(2)}, u32[]{:S(2)}) %collective-permute-start.13) | collective-permute-done | bytes 1572896 | tf_op jit(solution)/shard_map/ppermute | solution.py:141
  326.5 1.7 collective-permute-start.30
  328.5 46.6 %shard_map.95 = (f32[2048,2048]{1,0:T(8,128)}, f32[2048,2048]{1,0:T(8,128)}, bf16[4,2048,512]{2,1,0:T(8,128)(2,1)}, bf16[4,2048,512]{2,1,0:T(8,128)(2,1)}, bf16[...) custom-call(bf16[2048,2048]{1,0:T(8,128)(2,1)} %bitcast.78, ...), custom_call_target="tpu_custom_call", output_to_operand_aliasing={{2}: (8, {}), {3}: (9, {}), {4}: (10, {}), {5}: (11, {}), {... | custom-call | flops 32212254720 | bytes 104857600 | tf_op jit(solution)/shard_map/pallas_call | solution.py:233
  375.2 19.0 %shard_map.98 = (f32[1024,2048]{1,0:T(8,128)}, f32[1024,2048]{1,0:T(8,128)}, f32[2048,1024]{1,0:T(8,128)}) custom-call(bf16[1024,2048]{1,0:T(8,128)(2,1)} %bitcast.57, bf16[1024,2048]{1,0:T(8,128)(2,1)} %bitcast.61, bf16[4,2048,512]{2,1,0:T(8,128)(2,1)} %get-tuple-element.80.wg.refs_8_, ...), custom_call_target="tpu_custom_call", output_to_operand_aliasing={{0}: (5, {}), {1}: (6, {}), {2}: (7, {})} | custom-call | flops 9663676416 | bytes 52428800 | tf_op jit(solution)/shard_map/pallas_call | solution.py:205
  394.2 1.8 collective-permute-start.8
  396.3 8.8 %collective-permute-done.32.refs_0_ = bf16[256,2048]{1,0:T(8,128)(2,1)} collective-permute-done((bf16[256,2048]{1,0:T(8,128)(2,1)}, bf16[256,2048]{1,0:T(8,128)(2,1)}, u32[]{:S(2)}, u32[]{:S(2)}) %collective-permute-start.32) | collective-permute-done | bytes 1048608 | tf_op jit(solution)/shard_map/ppermute | solution.py:141
  405.1 46.7 %shard_map.99 = (f32[2048,2048]{1,0:T(8,128)}, f32[2048,2048]{1,0:T(8,128)}, bf16[4,2048,512]{2,1,0:T(8,128)(2,1)}, bf16[4,2048,512]{2,1,0:T(8,128)(2,1)}, bf16[...) custom-call(bf16[2048,2048]{1,0:T(8,128)(2,1)} %bitcast.79, ...), custom_call_target="tpu_custom_call", output_to_operand_aliasing={{2}: (8, {}), {3}: (9, {}), {4}: (10, {}), {5}: (11, {}), {... | custom-call | flops 32212254720 | bytes 104857600 | tf_op jit(solution)/shard_map/pallas_call | solution.py:233
  451.8 19.1 %shard_map.100 = (f32[1024,2048]{1,0:T(8,128)}, f32[1024,2048]{1,0:T(8,128)}, f32[2048,1024]{1,0:T(8,128)}) custom-call(bf16[1024,2048]{1,0:T(8,128)(2,1)} %bitcast.58, bf16[1024,2048]{1,0:T(8,128)(2,1)} %bitcast.62, bf16[4,2048,512]{2,1,0:T(8,128)(2,1)} %get-tuple-element.91.wg.refs_8_, ...), custom_call_target="tpu_custom_call", output_to_operand_aliasing={{0}: (5, {}), {1}: (6, {}), {2}: (7, {})} | custom-call | flops 9663676416 | bytes 52428800 | tf_op jit(solution)/shard_map/pallas_call | solution.py:205
  472.0 50.5 %shard_map.101 = (f32[1024,2048]{1,0:T(8,128)}, f32[1024,2048]{1,0:T(8,128)}, bf16[1024,2048]{1,0:T(8,128)(2,1)}, bf16[1024,2048]{1,0:T(8,128)(2,1)}, bf16[4,204...) custom-call(bf16[2048,2048]{1,0:T(8,128)(2,1)} %bitcast.80, ...), custom_call_target="tpu_custom_call", output_to_operand_aliasing={{4}: (8, {}), {5}: (9, {}), {6}: (10, {}), {7}: (11, {}), {... | custom-call | flops 32212254720 | bytes 104857600 | tf_op jit(solution)/shard_map/pallas_call | solution.py:233
  523.1 18.8 %shard_map.106 = (f32[1024,2048]{1,0:T(8,128)}, f32[1024,2048]{1,0:T(8,128)}, f32[2048,1024]{1,0:T(8,128)}) custom-call(bf16[1024,2048]{1,0:T(8,128)(2,1)} %bitcast.59, bf16[1024,2048]{1,0:T(8,128)(2,1)} %bitcast.63, bf16[4,2048,512]{2,1,0:T(8,128)(2,1)} %get-tuple-element.104.wg, ...), custom_call_target="tpu_custom_call", output_to_operand_aliasing={{0}: (5, {}), {1}: (6, {}), {2}: (7, {})} | custom-call | flops 9663676416 | bytes 52428800 | tf_op jit(solution)/shard_map/pallas_call | solution.py:205
  541.9 18.6 %shard_map.107 = (f32[1024,2048]{1,0:T(8,128)}, f32[1024,2048]{1,0:T(8,128)}, f32[2048,1024]{1,0:T(8,128)}) custom-call(bf16[1024,2048]{1,0:T(8,128)(2,1)} %bitcast.60, bf16[1024,2048]{1,0:T(8,128)(2,1)} %bitcast.64, bf16[4,2048,512]{2,1,0:T(8,128)(2,1)} %get-tuple-element.104.wg, ...), custom_call_target="tpu_custom_call", output_to_operand_aliasing={{0}: (5, {}), {1}: (6, {}), {2}: (7, {})} | custom-call | flops 9663676416 | bytes 52428800 | tf_op jit(solution)/shard_map/pallas_call | solution.py:205
  560.4 32.2 %shard_map.108 = (f32[1024,2048]{1,0:T(8,128)}, f32[1024,2048]{1,0:T(8,128)}, f32[2048,1024]{1,0:T(8,128)}) custom-call(bf16[512,2048]{1,0:T(8,128)(2,1)} %bitcast.81, bf16[512,2048]{1,0:T(8,128)(2,1)} %bitcast.82, bf16[4,2048,512]{2,1,0:T(8,128)(2,1)} %get-tuple-element.104.wg, ...), custom_call_target="tpu_custom_call", output_to_operand_aliasing={{0}: (5, {}), {1}: (6, {}), {2}: (7, {})} | custom-call | flops 19327352832 | bytes 52428800 | tf_op jit(solution)/shard_map/pallas_call | solution.py:205
  592.6 3.8 shard_map.102
  596.4 3.8 shard_map.103
  600.2 20.6 %shard_map.109 = (f32[512,4096]{1,0:T(8,128)}, f32[512,4096]{1,0:T(8,128)}, f32[4096,512]{1,0:T(8,128)}, f32[512,1024]{1,0:T(8,128)}, f32[512,1024]{1,0:T(8,128)}, /*index=5*/f32[1024,512]{1,0:T(8,128)}) custom-call(s32[1]{0:T(128)} %bitcast.28.core, bf16[512,2048]{1,0:T(8,128)(2,1)} %bitcast.65, bf16[512,2048]{1,0:T(8,128)(2,1)} %bitcast.67, ...), custom_call_target="tpu_custom_call" | custom-call | flops 9663676416 | bytes 52428800 | tf_op jit(solution)/shard_map/pallas_call | solution.py:271
  620.9 20.3 %shard_map.110 = (f32[512,4096]{1,0:T(8,128)}, f32[512,4096]{1,0:T(8,128)}, f32[4096,512]{1,0:T(8,128)}, f32[512,1024]{1,0:T(8,128)}, f32[512,1024]{1,0:T(8,128)}, /*index=5*/f32[1024,512]{1,0:T(8,128)}) custom-call(s32[1]{0:T(128)} %bitcast.28.core, bf16[512,2048]{1,0:T(8,128)(2,1)} %bitcast.66, ...), custom_call_target="tpu_custom_call", output_to_operand_aliasing={{0}: (9, {}), {1}: (10, {}), {2}: (11, {})} | custom-call | flops 9663676416 | bytes 52428800 | tf_op jit(solution)/shard_map/pallas_call | solution.py:271
  642.2 2.6 fusion
  646.0 2.7 add_convert_fusion.1
  648.7 1.7 collective-permute-start.29
  650.5 2.5 fusion.1
  654.7 3.1 constant_dynamic-update-slice_fusion.1
  665.6 31.7 %collective-permute-done.29 = bf16[512,2048]{1,0:T(8,128)(2,1)S(1)} collective-permute-done((bf16[512,2048]{1,0:T(8,128)(2,1)S(1)}, bf16[512,2048]{1,0:T(8,128)(2,1)S(1)}, u32[]{:S(2)}, u32[]{:S(2)}) %collective-permute-start.29) | collective-permute-done | bytes 2097184 | tf_op jit(solution)/shard_map/ppermute | solution.py:141
  698.8 42.6 %collective-permute-done.27 = bf16[512,2048]{1,0:T(8,128)(2,1)S(1)} collective-permute-done((bf16[512,2048]{1,0:T(8,128)(2,1)S(1)}, bf16[512,2048]{1,0:T(8,128)(2,1)S(1)}, u32[]{:S(2)}, u32[]{:S(2)}) %collective-permute-start.27) | collective-permute-done | bytes 2097184 | tf_op jit(solution)/shard_map/ppermute | solution.py:141
  742.8 1.6 pad_maximum_fusion.3
  (134 shorter events, 41.6 us)
Async XLA Ops:
  3.7 142.3 %copy-start = (bf16[512,2048]{1,0:T(8,128)(2,1)}, bf16[512,2048]{1,0:T(8,128)(2,1)S(1)}, u32[]{:S(2)}) copy-start(bf16[512,2048]{1,0:T(8,128)(2,1)S(1)} %pad_maximum_fusion.refs_0_) | copy-start | bytes 6291460
  3.9 27.4 %collective-permute-start.18 = (bf16[256,2048]{1,0:T(8,128)(2,1)S(1)}, bf16[256,2048]{1,0:T(8,128)(2,1)S(1)}, u32[]{:S(2)}, u32[]{:S(2)}) collective-permute-start(bf16[256,2048]{1,0:T(8,128)(2,1)S(1)} %get-tuple-element.174), channel_id=1, source_target_pairs={{0,4},{1,5},{2,6},{3,7},{4,0},{5,1},{6,2},{7,3}} | collective-permute-start | bytes 3145736 | tf_op jit(solution)/shard_map/ppermute | solution.py:141
  7.4 46.3 %collective-permute-start.22 = (bf16[256,2048]{1,0:T(8,128)(2,1)S(1)}, bf16[256,2048]{1,0:T(8,128)(2,1)S(1)}, u32[]{:S(2)}, u32[]{:S(2)}) collective-permute-start(bf16[256,2048]{1,0:T(8,128)(2,1)S(1)} %get-tuple-element.172), channel_id=1, source_target_pairs={{0,4},{1,5},{2,6},{3,7},{4,0},{5,1},{6,2},{7,3}} | collective-permute-start | bytes 3145736 | tf_op jit(solution)/shard_map/ppermute | solution.py:141
  7.4 90.5 %collective-permute-start.3 = (bf16[512,2048]{1,0:T(8,128)(2,1)S(1)}, bf16[512,2048]{1,0:T(8,128)(2,1)}, u32[]{:S(2)}, u32[]{:S(2)}) collective-permute-start(bf16[512,2048]{1,0:T(8,128)(2,1)S(1)} %pad_maximum_fusion.1.refs_0_), channel_id=1, source_target_pairs={{0,2},{1,3},{2,0},{3,1},{4,6},{5,7},{6,4},{7,5}} | collective-permute-start | bytes 6291464 | tf_op jit(solution)/shard_map/ppermute | solution.py:141
  9.4 90.2 %collective-permute-start.4 = (bf16[512,2048]{1,0:T(8,128)(2,1)S(1)}, bf16[512,2048]{1,0:T(8,128)(2,1)S(1)}, u32[]{:S(2)}, u32[]{:S(2)}) collective-permute-start(bf16[512,2048]{1,0:T(8,128)(2,1)S(1)} %pad_maximum_fusion.1.refs_0_), channel_id=1, source_target_pairs={{0,1},{1,0},{2,3},{3,2},{4,5},{5,4},{6,7},{7,6}} | collective-permute-start | bytes 6291464 | tf_op jit(solution)/shard_map/ppermute | solution.py:141
  9.4 91.5 %collective-permute-start = (bf16[512,2048]{1,0:T(8,128)(2,1)S(1)}, bf16[512,2048]{1,0:T(8,128)(2,1)S(1)}, u32[]{:S(2)}, u32[]{:S(2)}) collective-permute-start(bf16[512,2048]{1,0:T(8,128)(2,1)S(1)} %pad_maximum_fusion.refs_0_), channel_id=1, source_target_pairs={{0,2},{1,3},{2,0},{3,1},{4,6},{5,7},{6,4},{7,5}} | collective-permute-start | bytes 6291464 | tf_op jit(solution)/shard_map/ppermute | solution.py:141
  31.3 92.2 %copy-start.11 = (bf16[256,2048]{1,0:T(8,128)(2,1)}, bf16[256,2048]{1,0:T(8,128)(2,1)S(1)}, u32[]{:S(2)}) copy-start(bf16[256,2048]{1,0:T(8,128)(2,1)S(1)} %collective-permute-done.18.refs_0_) | copy-start | bytes 3145732
  31.3 44.9 %collective-permute-start.34 = (bf16[256,2048]{1,0:T(8,128)(2,1)S(1)}, bf16[256,2048]{1,0:T(8,128)(2,1)S(1)}, u32[]{:S(2)}, u32[]{:S(2)}) collective-permute-start(bf16[256,2048]{1,0:T(8,128)(2,1)S(1)} %get-tuple-element.173), channel_id=1, source_target_pairs={{0,4},{1,5},{2,6},{3,7},{4,0},{5,1},{6,2},{7,3}} | collective-permute-start | bytes 3145736 | tf_op jit(solution)/shard_map/ppermute | solution.py:141
  53.7 69.7 %copy-start.12 = (bf16[256,2048]{1,0:T(8,128)(2,1)}, bf16[256,2048]{1,0:T(8,128)(2,1)S(1)}, u32[]{:S(2)}) copy-start(bf16[256,2048]{1,0:T(8,128)(2,1)S(1)} %collective-permute-done.22.refs_0_) | copy-start | bytes 3145732
  53.7 44.2 %collective-permute-start.36 = (bf16[256,2048]{1,0:T(8,128)(2,1)S(1)}, bf16[256,2048]{1,0:T(8,128)(2,1)}, u32[]{:S(2)}, u32[]{:S(2)}) collective-permute-start(bf16[256,2048]{1,0:T(8,128)(2,1)S(1)} %get-tuple-element.171), channel_id=1, source_target_pairs={{0,4},{1,5},{2,6},{3,7},{4,0},{5,1},{6,2},{7,3}} | collective-permute-start | bytes 3145736 | tf_op jit(solution)/shard_map/ppermute | solution.py:141
  76.2 75.1 %copy-start.10 = (bf16[256,2048]{1,0:T(8,128)(2,1)}, bf16[256,2048]{1,0:T(8,128)(2,1)S(1)}, u32[]{:S(2)}) copy-start(bf16[256,2048]{1,0:T(8,128)(2,1)S(1)} %collective-permute-done.34.refs_0_) | copy-start | bytes 3145732
  76.2 47.3 %collective-permute-start.20 = (bf16[256,2048]{1,0:T(8,128)(2,1)S(1)}, bf16[256,2048]{1,0:T(8,128)(2,1)}, u32[]{:S(2)}, u32[]{:S(2)}) collective-permute-start(bf16[256,2048]{1,0:T(8,128)(2,1)S(1)} %collective-permute-done.18.refs_0_), channel_id=1, source_target_pairs={{0,2},{1,3},{2,0},{3,1},{4,6},{5,7},{6,4},{7,5}} | collective-permute-start | bytes 3145736 | tf_op jit(solution)/shard_map/ppermute | solution.py:141
  97.9 25.5 %collective-permute-start.19 = (bf16[256,2048]{1,0:T(8,128)(2,1)S(1)}, bf16[256,2048]{1,0:T(8,128)(2,1)S(1)}, u32[]{:S(2)}, u32[]{:S(2)}) collective-permute-start(bf16[256,2048]{1,0:T(8,128)(2,1)S(1)} %collective-permute-done.18.refs_0_), channel_id=1, source_target_pairs={{0,1},{1,0},{2,3},{3,2},{4,5},{5,4},{6,7},{7,6}} | collective-permute-start | bytes 3145736 | tf_op jit(solution)/shard_map/ppermute | solution.py:141
  97.9 46.6 %collective-permute-start.24 = (bf16[256,2048]{1,0:T(8,128)(2,1)S(1)}, bf16[256,2048]{1,0:T(8,128)(2,1)}, u32[]{:S(2)}, u32[]{:S(2)}) collective-permute-start(bf16[256,2048]{1,0:T(8,128)(2,1)S(1)} %collective-permute-done.22.refs_0_), channel_id=1, source_target_pairs={{0,2},{1,3},{2,0},{3,1},{4,6},{5,7},{6,4},{7,5}} | collective-permute-start | bytes 3145736 | tf_op jit(solution)/shard_map/ppermute | solution.py:141
  99.6 44.9 %collective-permute-start.23 = (bf16[256,2048]{1,0:T(8,128)(2,1)S(1)}, bf16[256,2048]{1,0:T(8,128)(2,1)S(1)}, u32[]{:S(2)}, u32[]{:S(2)}) collective-permute-start(bf16[256,2048]{1,0:T(8,128)(2,1)S(1)} %collective-permute-done.22.refs_0_), channel_id=1, source_target_pairs={{0,1},{1,0},{2,3},{3,2},{4,5},{5,4},{6,7},{7,6}} | collective-permute-start | bytes 3145736 | tf_op jit(solution)/shard_map/ppermute | solution.py:141
  102.2 53.6 %collective-permute-start.5 = (bf16[512,2048]{1,0:T(8,128)(2,1)}, bf16[512,2048]{1,0:T(8,128)(2,1)}, u32[]{:S(2)}, u32[]{:S(2)}) collective-permute-start(bf16[512,2048]{1,0:T(8,128)(2,1)} %collective-permute-done.3.refs_1_), channel_id=1, source_target_pairs={{0,1},{1,0},{2,3},{3,2},{4,5},{5,4},{6,7},{7,6}} | collective-permute-start | bytes 6291464 | tf_op jit(solution)/shard_map/ppermute | solution.py:141
  123.5 22.6 %collective-permute-start.35 = (bf16[256,2048]{1,0:T(8,128)(2,1)S(1)}, bf16[256,2048]{1,0:T(8,128)(2,1)}, u32[]{:S(2)}, u32[]{:S(2)}) collective-permute-start(bf16[256,2048]{1,0:T(8,128)(2,1)S(1)} %collective-permute-done.34.refs_0_), channel_id=1, source_target_pairs={{0,1},{1,0},{2,3},{3,2},{4,5},{5,4},{6,7},{7,6}} | collective-permute-start | bytes 3145736 | tf_op jit(solution)/shard_map/ppermute | solution.py:141
  123.5 22.6 %collective-permute-start.37 = (bf16[256,2048]{1,0:T(8,128)(2,1)}, bf16[256,2048]{1,0:T(8,128)(2,1)}, u32[]{:S(2)}, u32[]{:S(2)}) collective-permute-start(bf16[256,2048]{1,0:T(8,128)(2,1)} %collective-permute-done.36.refs_0_), channel_id=1, source_target_pairs={{0,1},{1,0},{2,3},{3,2},{4,5},{5,4},{6,7},{7,6}} | collective-permute-start | bytes 3145736 | tf_op jit(solution)/shard_map/ppermute | solution.py:141
  144.5 9.5 %collective-permute-start.21 = (bf16[256,2048]{1,0:T(8,128)(2,1)}, bf16[256,2048]{1,0:T(8,128)(2,1)}, u32[]{:S(2)}, u32[]{:S(2)}) collective-permute-start(bf16[256,2048]{1,0:T(8,128)(2,1)} %collective-permute-done.20.refs_2_), channel_id=1, source_target_pairs={{0,1},{1,0},{2,3},{3,2},{4,5},{5,4},{6,7},{7,6}} | collective-permute-start | bytes 3145736 | tf_op jit(solution)/shard_map/ppermute | solution.py:141
  145.5 8.6 %collective-permute-start.25 = (bf16[256,2048]{1,0:T(8,128)(2,1)}, bf16[256,2048]{1,0:T(8,128)(2,1)}, u32[]{:S(2)}, u32[]{:S(2)}) collective-permute-start(bf16[256,2048]{1,0:T(8,128)(2,1)} %collective-permute-done.24.refs_2_), channel_id=1, source_target_pairs={{0,1},{1,0},{2,3},{3,2},{4,5},{5,4},{6,7},{7,6}} | collective-permute-start | bytes 3145736 | tf_op jit(solution)/shard_map/ppermute | solution.py:141
  146.0 47.2 %collective-permute-start.1 = (bf16[512,2048]{1,0:T(8,128)(2,1)S(1)}, bf16[512,2048]{1,0:T(8,128)(2,1)}, u32[]{:S(2)}, u32[]{:S(2)}) collective-permute-start(bf16[512,2048]{1,0:T(8,128)(2,1)S(1)} %pad_maximum_fusion.refs_0_), channel_id=1, source_target_pairs={{0,1},{1,0},{2,3},{3,2},{4,5},{5,4},{6,7},{7,6}} | collective-permute-start | bytes 6291464 | tf_op jit(solution)/shard_map/ppermute | solution.py:141
  146.1 47.5 %collective-permute-start.2 = (bf16[512,2048]{1,0:T(8,128)(2,1)}, bf16[512,2048]{1,0:T(8,128)(2,1)}, u32[]{:S(2)}, u32[]{:S(2)}) collective-permute-start(bf16[512,2048]{1,0:T(8,128)(2,1)} %copy-done.4), channel_id=1, source_target_pairs={{0,1},{1,0},{2,3},{3,2},{4,5},{5,4},{6,7},{7,6}} | collective-permute-start | bytes 6291464 | tf_op jit(solution)/shard_map/ppermute | solution.py:141
  154.0 49.9 %collective-permute-start.15 = (bf16[3,512,512]{2,1,0:T(8,128)(2,1)}, bf16[3,512,512]{2,1,0:T(8,128)(2,1)}, u32[]{:S(2)}, u32[]{:S(2)}) collective-permute-start(bf16[3,512,512]{2,1,0:T(8,128)(2,1)} %pad_maximum_fusion.11), channel_id=1, source_target_pairs={{0,1},{1,0},{2,3},{3,2},{4,5},{5,4},{6,7},{7,6}} | collective-permute-start | bytes 4718600 | tf_op jit(solution)/shard_map/ppermute | solution.py:141
  154.1 50.1 %collective-permute-start.16 = (bf16[3,512,512]{2,1,0:T(8,128)(2,1)}, bf16[3,512,512]{2,1,0:T(8,128)(2,1)}, u32[]{:S(2)}, u32[]{:S(2)}) collective-permute-start(bf16[3,512,512]{2,1,0:T(8,128)(2,1)} %pad_maximum_fusion.10.refs_2_), channel_id=1, source_target_pairs={{0,4},{1,5},{2,6},{3,7},{4,0},{5,1},{6,2},{7,3}} | collective-permute-start | bytes 4718600 | tf_op jit(solution)/shard_map/ppermute | solution.py:141
  155.8 68.8 %collective-permute-start.17 = (bf16[3,512,512]{2,1,0:T(8,128)(2,1)}, bf16[3,512,512]{2,1,0:T(8,128)(2,1)}, u32[]{:S(2)}, u32[]{:S(2)}) collective-permute-start(bf16[3,512,512]{2,1,0:T(8,128)(2,1)} %pad_maximum_fusion.11), channel_id=1, source_target_pairs={{0,5},{1,4},{2,7},{3,6},{4,1},{5,0},{6,3},{7,2}} | collective-permute-start | bytes 4718600 | tf_op jit(solution)/shard_map/ppermute | solution.py:141
  193.2 75.8 %collective-permute-start.12 = (bf16[3,512,512]{2,1,0:T(8,128)(2,1)}, bf16[3,512,512]{2,1,0:T(8,128)(2,1)}, u32[]{:S(2)}, u32[]{:S(2)}) collective-permute-start(bf16[3,512,512]{2,1,0:T(8,128)(2,1)} %pad_maximum_fusion.9), channel_id=1, source_target_pairs={{0,1},{1,0},{2,3},{3,2},{4,5},{5,4},{6,7},{7,6}} | collective-permute-start | bytes 4718600 | tf_op jit(solution)/shard_map/ppermute | solution.py:141
  193.6 134.6 %collective-permute-start.14 = (bf16[3,512,512]{2,1,0:T(8,128)(2,1)}, bf16[3,512,512]{2,1,0:T(8,128)(2,1)}, u32[]{:S(2)}, u32[]{:S(2)}) collective-permute-start(bf16[3,512,512]{2,1,0:T(8,128)(2,1)} %pad_maximum_fusion.9), channel_id=1, source_target_pairs={{0,5},{1,4},{2,7},{3,6},{4,1},{5,0},{6,3},{7,2}} | collective-permute-start | bytes 4718600 | tf_op jit(solution)/shard_map/ppermute | solution.py:141
  203.9 190.3 %collective-permute-start.11 = (bf16[3,512,512]{2,1,0:T(8,128)(2,1)}, bf16[3,512,512]{2,1,0:T(8,128)(2,1)}, u32[]{:S(2)}, u32[]{:S(2)}) collective-permute-start(bf16[3,512,512]{2,1,0:T(8,128)(2,1)} %pad_maximum_fusion.7), channel_id=1, source_target_pairs={{0,5},{1,4},{2,7},{3,6},{4,1},{5,0},{6,3},{7,2}} | collective-permute-start | bytes 4718600 | tf_op jit(solution)/shard_map/ppermute | solution.py:141
  204.2 191.8 %collective-permute-start.9 = (bf16[3,512,512]{2,1,0:T(8,128)(2,1)}, bf16[3,512,512]{2,1,0:T(8,128)(2,1)}, u32[]{:S(2)}, u32[]{:S(2)}) collective-permute-start(bf16[3,512,512]{2,1,0:T(8,128)(2,1)} %pad_maximum_fusion.7), channel_id=1, source_target_pairs={{0,1},{1,0},{2,3},{3,2},{4,5},{5,4},{6,7},{7,6}} | collective-permute-start | bytes 4718600 | tf_op jit(solution)/shard_map/ppermute | solution.py:141
  224.6 101.9 %collective-permute-start.13 = (bf16[3,512,512]{2,1,0:T(8,128)(2,1)S(1)}, bf16[3,512,512]{2,1,0:T(8,128)(2,1)}, u32[]{:S(2)}, u32[]{:S(2)}) collective-permute-start(bf16[3,512,512]{2,1,0:T(8,128)(2,1)S(1)} %copy-done.9), channel_id=1, source_target_pairs={{0,4},{1,5},{2,6},{3,7},{4,0},{5,1},{6,2},{7,3}} | collective-permute-start | bytes 4718600 | tf_op jit(solution)/shard_map/ppermute | solution.py:141
  269.0 125.1 %collective-permute-start.10 = (bf16[3,512,512]{2,1,0:T(8,128)(2,1)}, bf16[3,512,512]{2,1,0:T(8,128)(2,1)}, u32[]{:S(2)}, u32[]{:S(2)}) collective-permute-start(bf16[3,512,512]{2,1,0:T(8,128)(2,1)} %pad_maximum_fusion.6.refs_2_), channel_id=1, source_target_pairs={{0,4},{1,5},{2,6},{3,7},{4,0},{5,1},{6,2},{7,3}} | collective-permute-start | bytes 4718600 | tf_op jit(solution)/shard_map/ppermute | solution.py:141
  326.5 69.8 %collective-permute-start.30 = (bf16[256,2048]{1,0:T(8,128)(2,1)}, bf16[256,2048]{1,0:T(8,128)(2,1)}, u32[]{:S(2)}, u32[]{:S(2)}) collective-permute-start(bf16[256,2048]{1,0:T(8,128)(2,1)} %slice.140), channel_id=1, source_target_pairs={{0,4},{1,5},{2,6},{3,7},{4,0},{5,1},{6,2},{7,3}} | collective-permute-start | bytes 3145736 | tf_op jit(solution)/shard_map/ppermute | solution.py:141
  328.2 76.9 %collective-permute-start.32 = (bf16[256,2048]{1,0:T(8,128)(2,1)}, bf16[256,2048]{1,0:T(8,128)(2,1)}, u32[]{:S(2)}, u32[]{:S(2)}) collective-permute-start(bf16[256,2048]{1,0:T(8,128)(2,1)} %slice.141), channel_id=1, source_target_pairs={{0,4},{1,5},{2,6},{3,7},{4,0},{5,1},{6,2},{7,3}} | collective-permute-start | bytes 3145736 | tf_op jit(solution)/shard_map/ppermute | solution.py:141
  394.2 76.8 %collective-permute-start.6 = (bf16[3,512,512]{2,1,0:T(8,128)(2,1)}, bf16[3,512,512]{2,1,0:T(8,128)(2,1)}, u32[]{:S(2)}, u32[]{:S(2)}) collective-permute-start(bf16[3,512,512]{2,1,0:T(8,128)(2,1)} %pad_maximum_fusion.5), channel_id=1, source_target_pairs={{0,1},{1,0},{2,3},{3,2},{4,5},{5,4},{6,7},{7,6}} | collective-permute-start | bytes 4718600 | tf_op jit(solution)/shard_map/ppermute | solution.py:141
  394.2 77.8 %collective-permute-start.8 = (bf16[3,512,512]{2,1,0:T(8,128)(2,1)}, bf16[3,512,512]{2,1,0:T(8,128)(2,1)}, u32[]{:S(2)}, u32[]{:S(2)}) collective-permute-start(bf16[3,512,512]{2,1,0:T(8,128)(2,1)} %pad_maximum_fusion.5), channel_id=1, source_target_pairs={{0,5},{1,4},{2,7},{3,6},{4,1},{5,0},{6,3},{7,2}} | collective-permute-start | bytes 4718600 | tf_op jit(solution)/shard_map/ppermute | solution.py:141
  396.0 76.0 %collective-permute-start.7 = (bf16[3,512,512]{2,1,0:T(8,128)(2,1)S(1)}, bf16[3,512,512]{2,1,0:T(8,128)(2,1)}, u32[]{:S(2)}, u32[]{:S(2)}) collective-permute-start(bf16[3,512,512]{2,1,0:T(8,128)(2,1)S(1)} %copy-done.8), channel_id=1, source_target_pairs={{0,4},{1,5},{2,6},{3,7},{4,0},{5,1},{6,2},{7,3}} | collective-permute-start | bytes 4718600 | tf_op jit(solution)/shard_map/ppermute | solution.py:141
  396.3 196.3 %collective-permute-start.31 = (bf16[256,2048]{1,0:T(8,128)(2,1)}, bf16[256,2048]{1,0:T(8,128)(2,1)}, u32[]{:S(2)}, u32[]{:S(2)}) collective-permute-start(bf16[256,2048]{1,0:T(8,128)(2,1)} %collective-permute-done.30.refs_0_), channel_id=1, source_target_pairs={{0,1},{1,0},{2,3},{3,2},{4,5},{5,4},{6,7},{7,6}} | collective-permute-start | bytes 3145736 | tf_op jit(solution)/shard_map/ppermute | solution.py:141
  405.1 191.2 %collective-permute-start.33 = (bf16[256,2048]{1,0:T(8,128)(2,1)}, bf16[256,2048]{1,0:T(8,128)(2,1)}, u32[]{:S(2)}, u32[]{:S(2)}) collective-permute-start(bf16[256,2048]{1,0:T(8,128)(2,1)} %collective-permute-done.32.refs_0_), channel_id=1, source_target_pairs={{0,1},{1,0},{2,3},{3,2},{4,5},{5,4},{6,7},{7,6}} | collective-permute-start | bytes 3145736 | tf_op jit(solution)/shard_map/ppermute | solution.py:141
  522.6 119.2 %collective-permute-start.28 = (bf16[1024,2048]{1,0:T(8,128)(2,1)}, bf16[1024,2048]{1,0:T(8,128)(2,1)}, u32[]{:S(2)}, u32[]{:S(2)}) collective-permute-start(bf16[1024,2048]{1,0:T(8,128)(2,1)} %get-tuple-element.103), channel_id=1, source_target_pairs={{0,1},{1,0},{2,3},{3,2},{4,5},{5,4},{6,7},{7,6}} | collective-permute-start | bytes 12582920 | tf_op jit(solution)/shard_map/ppermute | solution.py:141
  522.6 126.1 %collective-permute-start.26 = (bf16[1024,2048]{1,0:T(8,128)(2,1)}, bf16[1024,2048]{1,0:T(8,128)(2,1)}, u32[]{:S(2)}, u32[]{:S(2)}) collective-permute-start(bf16[1024,2048]{1,0:T(8,128)(2,1)} %get-tuple-element.101), channel_id=1, source_target_pairs={{0,1},{1,0},{2,3},{3,2},{4,5},{5,4},{6,7},{7,6}} | collective-permute-start | bytes 12582920 | tf_op jit(solution)/shard_map/ppermute | solution.py:141
  620.8 24.0 %collective-permute-start.42 = (f32[1024,512]{1,0:T(8,128)}, f32[1024,512]{1,0:T(8,128)}, u32[]{:S(2)}, u32[]{:S(2)}) collective-permute-start(f32[1024,512]{1,0:T(8,128)} %get-tuple-element.129), channel_id=1, source_target_pairs={{0,1},{1,0},{2,3},{3,2},{4,5},{5,4},{6,7},{7,6}} | collective-permute-start | bytes 6291464 | tf_op jit(solution)/shard_map/ppermute | solution.py:141
  641.2 4.5 collective-permute-start.43
  641.7 11.9 %collective-permute-start.40 = (f32[512,1024]{1,0:T(8,128)}, f32[512,1024]{1,0:T(8,128)S(1)}, u32[]{:S(2)}, u32[]{:S(2)}) collective-permute-start(f32[512,1024]{1,0:T(8,128)} %get-tuple-element.126), channel_id=1, source_target_pairs={{0,1},{1,0},{2,3},{3,2},{4,5},{5,4},{6,7},{7,6}} | collective-permute-start | bytes 6291464 | tf_op jit(solution)/shard_map/ppermute | solution.py:141
  641.7 19.1 %collective-permute-start.41 = (f32[512,1024]{1,0:T(8,128)}, f32[512,1024]{1,0:T(8,128)S(1)}, u32[]{:S(2)}, u32[]{:S(2)}) collective-permute-start(f32[512,1024]{1,0:T(8,128)} %get-tuple-element.127), channel_id=1, source_target_pairs={{0,1},{1,0},{2,3},{3,2},{4,5},{5,4},{6,7},{7,6}} | collective-permute-start | bytes 6291464 | tf_op jit(solution)/shard_map/ppermute | solution.py:141
  644.8 17.6 %collective-permute-start.38 = (f32[512,1024]{1,0:T(8,128)S(1)}, f32[512,1024]{1,0:T(8,128)S(1)}, u32[]{:S(2)}, u32[]{:S(2)}) collective-permute-start(f32[512,1024]{1,0:T(8,128)S(1)} %copy-done.15), channel_id=1, source_target_pairs={{0,1},{1,0},{2,3},{3,2},{4,5},{5,4},{6,7},{7,6}} | collective-permute-start | bytes 6291464 | tf_op jit(solution)/shard_map/ppermute | solution.py:141
  645.7 18.3 %collective-permute-start.39 = (f32[512,1024]{1,0:T(8,128)}, f32[512,1024]{1,0:T(8,128)S(1)}, u32[]{:S(2)}, u32[]{:S(2)}) collective-permute-start(f32[512,1024]{1,0:T(8,128)} %get-tuple-element.124), channel_id=1, source_target_pairs={{0,1},{1,0},{2,3},{3,2},{4,5},{5,4},{6,7},{7,6}} | collective-permute-start | bytes 6291464 | tf_op jit(solution)/shard_map/ppermute | solution.py:141
  648.7 48.5 %collective-permute-start.29 = (bf16[512,2048]{1,0:T(8,128)(2,1)S(1)}, bf16[512,2048]{1,0:T(8,128)(2,1)S(1)}, u32[]{:S(2)}, u32[]{:S(2)}) collective-permute-start(bf16[512,2048]{1,0:T(8,128)(2,1)S(1)} %add_convert_fusion.1), channel_id=1, source_target_pairs={{0,2},{1,3},{2,0},{3,1},{4,6},{5,7},{6,4},{7,5}} | collective-permute-start | bytes 6291464 | tf_op jit(solution)/shard_map/ppermute | solution.py:141
  653.5 87.8 %collective-permute-start.27 = (bf16[512,2048]{1,0:T(8,128)(2,1)S(1)}, bf16[512,2048]{1,0:T(8,128)(2,1)S(1)}, u32[]{:S(2)}, u32[]{:S(2)}) collective-permute-start(bf16[512,2048]{1,0:T(8,128)(2,1)S(1)} %add_convert_fusion.3), channel_id=1, source_target_pairs={{0,2},{1,3},{2,0},{3,1},{4,6},{5,7},{6,4},{7,5}} | collective-permute-start | bytes 6291464 | tf_op jit(solution)/shard_map/ppermute | solution.py:141
  (16 other events, 260.7 us)

commit v2 on v0

v2 whole, which is shorter than its diff:
```python
import functools

import jax
import jax.numpy as jnp
from jax import lax
from jax.experimental import pallas as pl
from jax.experimental.pallas import tpu as pltpu
from jax.sharding import PartitionSpec as P


ROW_SPEC = P(("datb", "data", "model"), None)
GATE_SPEC = P(("datb", "data"), "model")
DOWN_SPEC = P("model", ("datb", "data"))
AXES = ("datb", "model", "data")
WIDTHS = (512, 512, 512, 512)
TILE = 512
SPANS = ((0, 1024), (1024, 512), (1536, 512))
LIMIT = 62 * 1024 * 1024
bf16, f32 = jnp.bfloat16, jnp.float32
ANY = pl.BlockSpec(memory_space=pl.ANY)


CHUNKS = len(WIDTHS)


def mm(a, b, ca=1, cb=0):
    return lax.dot_general(a, b, (((ca,), (cb,)), ((), ())), preferred_element_type=f32)


def activations(x, dy, wg, wu, wd):
    a = mm(x, wg).astype(bf16).astype(f32)
    b = mm(x, wu).astype(bf16).astype(f32)
    g = mm(dy, wd, 1, 1).astype(bf16).astype(f32)
    sig = jax.nn.sigmoid(a)
    silu = a * sig
    h = (silu * b).astype(bf16)
    da = (g * b * sig * (1.0 + a * (1.0 - sig))).astype(bf16)
    db = (g * silu).astype(bf16)
    return h, da, db


def add_grads(x, dy, h, da, db, refs, half):
    part = half // 2
    for n in range(2):
        at = slice(n * part, (n + 1) * part)
        gate, up, down = refs[3 * n:3 * n + 3]
        gate[...] += mm(x[:, at], da, 0, 0)
        up[...] += mm(x[:, at], db, 0, 0)
        down[...] += mm(h, dy[:, at], 0, 0)


def own_kernel(half, *refs):
    x_ref, dy_ref, *pieces = refs[:6]
    (h_out, da_out, db_out, wg, wu, wd), grads = refs[-12:-6], refs[-6:]
    part = pieces[0].shape[1]

    @pl.when(pl.program_id(0) == 0)
    def _():
        for i, piece in enumerate(pieces):
            at = slice(i * part, (i + 1) * part)
            wg[at, :] = piece[:part, :]
            wu[at, :] = piece[part:2 * part, :]
            wd[:, at] = piece[2 * part:, :]
        for grad in grads:
            grad[...] = jnp.zeros_like(grad)

    x, dy = x_ref[...], dy_ref[...]
    h, da, db = activations(x, dy, wg[...], wu[...], wd[...])
    h_out[...] = h
    da_out[...] = da
    db_out[...] = db
    add_grads(x, dy, h, da, db, grads, half)


def sum_kernel(down, grown, *refs):
    if down:
        h, wd, *refs = refs
        total = mm(h[...], wd[...])
    else:
        da, db, wg, wu, *refs = refs
        total = mm(da[...], wg[...], 1, 1) + mm(db[...], wu[...], 1, 1)
    if grown:
        total += refs[0][...]
    refs[-1][...] = total.astype(refs[-1].dtype)


def late_kernel(part, xd, xp, dyd, dyp, wg, wu, wd, *refs):
    h_out, da_out, db_out, x_q, dy_q, x_sw, dy_sw, xs, dys = refs[-9:]
    block = xd.shape[0]

    @pl.when(pl.program_id(0) == 0)
    def _():
        for slot, (src_x, src_dy, mask) in enumerate(((xd, dyd, 2), (xp, dyp, 3))):
            rows, swapped = (slice(n * block, (n + 1) * block) for n in (slot, 1 - slot))
            for i in range(4):
                to, at = slice((i ^ mask) * part, ((i ^ mask) + 1) * part), slice(i * part, (i + 1) * part)
                xs[rows, to] = src_x[:, at]
                dys[rows, to] = src_dy[:, at]
            at = slice(mask * part, (mask + 1) * part)
            turned = src_x[:, at].T
            x_q[:, rows] = turned
            dy_q[rows, :] = src_dy[:, at]
            x_sw[:, swapped] = turned
            dy_sw[swapped, :] = src_dy[:, at]

    h, da, db = activations(xs[...], dys[...], wg[...], wu[...], wd[...])
    h_out[...] = h.T
    da_out[...] = da
    db_out[...] = db


def last_kernel(count, where, *refs):
    gate_in, up_in, down_in = refs[5 * count:5 * count + 3]
    gate, up, down = refs[-3:]
    dg, du, dd = gate_in[...], up_in[...], down_in[...]
    for n in range(count):
        x, dy, h, da, db = (ref[...] for ref in refs[5 * n:5 * n + 5])
        dg += mm(x, da)
        du += mm(x, db)
        dd += mm(h, dy)
    gate[...] = dg
    up[...] = du
    down[...] = dd


def pair_kernel(kept, near, out):
    out[...] = (kept[...].astype(f32) + near[...].astype(f32)).astype(bf16)


def join_kernel(where, residual, kept, near, far, out):
    out[...] = (residual[...].astype(f32) + kept[...].astype(f32) + near[...].astype(f32) + far[...].astype(f32)).astype(bf16)


def gather_kernel(masks, *refs):
    *srcs, out = refs
    part = out.shape[2] // 4
    for n, (src, mask) in enumerate(zip(srcs, masks)):
        for i in range(4):
            out[n, :, (i ^ mask) * part:((i ^ mask) + 1) * part] = src[:, i * part:(i + 1) * part]


def gather_rows(blocks, masks):
    count, (rows, cols) = len(blocks), blocks[0].shape
    tile = 128
    out = pl.pallas_call(
        functools.partial(gather_kernel, masks),
        grid=(rows // tile,),
        in_specs=[pl.BlockSpec((tile, cols), lambda t: (t, 0))] * count,
        out_specs=pl.BlockSpec((count, tile, cols), lambda t: (0, t, 0)),
        out_shape=jax.ShapeDtypeStruct((count, rows, cols), blocks[0].dtype),
        cost_estimate=pl.CostEstimate(flops=1000000, bytes_accessed=2 * count * rows * cols * 2, transcendentals=0),
    )(*blocks)
    return out.reshape(count * rows, cols)


def solution(mesh):
    def flip(value, names):
        mask = sum(4 >> AXES.index(name) for name in names)
        return lax.ppermute(value, AXES, [(i, i ^ mask) for i in range(8)])

    def local_step(tok, wg, wu, wd, dy):
        rows, d_model = tok.shape
        part = d_model // 4
        half = d_model // 2
        ff = wg.shape[1] // 2
        starts = [sum(WIDTHS[:j]) for j in range(CHUNKS)]
        core = lax.axis_index("data")
        place = 2 * lax.axis_index("datb") + core
        once = pl.Buffered(1)

        def relative(value):
            return jnp.concatenate([lax.dynamic_slice(value, (0, (place ^ i) * part), (value.shape[0], part)) for i in range(4)], axis=1)

        def pieces(which, j):
            start, width = which * ff + starts[j], WIDTHS[j]
            gate = lax.dynamic_slice(wg, (0, start), (part, width))
            up = lax.dynamic_slice(wu, (0, start), (part, width))
            down = lax.dynamic_slice(wd, (start, 0), (width, part))
            return lax.optimization_barrier(jnp.concatenate([gate, up, down], axis=0))

        tok_r, dy_r = lax.optimization_barrier((relative(tok), relative(dy)))
        weights = []
        for j in range(CHUNKS):
            same, other = pieces(core, j), pieces(1 - core, j)
            weights.append((same, flip(other, ["data"]), flip(same, ["datb"]), flip(other, ["datb", "data"])))
        tok_x = flip(tok_r, ["model"])
        dy_x = flip(dy_r, ["model"])
        x_own = gather_rows([tok_r, tok_x, flip(tok_r, ["data"]), flip(tok_x, ["data"])], (0, 0, 1, 1))
        dy_own = gather_rows([dy_r, dy_x, flip(dy_r, ["data"]), flip(dy_x, ["data"])], (0, 0, 1, 1))

        tok_y = flip(tok_r, ["datb"])
        dy_y = flip(dy_r, ["datb"])
        tok_yx = flip(tok_y, ["model"])
        dy_yx = flip(dy_x, ["datb"])

        act_shapes = [jax.ShapeDtypeStruct((4 * rows, ff), bf16)] * 3
        w_shapes = [jax.ShapeDtypeStruct((d_model, ff), bf16)] * 2 + [jax.ShapeDtypeStruct((ff, d_model), bf16)]
        g_shapes = ([jax.ShapeDtypeStruct((part, ff), f32)] * 2 + [jax.ShapeDtypeStruct((ff, part), f32)]) * 2

        def w_specs(width, at, **mode):
            return [pl.BlockSpec((d_model, width), lambda *g: (0, at(*g)), **mode)] * 2 + [pl.BlockSpec((width, d_model), lambda *g: (at(*g), 0), **mode)]

        def g_specs(width, at, **mode):
            return [pl.BlockSpec((part, width), lambda *g: (0, at(*g)), **mode)] * 2 + [pl.BlockSpec((width, part), lambda *g: (at(*g), 0), **mode)]

        def cost(flops):
            return pl.CostEstimate(flops=flops, bytes_accessed=50 << 20, transcendentals=0)

        params = pltpu.CompilerParams(vmem_limit_bytes=LIMIT)

        def sums(down, first_row, count, span, before, dtype):
            (start, width), skip = span, first_row // TILE
            index = start // width
            act = pl.BlockSpec((TILE, width), lambda r: (r + skip, index))
            row_block = pl.BlockSpec((TILE, d_model), lambda r: (r, 0))
            old_block = pl.BlockSpec((TILE, d_model), lambda r: (r + skip, 0))
            every = w_specs(width, lambda r: index, pipeline_mode=once)
            args, specs = (([acts[0], w_all[2]], [act, every[2]]) if down else ([acts[1], acts[2], w_all[0], w_all[1]], [act] * 2 + every[:2]))
            return pl.pallas_call(
                functools.partial(sum_kernel, down, before is not None),
                grid=(count // TILE,),
                in_specs=specs + ([] if before is None else [old_block]),
                out_specs=row_block,
                out_shape=jax.ShapeDtypeStruct((count, d_model), dtype),
                compiler_params=params,
                cost_estimate=cost((2 if down else 4) * count * d_model * width),
            )(*args, *([] if before is None else [before]))

        own_count = 4 * rows
        carry = None
        y_old = dx_old = None
        for j in range(CHUNKS):
            width, index = WIDTHS[j], starts[j] // WIDTHS[j]
            at = lambda r, index=index: index
            row_block = pl.BlockSpec((TILE, d_model), lambda r: (r, 0))
            act_block = pl.BlockSpec((TILE, width), lambda r, index=index: (r, index))
            piece_block = pl.BlockSpec(weights[j][0].shape, lambda r: (0, 0), pipeline_mode=once)
            carry = pl.pallas_call(
                functools.partial(own_kernel, half),
                grid=(own_count // TILE,),
                in_specs=[row_block] * 2 + [piece_block] * 4 + ([] if carry is None else [ANY] * 12),
                out_specs=[act_block] * 3 + w_specs(width, at, pipeline_mode=once) + g_specs(width, at, pipeline_mode=once) * 2,
                out_shape=act_shapes + w_shapes + g_shapes,
                input_output_aliases={} if carry is None else {6 + i: i for i in range(12)},
                compiler_params=params,
                cost_estimate=cost(9 * own_count * d_model * width),
            )(x_own, dy_own, *weights[j], *([] if carry is None else carry))
            acts, w_all, grads = carry[:3], carry[3:6], carry[6:]
            for span in SPANS[:-1]:
                if sum(span) == starts[j] + width:
                    y_old = sums(True, 0, own_count, span, y_old, f32)
                    dx_old = sums(False, 0, own_count, span, dx_old, f32)

        def scatter(down, before, residual):
            sent = sums(down, 2 * rows, 2 * rows, SPANS[-1], before, bf16)
            kept = sums(down, 0, 2 * rows, SPANS[-1], before, bf16)
            near = flip(sent, ["data"])
            quarter = pl.BlockSpec((rows, part), lambda i: (1, i))
            swapped = pl.BlockSpec((rows, part), lambda i: (1, i + 1 - 2 * (i % 2)))
            far_part = pl.pallas_call(
                pair_kernel,
                grid=(4,),
                in_specs=[quarter, swapped],
                out_specs=pl.BlockSpec((rows, part), lambda i: (0, i)),
                out_shape=jax.ShapeDtypeStruct((rows, d_model), bf16),
                compiler_params=params,
                cost_estimate=cost(1 << 22),
            )(kept, near)
            far = flip(far_part, ["model"])
            block_of = lambda i, c: (0, i)
            place_of = lambda i, c: (0, c[i])
            return pl.pallas_call(
                join_kernel,
                grid_spec=pltpu.PrefetchScalarGridSpec(
                    num_scalar_prefetch=1,
                    grid=(4,),
                    in_specs=[pl.BlockSpec((rows, part), block_of)] * 2 + [pl.BlockSpec((rows, part), lambda i, c: (0, i + 1 - 2 * (i % 2))), pl.BlockSpec((rows, part), block_of)],
                    out_specs=pl.BlockSpec((rows, part), place_of),
                ),
                out_shape=jax.ShapeDtypeStruct((rows, d_model), bf16),
                compiler_params=params,
                cost_estimate=cost(1 << 22),
            )(place ^ jnp.arange(4, dtype=jnp.int32), residual, kept, near, far)

        out = scatter(True, y_old, tok_r)
        grad_in = scatter(False, dx_old, dy_r)

        got = [flip(v, ["data"]) for v in grads[3:]]

        late, late_got, step = [], [], 256
        tok_n, dy_n, tok_xn = flip(tok_y, ["data"]), flip(dy_y, ["data"]), flip(tok_yx, ["data"])
        groups = [(rows, (tok_y, tok_n, dy_y, dy_n)), (rows, (tok_yx, tok_xn, dy_yx, flip(dy_yx, ["data"])))]
        for size, blocks in groups:
            blk = [pl.BlockSpec((size, d_model), lambda j: (0, 0), pipeline_mode=once)] * 4
            outs = pl.pallas_call(
                functools.partial(late_kernel, part),
                grid=(ff // step,),
                in_specs=blk + w_specs(step, lambda j: j),
                out_specs=[pl.BlockSpec((step, 2 * size), lambda j: (j, 0))] + [pl.BlockSpec((2 * size, step), lambda j: (0, j))] * 2 + [pl.BlockSpec((part, 2 * size), lambda j: (0, 0)), pl.BlockSpec((2 * size, part), lambda j: (0, 0))] * 2,
                out_shape=[jax.ShapeDtypeStruct((ff, 2 * size), bf16)] + [jax.ShapeDtypeStruct((2 * size, ff), bf16)] * 2 + [jax.ShapeDtypeStruct((part, 2 * size), bf16), jax.ShapeDtypeStruct((2 * size, part), bf16)] * 2,
                scratch_shapes=[pltpu.VMEM((2 * size, d_model), bf16)] * 2,
                compiler_params=params,
                cost_estimate=cost(6 * 2 * size * d_model * ff),
            )(*blocks, *w_all)
            late.append(outs)
            late_got.append([flip(v, ["data"]) for v in outs[:3]])
        count = len(groups)

        finals = ()
        unit = 256
        units = ff // unit
        stages = [(grads[:3], core, [[*late[k][3:5], *late[k][:3]] for k in range(count)]), (got, 1 - core, [[*late[k][5:7], *late_got[k]] for k in range(count)])]
        for before, side, parts in stages:
            late_specs = []
            for size, _ in groups:
                late_specs += [pl.BlockSpec((part, 2 * size), lambda j, c: (0, 0), pipeline_mode=once), pl.BlockSpec((2 * size, part), lambda j, c: (0, 0), pipeline_mode=once), pl.BlockSpec((unit, 2 * size), lambda j, c: (j, 0))] + [pl.BlockSpec((2 * size, unit), lambda j, c: (0, j))] * 2
            place_at = lambda j, c: c[0] * units + j
            finals = pl.pallas_call(
                functools.partial(last_kernel, count),
                grid_spec=pltpu.PrefetchScalarGridSpec(
                    num_scalar_prefetch=1,
                    grid=(units,),
                    in_specs=late_specs + g_specs(unit, lambda j, c: j) + [ANY] * len(finals),
                    out_specs=g_specs(unit, place_at),
                ),
                out_shape=[jax.ShapeDtypeStruct((part, 2 * ff), f32)] * 2 + [jax.ShapeDtypeStruct((2 * ff, part), f32)],
                input_output_aliases={1 + 5 * count + 3 + i: i for i in range(len(finals))},
                compiler_params=params,
                cost_estimate=cost(6 * 4 * rows * part * ff),
            )(side.reshape(1), *[v for group in parts for v in group], *before, *finals)
        return out, grad_in, *finals

    return jax.shard_map(local_step, mesh=mesh, in_specs=(ROW_SPEC, GATE_SPEC, GATE_SPEC, DOWN_SPEC, ROW_SPEC), out_specs=(ROW_SPEC, ROW_SPEC, GATE_SPEC, GATE_SPEC, DOWN_SPEC), check_vma=False)
```

time: 1430 us -> 751 us (0.53)
  waiting for transfers between devices: 1050 us -> 323 us
  Pallas kernels: 0 us -> 380 us
  matrix products: 216 us -> 0 us
  local copies, waits for them, and re-layouts: 65.2 us -> 8.88 us
  blocking collectives: 36 us -> 0 us
  starting transfers between devices: 1.24 us -> 22.3 us
  other arithmetic: 32.8 us -> 12.7 us
    reduce_scatter x6 -> x0, waiting for transfers between devices: 557 us -> none  [the longest x1 180 us: local_step(): lax.psum_scatter(jnp.einsum('atf,tbae->fbe', hid_all, grad_split, preferr...]
    pallas_call x0 -> x22, Pallas kernels: none -> 380 us  [the longest x4 119 us: local_step(): pl.pallas_call(functools.partial(own_kernel, half), grid=(own_count // TI...]
    all_gather x8 -> x0, waiting for transfers between devices: 372 us -> none  [the longest x1 86.1 us: local_step(): gate_w = lax.all_gather(wg_loc, 'datb', axis=0)]
    ppermute x0 -> x39, waiting for transfers between devices: none -> 323 us  [flip(): return lax.ppermute(value, AXES, [(i, i ^ mask) for i in range(8)])]
    dot_general x9 -> x0, matrix products: 216 us -> none  [the longest x1 24.4 us: local_step(): jnp.einsum('atf,bef->atbe', dgate_all, gate_w, preferred_element_type=jnp...]
    unnamed x16 -> x0, waiting for transfers between devices: 123 us -> none
    unnamed x16 -> x10, local copies, waits for them, and re-layouts: 39.7 us -> 1.56 us
    all_to_all x4 -> x0, blocking collectives: 36 us -> none  [the longest x2 12.5 us: to_rows(): lax.all_to_all(per_model[:, :, :, None, :], 'data', 0, 3, tiled=True)]
  transfers between devices with their start and end apart: 15 -> 39, of which waited for: 14 -> 9; matrix products, arithmetic and copies ran while one was open for 18% -> 2% of each run, Pallas kernels for 0% -> 48%
where the time goes in v2:
time: 751 us; the launch traced here: 748 us
  Pallas kernels  380 us (51%)
  waiting for transfers between devices  323 us (43%)
  starting transfers between devices  22.3 us (3%)
  other arithmetic  12.7 us (2%)
  local copies, waits for them, and re-layouts  8.88 us (1%)
    ppermute x39, waiting for transfers between devices, flip(): return lax.ppermute(value, AXES, [(i, i ^ mask) for i in range(8)])  323 us
    pallas_call x4, Pallas kernels, local_step(): pl.pallas_call(functools.partial(own_kernel, half), grid=(own_count // TI...  119 us
    pallas_call x8, Pallas kernels, sums(): pl.pallas_call(functools.partial(sum_kernel, down, before is not None), g...  105 us
    pallas_call x2, Pallas kernels, local_step(): pl.pallas_call(functools.partial(late_kernel, part), grid=(ff // step,),...  73 us
    pallas_call x2, Pallas kernels, local_step(): pl.pallas_call(functools.partial(last_kernel, count), grid_spec=pltpu.Pre...  46.5 us
    ppermute x39, starting transfers between devices, flip(): return lax.ppermute(value, AXES, [(i, i ^ mask) for i in range(8)])  22.3 us
  transfers between devices with their start and end apart: 39, of which 9 were waited for; matrix products, arithmetic and copies ran while one was open for 2% of the time, Pallas kernels for 48%

profile of v2, /device:TPU:0, one launch (start us, length us, event | category | flops | bytes accessed | tf_op | source)
XLA Modules:
  0.0 748.0 jit_solution(13146901596407105130)
XLA Ops:
  0.7 2.5 constant_dynamic-slice_fusion.27
  3.4 1.8 pad_maximum_fusion.refs_0_.residual
  5.2 3.3 collective-permute-start.3
  8.6 46.6 %collective-permute-done.3.refs_1_ = bf16[512,2048]{1,0:T(8,128)(2,1)} collective-permute-done((bf16[512,2048]{1,0:T(8,128)(2,1)S(1)}, bf16[512,2048]{1,0:T(8,128)(2,1)}, u32[]{:S(2)}, u32[]{:S(2)}) %collective-permute-start.3) | collective-permute-done | bytes 2097184 | tf_op jit(solution)/shard_map/ppermute | solution.py:159
  55.7 3.6 constant_dynamic-slice_fusion.2
  59.3 1.5 copy-done.3
  60.8 1.3 constant_dynamic-slice_fusion
  62.1 37.1 %collective-permute-done.refs_1_ = bf16[512,2048]{1,0:T(8,128)(2,1)} collective-permute-done((bf16[512,2048]{1,0:T(8,128)(2,1)}, bf16[512,2048]{1,0:T(8,128)(2,1)}, u32[]{:S(2)}, u32[]{:S(2)}) %collective-permute-start) | collective-permute-done | bytes 2097184 | tf_op jit(solution)/shard_map/ppermute | solution.py:159
  99.2 2.3 pad_maximum_fusion.9
  102.0 1.3 pad_maximum_fusion.8.refs_2_
  103.3 1.4 collective-permute-start.17
  108.9 1.3 pad_maximum_fusion.5
  110.2 1.3 pad_maximum_fusion.3
  111.6 7.6 %shard_map.93 = bf16[4,512,2048]{2,1,0:T(8,128)(2,1)} custom-call(bf16[512,2048]{1,0:T(8,128)(2,1)} %copy-done, bf16[512,2048]{1,0:T(8,128)(2,1)} %collective-permute-done.3.refs_1_, bf16[512,2048]{1,0:T(8,128)(2,1)} %collective-permute-done.4.refs_2_, bf16[512,2048]{1,0:T(8,128)(2,1)} %collective-permute-done.5.refs_3_), custom_call_target="tpu_custom_call" | custom-call | flops 1000000 | bytes 16777216 | tf_op jit(solution)/shard_map/pallas_call | solution.py:145
  119.2 1.6 collective-permute-start.14
  120.9 7.0 shard_map.92
  128.0 46.4 %collective-permute-done.16.refs_4_ = bf16[1536,512]{1,0:T(8,128)(2,1)} collective-permute-done((bf16[1536,512]{1,0:T(8,128)(2,1)}, bf16[1536,512]{1,0:T(8,128)(2,1)}, u32[]{:S(2)}, u32[]{:S(2)}) %collective-permute-start.16) | collective-permute-done | bytes 1572896 | tf_op jit(solution)/shard_map/ppermute | solution.py:159
  174.4 1.6 collective-permute-start.13
  176.0 29.7 %shard_map.94 = (bf16[2048,2048]{1,0:T(8,128)(2,1)}, bf16[2048,2048]{1,0:T(8,128)(2,1)}, bf16[2048,2048]{1,0:T(8,128)(2,1)}, bf16[2048,2048]{1,0:T(8,128)(2,1)},...) custom-call(bf16[2048,2048]{1,0:T(8,128)(2,1)} %bitcast.8, ...), custom_call_target="tpu_custom_call" | custom-call | flops 19327352832 | bytes 52428800 | tf_op jit(solution)/shard_map/pallas_call | solution.py:238
  205.9 69.3 %collective-permute-done.13.refs_4_ = bf16[1536,512]{1,0:T(8,128)(2,1)} collective-permute-done((bf16[1536,512]{1,0:T(8,128)(2,1)}, bf16[1536,512]{1,0:T(8,128)(2,1)}, u32[]{:S(2)}, u32[]{:S(2)}) %collective-permute-start.13) | collective-permute-done | bytes 1572896 | tf_op jit(solution)/shard_map/ppermute | solution.py:159
  275.2 1.3 collective-permute-start.8
  276.9 29.8 %shard_map.95 = (bf16[2048,2048]{1,0:T(8,128)(2,1)}, bf16[2048,2048]{1,0:T(8,128)(2,1)}, bf16[2048,2048]{1,0:T(8,128)(2,1)}, bf16[2048,2048]{1,0:T(8,128)(2,1)},...) custom-call(bf16[2048,2048]{1,0:T(8,128)(2,1)} %bitcast.9, ...), custom_call_target="tpu_custom_call", output_to_operand_aliasing={{0}: (6, {}), {1}: (7, {}), {2}: (8, {}), {3}: (9, {}), {4}... | custom-call | flops 19327352832 | bytes 52428800 | tf_op jit(solution)/shard_map/pallas_call | solution.py:238
  306.8 14.0 %shard_map.98.refs_2_ = f32[2048,2048]{1,0:T(8,128)} custom-call(bf16[2048,2048]{1,0:T(8,128)(2,1)} %get-tuple-element.89.refs_6_.refs_0_, bf16[2048,2048]{1,0:T(8,128)(2,1)} %get-tuple-element.94.refs_11_.refs_1_), custom_call_target="tpu_custom_call" | custom-call | flops 8589934592 | bytes 52428800 | tf_op jit(solution)/shard_map/pallas_call | solution.py:219
  320.8 24.2 %shard_map.104.refs_4_ = f32[2048,2048]{1,0:T(8,128)} custom-call(bf16[2048,2048]{1,0:T(8,128)(2,1)} %get-tuple-element.90.refs_7_.refs_0_, bf16[2048,2048]{1,0:T(8,128)(2,1)} %get-tuple-element.91.refs_8_.refs_1_, bf16[2048,2048]{1,0:T(8,128)(2,1)} %get-tuple-element.92.refs_9_.refs_2_, bf16[2048,2048]{1,0:T(8,128)(2,1)} %get-tuple-element.93.refs_10_.refs_3_), custom_call_target="tpu_custom_call" | custom-call | flops 17179869184 | bytes 52428800 | tf_op jit(solution)/shard_map/pallas_call | solution.py:219
  345.9 1.8 collective-permute-start.22
  347.9 1.8 collective-permute-start.7
  349.7 29.8 %shard_map.96 = (bf16[2048,2048]{1,0:T(8,128)(2,1)}, bf16[2048,2048]{1,0:T(8,128)(2,1)}, bf16[2048,2048]{1,0:T(8,128)(2,1)}, bf16[2048,2048]{1,0:T(8,128)(2,1)},...) custom-call(bf16[2048,2048]{1,0:T(8,128)(2,1)} %bitcast.10, ...), custom_call_target="tpu_custom_call", output_to_operand_aliasing={{0}: (6, {}), {1}: (7, {}), {2}: (8, {}), {3}: (9, {}), {4}... | custom-call | flops 19327352832 | bytes 52428800 | tf_op jit(solution)/shard_map/pallas_call | solution.py:238
  379.5 14.2 %shard_map.99.refs_2_ = f32[2048,2048]{1,0:T(8,128)} custom-call(bf16[2048,2048]{1,0:T(8,128)(2,1)} %get-tuple-element.101.refs_6_.refs_0_, bf16[2048,2048]{1,0:T(8,128)(2,1)} %get-tuple-element.106.refs_11_.refs_1_, f32[2048,2048]{1,0:T(8,128)} %shard_map.98.refs_2_), custom_call_target="tpu_custom_call" | custom-call | flops 4294967296 | bytes 52428800 | tf_op jit(solution)/shard_map/pallas_call | solution.py:219
  393.7 18.8 %shard_map.105.refs_4_ = f32[2048,2048]{1,0:T(8,128)} custom-call(bf16[2048,2048]{1,0:T(8,128)(2,1)} %get-tuple-element.102.refs_7_.refs_0_, bf16[2048,2048]{1,0:T(8,128)(2,1)} %get-tuple-element.103.refs_8_.refs_1_, bf16[2048,2048]{1,0:T(8,128)(2,1)} %get-tuple-element.104.refs_9_.refs_2_, bf16[2048,2048]{1,0:T(8,128)(2,1)} %get-tuple-element.105.refs_10_.refs_3_, ...), custom_call_target="tpu_custom_call" | custom-call | flops 8589934592 | bytes 52428800 | tf_op jit(solution)/shard_map/pallas_call | solution.py:219
  412.8 1.8 collective-permute-start.29
  414.5 58.8 %collective-permute-done.7.refs_4_ = bf16[1536,512]{1,0:T(8,128)(2,1)} collective-permute-done((bf16[1536,512]{1,0:T(8,128)(2,1)S(1)}, bf16[1536,512]{1,0:T(8,128)(2,1)}, u32[]{:S(2)}, u32[]{:S(2)}) %collective-permute-start.7) | collective-permute-done | bytes 1572896 | tf_op jit(solution)/shard_map/ppermute | solution.py:159
  473.9 29.9 %shard_map.97 = (bf16[2048,2048]{1,0:T(8,128)(2,1)}, bf16[2048,2048]{1,0:T(8,128)(2,1)}, bf16[2048,2048]{1,0:T(8,128)(2,1)}, bf16[2048,2048]{1,0:T(8,128)(2,1)},...) custom-call(bf16[2048,2048]{1,0:T(8,128)(2,1)} %bitcast.11, ...), custom_call_target="tpu_custom_call", output_to_operand_aliasing={{0}: (6, {}), {1}: (7, {}), {2}: (8, {}), {3}: (9, {}), {4}... | custom-call | flops 19327352832 | bytes 52428800 | tf_op jit(solution)/shard_map/pallas_call | solution.py:238
  503.7 10.1 %shard_map.107 = bf16[1024,2048]{1,0:T(8,128)(2,1)} custom-call(bf16[2048,2048]{1,0:T(8,128)(2,1)} %get-tuple-element.115.refs_0_, bf16[2048,2048]{1,0:T(8,128)(2,1)} %get-tuple-element.116.refs_1_, bf16[2048,2048]{1,0:T(8,128)(2,1)} %get-tuple-element.117.refs_2_.wg, bf16[2048,2048]{1,0:T(8,128)(2,1)} %get-tuple-element.118.refs_3_.wu, ...), custom_call_target="tpu_custom_call" | custom-call | flops 4294967296 | bytes 52428800 | tf_op jit(solution)/shard_map/pallas_call | solution.py:219
  513.9 7.0 shard_map.101
  521.3 36.6 %shard_map.110 = (bf16[2048,1024]{1,0:T(8,128)(2,1)}, bf16[1024,2048]{1,0:T(8,128)(2,1)}, bf16[1024,2048]{1,0:T(8,128)(2,1)}, bf16[512,1024]{1,0:T(8,128)(2,1)},...) custom-call(bf16[512,2048]{1,0:T(8,128)(2,1)} %collective-permute-done.22.xd, ...), custom_call_target="tpu_custom_call" | custom-call | flops 25769803776 | bytes 52428800 | tf_op jit(solution)/shard_map/pallas_call | solution.py:295
  558.6 9.9 %collective-permute-done.30.xp = bf16[512,2048]{1,0:T(8,128)(2,1)} collective-permute-done((bf16[512,2048]{1,0:T(8,128)(2,1)}, bf16[512,2048]{1,0:T(8,128)(2,1)}, u32[]{:S(2)}, u32[]{:S(2)}) %collective-permute-start.30) | collective-permute-done | bytes 2097184 | tf_op jit(solution)/shard_map/ppermute | solution.py:159
  569.1 7.0 shard_map.100.kept
  576.1 10.1 %shard_map.106.kept = bf16[1024,2048]{1,0:T(8,128)(2,1)} custom-call(bf16[2048,2048]{1,0:T(8,128)(2,1)} %get-tuple-element.115.refs_0_, bf16[2048,2048]{1,0:T(8,128)(2,1)} %get-tuple-element.116.refs_1_, bf16[2048,2048]{1,0:T(8,128)(2,1)} %get-tuple-element.117.refs_2_.wg, bf16[2048,2048]{1,0:T(8,128)(2,1)} %get-tuple-element.118.refs_3_.wu, ...), custom_call_target="tpu_custom_call" | custom-call | flops 4294967296 | bytes 52428800 | tf_op jit(solution)/shard_map/pallas_call | solution.py:219
  586.2 4.3 shard_map.108
  590.5 4.3 shard_map.102
  594.8 1.7 collective-permute-start.21
  596.9 36.4 %shard_map.111 = (bf16[2048,1024]{1,0:T(8,128)(2,1)}, bf16[1024,2048]{1,0:T(8,128)(2,1)}, bf16[1024,2048]{1,0:T(8,128)(2,1)}, bf16[512,1024]{1,0:T(8,128)(2,1)},...) custom-call(bf16[512,2048]{1,0:T(8,128)(2,1)} %collective-permute-done.29.xd, ...), custom_call_target="tpu_custom_call" | custom-call | flops 25769803776 | bytes 52428800 | tf_op jit(solution)/shard_map/pallas_call | solution.py:295
  633.8 9.8 %collective-permute-done.21.far = bf16[512,2048]{1,0:T(8,128)(2,1)} collective-permute-done((bf16[512,2048]{1,0:T(8,128)(2,1)}, bf16[512,2048]{1,0:T(8,128)(2,1)}, u32[]{:S(2)}, u32[]{:S(2)}) %collective-permute-start.21) | collective-permute-done | bytes 2097184 | tf_op jit(solution)/shard_map/ppermute | solution.py:159
  643.7 44.3 %collective-permute-done.19.far = bf16[512,2048]{1,0:T(8,128)(2,1)} collective-permute-done((bf16[512,2048]{1,0:T(8,128)(2,1)}, bf16[512,2048]{1,0:T(8,128)(2,1)}, u32[]{:S(2)}, u32[]{:S(2)}) %collective-permute-start.19) | collective-permute-done | bytes 2097184 | tf_op jit(solution)/shard_map/ppermute | solution.py:159
  688.6 23.4 %shard_map.112 = (f32[512,4096]{1,0:T(8,128)}, f32[512,4096]{1,0:T(8,128)}, f32[4096,512]{1,0:T(8,128)}) custom-call(s32[1]{0:T(128)} %bitcast.3.where, bf16[512,1024]{1,0:T(8,128)(2,1)} %get-tuple-element.132.refs_0_, bf16[1024,512]{1,0:T(8,128)(2,1)} %get-tuple-element.133.refs_1_, bf16[2048,1024]{1,0:T(8,128)(2,1)} %get-tuple-element.121.refs_2_, ...), custom_call_target="tpu_custom_call" | custom-call | flops 12884901888 | bytes 52428800 | tf_op jit(solution)/shard_map/pallas_call | solution.py:318
  711.9 6.2 shard_map.109
  718.1 6.2 shard_map.103
  724.4 23.1 %shard_map.113 = (f32[512,4096]{1,0:T(8,128)}, f32[512,4096]{1,0:T(8,128)}, f32[4096,512]{1,0:T(8,128)}) custom-call(s32[1]{0:T(128)} %bitcast.2.where, bf16[512,1024]{1,0:T(8,128)(2,1)} %get-tuple-element.119.refs_0_, bf16[1024,512]{1,0:T(8,128)(2,1)} %get-tuple-element.120.refs_1_, ...), custom_call_target="tpu_custom_call", output_to_operand_aliasing={{0}: (14, {}), {1}: (15, {}), {2}: (16, {})} | custom-call | flops 12884901888 | bytes 52428800 | tf_op jit(solution)/shard_map/pallas_call | solution.py:318
  (76 shorter events, 11.6 us)
Async XLA Ops:
  3.4 55.8 %copy-start = (bf16[512,2048]{1,0:T(8,128)(2,1)}, bf16[512,2048]{1,0:T(8,128)(2,1)S(1)}, u32[]{:S(2)}) copy-start(bf16[512,2048]{1,0:T(8,128)(2,1)S(1)} %pad_maximum_fusion.1.refs_0_.residual) | copy-start | bytes 6291460
  5.2 49.9 %collective-permute-start.3 = (bf16[512,2048]{1,0:T(8,128)(2,1)S(1)}, bf16[512,2048]{1,0:T(8,128)(2,1)}, u32[]{:S(2)}, u32[]{:S(2)}) collective-permute-start(bf16[512,2048]{1,0:T(8,128)(2,1)S(1)} %pad_maximum_fusion.1.refs_0_.residual), channel_id=1, source_target_pairs={{0,2},{1,3},{2,0},{3,1},{4,6},{5,7},{6,4},{7,5}} | collective-permute-start | bytes 6291464 | tf_op jit(solution)/shard_map/ppermute | solution.py:159
  8.6 90.7 %collective-permute-start = (bf16[512,2048]{1,0:T(8,128)(2,1)}, bf16[512,2048]{1,0:T(8,128)(2,1)}, u32[]{:S(2)}, u32[]{:S(2)}) collective-permute-start(bf16[512,2048]{1,0:T(8,128)(2,1)} %pad_maximum_fusion.refs_0_.residual), channel_id=1, source_target_pairs={{0,2},{1,3},{2,0},{3,1},{4,6},{5,7},{6,4},{7,5}} | collective-permute-start | bytes 6291464 | tf_op jit(solution)/shard_map/ppermute | solution.py:159
  8.6 94.8 %collective-permute-start.4 = (bf16[512,2048]{1,0:T(8,128)(2,1)S(1)}, bf16[512,2048]{1,0:T(8,128)(2,1)}, u32[]{:S(2)}, u32[]{:S(2)}) collective-permute-start(bf16[512,2048]{1,0:T(8,128)(2,1)S(1)} %pad_maximum_fusion.1.refs_0_.residual), channel_id=1, source_target_pairs={{0,1},{1,0},{2,3},{3,2},{4,5},{5,4},{6,7},{7,6}} | collective-permute-start | bytes 6291464 | tf_op jit(solution)/shard_map/ppermute | solution.py:159
  55.1 49.6 %collective-permute-start.5 = (bf16[512,2048]{1,0:T(8,128)(2,1)}, bf16[512,2048]{1,0:T(8,128)(2,1)}, u32[]{:S(2)}, u32[]{:S(2)}) collective-permute-start(bf16[512,2048]{1,0:T(8,128)(2,1)} %collective-permute-done.3.refs_1_), channel_id=1, source_target_pairs={{0,1},{1,0},{2,3},{3,2},{4,5},{5,4},{6,7},{7,6}} | collective-permute-start | bytes 6291464 | tf_op jit(solution)/shard_map/ppermute | solution.py:159
  55.1 64.0 %collective-permute-start.1 = (bf16[512,2048]{1,0:T(8,128)(2,1)}, bf16[512,2048]{1,0:T(8,128)(2,1)}, u32[]{:S(2)}, u32[]{:S(2)}) collective-permute-start(bf16[512,2048]{1,0:T(8,128)(2,1)} %pad_maximum_fusion.refs_0_.residual), channel_id=1, source_target_pairs={{0,1},{1,0},{2,3},{3,2},{4,5},{5,4},{6,7},{7,6}} | collective-permute-start | bytes 6291464 | tf_op jit(solution)/shard_map/ppermute | solution.py:159
  55.6 3.6 copy-start.2
  55.6 5.1 copy-start.3
  62.1 40.0 %copy-start.4 = (bf16[512,512]{1,0:T(8,128)(2,1)S(1)}, bf16[512,512]{1,0:T(8,128)(2,1)}, u32[]{:S(2)}) copy-start(bf16[512,512]{1,0:T(8,128)(2,1)} %get-tuple-element.152) | copy-start | bytes 1572868
  99.2 20.0 %collective-permute-start.2 = (bf16[512,2048]{1,0:T(8,128)(2,1)}, bf16[512,2048]{1,0:T(8,128)(2,1)}, u32[]{:S(2)}, u32[]{:S(2)}) collective-permute-start(bf16[512,2048]{1,0:T(8,128)(2,1)} %collective-permute-done.refs_1_), channel_id=1, source_target_pairs={{0,1},{1,0},{2,3},{3,2},{4,5},{5,4},{6,7},{7,6}} | collective-permute-start | bytes 6291464 | tf_op jit(solution)/shard_map/ppermute | solution.py:159
  101.5 26.4 %collective-permute-start.15 = (bf16[1536,512]{1,0:T(8,128)(2,1)}, bf16[1536,512]{1,0:T(8,128)(2,1)}, u32[]{:S(2)}, u32[]{:S(2)}) collective-permute-start(bf16[1536,512]{1,0:T(8,128)(2,1)} %pad_maximum_fusion.9), channel_id=1, source_target_pairs={{0,1},{1,0},{2,3},{3,2},{4,5},{5,4},{6,7},{7,6}} | collective-permute-start | bytes 4718600 | tf_op jit(solution)/shard_map/ppermute | solution.py:159
  103.3 71.0 %collective-permute-start.17 = (bf16[1536,512]{1,0:T(8,128)(2,1)}, bf16[1536,512]{1,0:T(8,128)(2,1)}, u32[]{:S(2)}, u32[]{:S(2)}) collective-permute-start(bf16[1536,512]{1,0:T(8,128)(2,1)} %pad_maximum_fusion.9), channel_id=1, source_target_pairs={{0,5},{1,4},{2,7},{3,6},{4,1},{5,0},{6,3},{7,2}} | collective-permute-start | bytes 4718600 | tf_op jit(solution)/shard_map/ppermute | solution.py:159
  104.7 69.7 %collective-permute-start.16 = (bf16[1536,512]{1,0:T(8,128)(2,1)}, bf16[1536,512]{1,0:T(8,128)(2,1)}, u32[]{:S(2)}, u32[]{:S(2)}) collective-permute-start(bf16[1536,512]{1,0:T(8,128)(2,1)} %pad_maximum_fusion.8.refs_2_), channel_id=1, source_target_pairs={{0,4},{1,5},{2,6},{3,7},{4,0},{5,1},{6,2},{7,3}} | collective-permute-start | bytes 4718600 | tf_op jit(solution)/shard_map/ppermute | solution.py:159
  111.6 236.4 %copy-start.1 = (bf16[1536,512]{1,0:T(8,128)(2,1)}, bf16[1536,512]{1,0:T(8,128)(2,1)S(1)}, u32[]{:S(2)}) copy-start(bf16[1536,512]{1,0:T(8,128)(2,1)S(1)} %pad_maximum_fusion.2.refs_2_) | copy-start | bytes 4718596
  119.1 86.5 %collective-permute-start.12 = (bf16[1536,512]{1,0:T(8,128)(2,1)}, bf16[1536,512]{1,0:T(8,128)(2,1)}, u32[]{:S(2)}, u32[]{:S(2)}) collective-permute-start(bf16[1536,512]{1,0:T(8,128)(2,1)} %pad_maximum_fusion.7), channel_id=1, source_target_pairs={{0,1},{1,0},{2,3},{3,2},{4,5},{5,4},{6,7},{7,6}} | collective-permute-start | bytes 4718600 | tf_op jit(solution)/shard_map/ppermute | solution.py:159
  119.2 157.2 %collective-permute-start.14 = (bf16[1536,512]{1,0:T(8,128)(2,1)}, bf16[1536,512]{1,0:T(8,128)(2,1)}, u32[]{:S(2)}, u32[]{:S(2)}) collective-permute-start(bf16[1536,512]{1,0:T(8,128)(2,1)} %pad_maximum_fusion.7), channel_id=1, source_target_pairs={{0,5},{1,4},{2,7},{3,6},{4,1},{5,0},{6,3},{7,2}} | collective-permute-start | bytes 4718600 | tf_op jit(solution)/shard_map/ppermute | solution.py:159
  127.9 219.8 %collective-permute-start.11 = (bf16[1536,512]{1,0:T(8,128)(2,1)}, bf16[1536,512]{1,0:T(8,128)(2,1)}, u32[]{:S(2)}, u32[]{:S(2)}) collective-permute-start(bf16[1536,512]{1,0:T(8,128)(2,1)} %pad_maximum_fusion.5), channel_id=1, source_target_pairs={{0,5},{1,4},{2,7},{3,6},{4,1},{5,0},{6,3},{7,2}} | collective-permute-start | bytes 4718600 | tf_op jit(solution)/shard_map/ppermute | solution.py:159
  174.4 173.5 %collective-permute-start.9 = (bf16[1536,512]{1,0:T(8,128)(2,1)}, bf16[1536,512]{1,0:T(8,128)(2,1)}, u32[]{:S(2)}, u32[]{:S(2)}) collective-permute-start(bf16[1536,512]{1,0:T(8,128)(2,1)} %pad_maximum_fusion.5), channel_id=1, source_target_pairs={{0,1},{1,0},{2,3},{3,2},{4,5},{5,4},{6,7},{7,6}} | collective-permute-start | bytes 4718600 | tf_op jit(solution)/shard_map/ppermute | solution.py:159
  174.4 100.8 %collective-permute-start.13 = (bf16[1536,512]{1,0:T(8,128)(2,1)}, bf16[1536,512]{1,0:T(8,128)(2,1)}, u32[]{:S(2)}, u32[]{:S(2)}) collective-permute-start(bf16[1536,512]{1,0:T(8,128)(2,1)} %pad_maximum_fusion.6.refs_2_), channel_id=1, source_target_pairs={{0,4},{1,5},{2,6},{3,7},{4,0},{5,1},{6,2},{7,3}} | collective-permute-start | bytes 4718600 | tf_op jit(solution)/shard_map/ppermute | solution.py:159
  205.7 206.8 %collective-permute-start.6 = (bf16[1536,512]{1,0:T(8,128)(2,1)}, bf16[1536,512]{1,0:T(8,128)(2,1)}, u32[]{:S(2)}, u32[]{:S(2)}) collective-permute-start(bf16[1536,512]{1,0:T(8,128)(2,1)} %pad_maximum_fusion.3), channel_id=1, source_target_pairs={{0,1},{1,0},{2,3},{3,2},{4,5},{5,4},{6,7},{7,6}} | collective-permute-start | bytes 4718600 | tf_op jit(solution)/shard_map/ppermute | solution.py:159
  275.2 198.7 %collective-permute-start.8 = (bf16[1536,512]{1,0:T(8,128)(2,1)}, bf16[1536,512]{1,0:T(8,128)(2,1)}, u32[]{:S(2)}, u32[]{:S(2)}) collective-permute-start(bf16[1536,512]{1,0:T(8,128)(2,1)} %pad_maximum_fusion.3), channel_id=1, source_target_pairs={{0,5},{1,4},{2,7},{3,6},{4,1},{5,0},{6,3},{7,2}} | collective-permute-start | bytes 4718600 | tf_op jit(solution)/shard_map/ppermute | solution.py:159
  276.5 69.4 %collective-permute-start.10 = (bf16[1536,512]{1,0:T(8,128)(2,1)}, bf16[1536,512]{1,0:T(8,128)(2,1)}, u32[]{:S(2)}, u32[]{:S(2)}) collective-permute-start(bf16[1536,512]{1,0:T(8,128)(2,1)} %pad_maximum_fusion.4.refs_2_), channel_id=1, source_target_pairs={{0,4},{1,5},{2,6},{3,7},{4,0},{5,1},{6,2},{7,3}} | collective-permute-start | bytes 4718600 | tf_op jit(solution)/shard_map/ppermute | solution.py:159
  345.9 66.9 %collective-permute-start.22 = (bf16[512,2048]{1,0:T(8,128)(2,1)}, bf16[512,2048]{1,0:T(8,128)(2,1)}, u32[]{:S(2)}, u32[]{:S(2)}) collective-permute-start(bf16[512,2048]{1,0:T(8,128)(2,1)} %pad_maximum_fusion.refs_0_.residual), channel_id=1, source_target_pairs={{0,4},{1,5},{2,6},{3,7},{4,0},{5,1},{6,2},{7,3}} | collective-permute-start | bytes 6291464 | tf_op jit(solution)/shard_map/ppermute | solution.py:159
  347.7 125.7 %collective-permute-start.24 = (bf16[512,2048]{1,0:T(8,128)(2,1)}, bf16[512,2048]{1,0:T(8,128)(2,1)}, u32[]{:S(2)}, u32[]{:S(2)}) collective-permute-start(bf16[512,2048]{1,0:T(8,128)(2,1)} %copy-done), channel_id=1, source_target_pairs={{0,4},{1,5},{2,6},{3,7},{4,0},{5,1},{6,2},{7,3}} | collective-permute-start | bytes 6291464 | tf_op jit(solution)/shard_map/ppermute | solution.py:159
  347.9 125.4 %collective-permute-start.7 = (bf16[1536,512]{1,0:T(8,128)(2,1)S(1)}, bf16[1536,512]{1,0:T(8,128)(2,1)}, u32[]{:S(2)}, u32[]{:S(2)}) collective-permute-start(bf16[1536,512]{1,0:T(8,128)(2,1)S(1)} %pad_maximum_fusion.2.refs_2_), channel_id=1, source_target_pairs={{0,4},{1,5},{2,6},{3,7},{4,0},{5,1},{6,2},{7,3}} | collective-permute-start | bytes 4718600 | tf_op jit(solution)/shard_map/ppermute | solution.py:159
  412.5 146.0 %collective-permute-start.31 = (bf16[512,2048]{1,0:T(8,128)(2,1)}, bf16[512,2048]{1,0:T(8,128)(2,1)}, u32[]{:S(2)}, u32[]{:S(2)}) collective-permute-start(bf16[512,2048]{1,0:T(8,128)(2,1)} %collective-permute-done.3.refs_1_), channel_id=1, source_target_pairs={{0,4},{1,5},{2,6},{3,7},{4,0},{5,1},{6,2},{7,3}} | collective-permute-start | bytes 6291464 | tf_op jit(solution)/shard_map/ppermute | solution.py:159
  412.8 145.3 %collective-permute-start.29 = (bf16[512,2048]{1,0:T(8,128)(2,1)}, bf16[512,2048]{1,0:T(8,128)(2,1)}, u32[]{:S(2)}, u32[]{:S(2)}) collective-permute-start(bf16[512,2048]{1,0:T(8,128)(2,1)} %collective-permute-done.22.xd), channel_id=1, source_target_pairs={{0,2},{1,3},{2,0},{3,1},{4,6},{5,7},{6,4},{7,5}} | collective-permute-start | bytes 6291464 | tf_op jit(solution)/shard_map/ppermute | solution.py:159
  473.4 47.5 %collective-permute-start.23 = (bf16[512,2048]{1,0:T(8,128)(2,1)}, bf16[512,2048]{1,0:T(8,128)(2,1)}, u32[]{:S(2)}, u32[]{:S(2)}) collective-permute-start(bf16[512,2048]{1,0:T(8,128)(2,1)} %collective-permute-done.22.xd), channel_id=1, source_target_pairs={{0,1},{1,0},{2,3},{3,2},{4,5},{5,4},{6,7},{7,6}} | collective-permute-start | bytes 6291464 | tf_op jit(solution)/shard_map/ppermute | solution.py:159
  473.4 48.0 %collective-permute-start.25 = (bf16[512,2048]{1,0:T(8,128)(2,1)}, bf16[512,2048]{1,0:T(8,128)(2,1)}, u32[]{:S(2)}, u32[]{:S(2)}) collective-permute-start(bf16[512,2048]{1,0:T(8,128)(2,1)} %collective-permute-done.24.dyd), channel_id=1, source_target_pairs={{0,1},{1,0},{2,3},{3,2},{4,5},{5,4},{6,7},{7,6}} | collective-permute-start | bytes 6291464 | tf_op jit(solution)/shard_map/ppermute | solution.py:159
  513.8 54.8 %collective-permute-start.20 = (bf16[1024,2048]{1,0:T(8,128)(2,1)}, bf16[1024,2048]{1,0:T(8,128)(2,1)}, u32[]{:S(2)}, u32[]{:S(2)}) collective-permute-start(bf16[1024,2048]{1,0:T(8,128)(2,1)} %shard_map.107), channel_id=1, source_target_pairs={{0,1},{1,0},{2,3},{3,2},{4,5},{5,4},{6,7},{7,6}} | collective-permute-start | bytes 12582920 | tf_op jit(solution)/shard_map/ppermute | solution.py:159
  520.9 48.1 %collective-permute-start.18 = (bf16[1024,2048]{1,0:T(8,128)(2,1)}, bf16[1024,2048]{1,0:T(8,128)(2,1)}, u32[]{:S(2)}, u32[]{:S(2)}) collective-permute-start(bf16[1024,2048]{1,0:T(8,128)(2,1)} %shard_map.101), channel_id=1, source_target_pairs={{0,1},{1,0},{2,3},{3,2},{4,5},{5,4},{6,7},{7,6}} | collective-permute-start | bytes 12582920 | tf_op jit(solution)/shard_map/ppermute | solution.py:159
  558.0 38.6 %collective-permute-start.26 = (bf16[2048,1024]{1,0:T(8,128)(2,1)}, bf16[2048,1024]{1,0:T(8,128)(2,1)}, u32[]{:S(2)}, u32[]{:S(2)}) collective-permute-start(bf16[2048,1024]{1,0:T(8,128)(2,1)} %get-tuple-element.121.refs_2_), channel_id=1, source_target_pairs={{0,1},{1,0},{2,3},{3,2},{4,5},{5,4},{6,7},{7,6}} | collective-permute-start | bytes 12582920 | tf_op jit(solution)/shard_map/ppermute | solution.py:159
  558.0 10.4 %collective-permute-start.30 = (bf16[512,2048]{1,0:T(8,128)(2,1)}, bf16[512,2048]{1,0:T(8,128)(2,1)}, u32[]{:S(2)}, u32[]{:S(2)}) collective-permute-start(bf16[512,2048]{1,0:T(8,128)(2,1)} %collective-permute-done.29.xd), channel_id=1, source_target_pairs={{0,1},{1,0},{2,3},{3,2},{4,5},{5,4},{6,7},{7,6}} | collective-permute-start | bytes 6291464 | tf_op jit(solution)/shard_map/ppermute | solution.py:159
  558.5 36.3 %collective-permute-start.32 = (bf16[512,2048]{1,0:T(8,128)(2,1)}, bf16[512,2048]{1,0:T(8,128)(2,1)}, u32[]{:S(2)}, u32[]{:S(2)}) collective-permute-start(bf16[512,2048]{1,0:T(8,128)(2,1)} %collective-permute-done.31.dyd), channel_id=1, source_target_pairs={{0,1},{1,0},{2,3},{3,2},{4,5},{5,4},{6,7},{7,6}} | collective-permute-start | bytes 6291464 | tf_op jit(solution)/shard_map/ppermute | solution.py:159
  568.5 64.8 %collective-permute-start.27 = (bf16[1024,2048]{1,0:T(8,128)(2,1)}, bf16[1024,2048]{1,0:T(8,128)(2,1)}, u32[]{:S(2)}, u32[]{:S(2)}) collective-permute-start(bf16[1024,2048]{1,0:T(8,128)(2,1)} %get-tuple-element.122.refs_3_), channel_id=1, source_target_pairs={{0,1},{1,0},{2,3},{3,2},{4,5},{5,4},{6,7},{7,6}} | collective-permute-start | bytes 12582920 | tf_op jit(solution)/shard_map/ppermute | solution.py:159
  568.6 64.7 %collective-permute-start.28 = (bf16[1024,2048]{1,0:T(8,128)(2,1)}, bf16[1024,2048]{1,0:T(8,128)(2,1)}, u32[]{:S(2)}, u32[]{:S(2)}) collective-permute-start(bf16[1024,2048]{1,0:T(8,128)(2,1)} %get-tuple-element.123.refs_4_), channel_id=1, source_target_pairs={{0,1},{1,0},{2,3},{3,2},{4,5},{5,4},{6,7},{7,6}} | collective-permute-start | bytes 12582920 | tf_op jit(solution)/shard_map/ppermute | solution.py:159
  569.0 64.8 %collective-permute-start.36 = (f32[512,2048]{1,0:T(8,128)}, f32[512,2048]{1,0:T(8,128)}, u32[]{:S(2)}, u32[]{:S(2)}) collective-permute-start(f32[512,2048]{1,0:T(8,128)} %get-tuple-element.129), channel_id=1, source_target_pairs={{0,1},{1,0},{2,3},{3,2},{4,5},{5,4},{6,7},{7,6}} | collective-permute-start | bytes 12582920 | tf_op jit(solution)/shard_map/ppermute | solution.py:159
  594.8 48.8 %collective-permute-start.21 = (bf16[512,2048]{1,0:T(8,128)(2,1)}, bf16[512,2048]{1,0:T(8,128)(2,1)}, u32[]{:S(2)}, u32[]{:S(2)}) collective-permute-start(bf16[512,2048]{1,0:T(8,128)(2,1)} %shard_map.108), channel_id=1, source_target_pairs={{0,2},{1,3},{2,0},{3,1},{4,6},{5,7},{6,4},{7,5}} | collective-permute-start | bytes 6291464 | tf_op jit(solution)/shard_map/ppermute | solution.py:159
  596.6 91.4 %collective-permute-start.19 = (bf16[512,2048]{1,0:T(8,128)(2,1)}, bf16[512,2048]{1,0:T(8,128)(2,1)}, u32[]{:S(2)}, u32[]{:S(2)}) collective-permute-start(bf16[512,2048]{1,0:T(8,128)(2,1)} %shard_map.102), channel_id=1, source_target_pairs={{0,2},{1,3},{2,0},{3,1},{4,6},{5,7},{6,4},{7,5}} | collective-permute-start | bytes 6291464 | tf_op jit(solution)/shard_map/ppermute | solution.py:159
  633.3 91.1 %collective-permute-start.37 = (f32[512,2048]{1,0:T(8,128)}, f32[512,2048]{1,0:T(8,128)}, u32[]{:S(2)}, u32[]{:S(2)}) collective-permute-start(f32[512,2048]{1,0:T(8,128)} %get-tuple-element.130), channel_id=1, source_target_pairs={{0,1},{1,0},{2,3},{3,2},{4,5},{5,4},{6,7},{7,6}} | collective-permute-start | bytes 12582920 | tf_op jit(solution)/shard_map/ppermute | solution.py:159
  633.3 91.0 %collective-permute-start.38 = (f32[2048,512]{1,0:T(8,128)}, f32[2048,512]{1,0:T(8,128)}, u32[]{:S(2)}, u32[]{:S(2)}) collective-permute-start(f32[2048,512]{1,0:T(8,128)} %get-tuple-element.131), channel_id=1, source_target_pairs={{0,1},{1,0},{2,3},{3,2},{4,5},{5,4},{6,7},{7,6}} | collective-permute-start | bytes 12582920 | tf_op jit(solution)/shard_map/ppermute | solution.py:159
  633.8 90.5 %collective-permute-start.33 = (bf16[2048,1024]{1,0:T(8,128)(2,1)}, bf16[2048,1024]{1,0:T(8,128)(2,1)}, u32[]{:S(2)}, u32[]{:S(2)}) collective-permute-start(bf16[2048,1024]{1,0:T(8,128)(2,1)} %get-tuple-element.126.refs_7_), channel_id=1, source_target_pairs={{0,1},{1,0},{2,3},{3,2},{4,5},{5,4},{6,7},{7,6}} | collective-permute-start | bytes 12582920 | tf_op jit(solution)/shard_map/ppermute | solution.py:159
  643.7 80.7 %collective-permute-start.34 = (bf16[1024,2048]{1,0:T(8,128)(2,1)}, bf16[1024,2048]{1,0:T(8,128)(2,1)}, u32[]{:S(2)}, u32[]{:S(2)}) collective-permute-start(bf16[1024,2048]{1,0:T(8,128)(2,1)} %get-tuple-element.127.refs_8_), channel_id=1, source_target_pairs={{0,1},{1,0},{2,3},{3,2},{4,5},{5,4},{6,7},{7,6}} | collective-permute-start | bytes 12582920 | tf_op jit(solution)/shard_map/ppermute | solution.py:159
  688.0 36.3 %collective-permute-start.35 = (bf16[1024,2048]{1,0:T(8,128)(2,1)}, bf16[1024,2048]{1,0:T(8,128)(2,1)}, u32[]{:S(2)}, u32[]{:S(2)}) collective-permute-start(bf16[1024,2048]{1,0:T(8,128)(2,1)} %get-tuple-element.128.refs_9_), channel_id=1, source_target_pairs={{0,1},{1,0},{2,3},{3,2},{4,5},{5,4},{6,7},{7,6}} | collective-permute-start | bytes 12582920 | tf_op jit(solution)/shard_map/ppermute | solution.py:159

commit v3 on v2

--- a/solution.py
+++ b/solution.py
@@ -27,16 +27,18 @@
     return lax.dot_general(a, b, (((ca,), (cb,)), ((), ())), preferred_element_type=f32)
 
 
-def activations(x, dy, wg, wu, wd):
-    a = mm(x, wg).astype(bf16).astype(f32)
-    b = mm(x, wu).astype(bf16).astype(f32)
-    g = mm(dy, wd, 1, 1).astype(bf16).astype(f32)
+def gated(a, b, g):
+    a, b, g = (v.astype(bf16).astype(f32) for v in (a, b, g))
     sig = jax.nn.sigmoid(a)
     silu = a * sig
     h = (silu * b).astype(bf16)
     da = (g * b * sig * (1.0 + a * (1.0 - sig))).astype(bf16)
     db = (g * silu).astype(bf16)
     return h, da, db
+
+
+def activations(x, dy, wg, wu, wd):
+    return gated(mm(x, wg), mm(x, wu), mm(dy, wd, 1, 1))
 
 
 def add_grads(x, dy, h, da, db, refs, half):
@@ -84,26 +86,43 @@
     refs[-1][...] = total.astype(refs[-1].dtype)
 
 
-def late_kernel(part, xd, xp, dyd, dyp, wg, wu, wd, *refs):
-    h_out, da_out, db_out, x_q, dy_q, x_sw, dy_sw, xs, dys = refs[-9:]
-    block = xd.shape[0]
-
+def close_kernel(h, da, db, wg, wu, wd, y_old, dx_old, y_out, dx_out):
+    y_out[...] = (mm(h[...], wd[...]) + y_old[...]).astype(bf16)
+    dx_out[...] = (mm(da[...], wg[...], 1, 1) + mm(db[...], wu[...], 1, 1) + dx_old[...]).astype(bf16)
+
+
+def place_rows(direct, near, out):
+    block, part = direct.shape[0], direct.shape[1] // 4
+    for slot, (src, mask) in enumerate(((direct, 2), (near, 3))):
+        for i in range(4):
+            out[slot * block:(slot + 1) * block, (i ^ mask) * part:((i ^ mask) + 1) * part] = src[:, i * part:(i + 1) * part]
+
+
+def gate_up_kernel(xd, xp, wg, wu, a_out, b_out, x_t, xs):
     @pl.when(pl.program_id(0) == 0)
     def _():
-        for slot, (src_x, src_dy, mask) in enumerate(((xd, dyd, 2), (xp, dyp, 3))):
+        place_rows(xd, xp, xs)
+
+    a_out[...] = mm(xs[...], wg[...]).astype(bf16)
+    b_out[...] = mm(xs[...], wu[...]).astype(bf16)
+    count = x_t.shape[0]
+    x_t[...] = xs[:, pl.ds(pl.multiple_of(pl.program_id(0) * count, count), count)].T
+
+
+def late_kernel(part, dyd, dyp, wd, a, b, x, h_out, da_out, db_out, x_q, dy_q, x_sw, dy_sw, dys):
+    block = dyd.shape[0]
+
+    @pl.when(pl.program_id(0) == 0)
+    def _():
+        place_rows(dyd, dyp, dys)
+        for slot in range(2):
             rows, swapped = (slice(n * block, (n + 1) * block) for n in (slot, 1 - slot))
-            for i in range(4):
-                to, at = slice((i ^ mask) * part, ((i ^ mask) + 1) * part), slice(i * part, (i + 1) * part)
-                xs[rows, to] = src_x[:, at]
-                dys[rows, to] = src_dy[:, at]
-            at = slice(mask * part, (mask + 1) * part)
-            turned = src_x[:, at].T
-            x_q[:, rows] = turned
-            dy_q[rows, :] = src_dy[:, at]
-            x_sw[:, swapped] = turned
-            dy_sw[swapped, :] = src_dy[:, at]
-
-    h, da, db = activations(xs[...], dys[...], wg[...], wu[...], wd[...])
+            x_q[:, rows] = x[:, rows]
+            x_sw[:, swapped] = x[:, rows]
+            dy_q[rows, :] = dys[rows, :part]
+            dy_sw[swapped, :] = dys[rows, :part]
+
+    h, da, db = gated(a[...], b[...], mm(dys[...], wd[...], 1, 1))
     h_out[...] = h.T
     da_out[...] = da
     db_out[...] = db
@@ -251,9 +270,25 @@
                     y_old = sums(True, 0, own_count, span, y_old, f32)
                     dx_old = sums(False, 0, own_count, span, dx_old, f32)
 
-        def scatter(down, before, residual):
-            sent = sums(down, 2 * rows, 2 * rows, SPANS[-1], before, bf16)
-            kept = sums(down, 0, 2 * rows, SPANS[-1], before, bf16)
+        def close(first_row):
+            (start, width), skip = SPANS[-1], first_row // TILE
+            old_block = pl.BlockSpec((TILE, d_model), lambda r: (r + skip, 0))
+            act = pl.BlockSpec((TILE, width), lambda r: (r + skip, start // width))
+            row_block = pl.BlockSpec((TILE, d_model), lambda r: (r, 0))
+            return pl.pallas_call(
+                close_kernel,
+                grid=(2 * rows // TILE,),
+                in_specs=[act] * 3 + w_specs(width, lambda r: start // width, pipeline_mode=once) + [old_block] * 2,
+                out_specs=[row_block] * 2,
+                out_shape=[jax.ShapeDtypeStruct((2 * rows, d_model), bf16)] * 2,
+                compiler_params=params,
+                cost_estimate=cost(6 * 2 * rows * d_model * width),
+            )(*acts, *w_all, y_old, dx_old)
+
+        y_send, dx_send = close(2 * rows)
+        y_keep, dx_keep = close(0)
+
+        def scatter(kept, sent, residual):
             near = flip(sent, ["data"])
             quarter = pl.BlockSpec((rows, part), lambda i: (1, i))
             swapped = pl.BlockSpec((rows, part), lambda i: (1, i + 1 - 2 * (i % 2)))
@@ -267,43 +302,65 @@
                 cost_estimate=cost(1 << 22),
             )(kept, near)
             far = flip(far_part, ["model"])
-            block_of = lambda i, c: (0, i)
-            place_of = lambda i, c: (0, c[i])
+            piece = pl.BlockSpec((rows, part), lambda i, c: (0, i))
             return pl.pallas_call(
                 join_kernel,
                 grid_spec=pltpu.PrefetchScalarGridSpec(
                     num_scalar_prefetch=1,
                     grid=(4,),
-                    in_specs=[pl.BlockSpec((rows, part), block_of)] * 2 + [pl.BlockSpec((rows, part), lambda i, c: (0, i + 1 - 2 * (i % 2))), pl.BlockSpec((rows, part), block_of)],
-                    out_specs=pl.BlockSpec((rows, part), place_of),
+                    in_specs=[piece, piece, pl.BlockSpec((rows, part), lambda i, c: (0, i + 1 - 2 * (i % 2))), piece],
+                    out_specs=pl.BlockSpec((rows, part), lambda i, c: (0, c[i])),
                 ),
                 out_shape=jax.ShapeDtypeStruct((rows, d_model), bf16),
                 compiler_params=params,
                 cost_estimate=cost(1 << 22),
             )(place ^ jnp.arange(4, dtype=jnp.int32), residual, kept, near, far)
 
-        out = scatter(True, y_old, tok_r)
-        grad_in = scatter(False, dx_old, dy_r)
+        out = scatter(y_keep, y_send, tok_r)
+        grad_in = scatter(dx_keep, dx_send, dy_r)
+
+        step = 256
+        tok_n, dy_n, tok_xn = flip(tok_y, ["data"]), flip(dy_y, ["data"]), flip(tok_yx, ["data"])
+
+        def column(j):
+            return (0, j)
+
+        def fixed(j):
+            return (0, 0)
+
+        blk = [pl.BlockSpec((rows, d_model), fixed, pipeline_mode=once)] * 2
+        every = w_specs(step, lambda j: j)
+        ab_block = pl.BlockSpec((2 * rows, step), column)
+
+        def gate_up(direct, near):
+            return pl.pallas_call(
+                gate_up_kernel,
+                grid=(ff // step,),
+                in_specs=blk + every[:2],
+                out_specs=[ab_block] * 2 + [pl.BlockSpec((half * step // ff, 2 * rows), lambda j: (j, 0))],
+                out_shape=[jax.ShapeDtypeStruct((2 * rows, ff), bf16)] * 2 + [jax.ShapeDtypeStruct((half, 2 * rows), bf16)],
+                scratch_shapes=[pltpu.VMEM((2 * rows, d_model), bf16)],
+                compiler_params=params,
+                cost_estimate=cost(4 * 2 * rows * d_model * ff),
+            )(direct, near, *w_all[:2])
 
         got = [flip(v, ["data"]) for v in grads[3:]]
-
-        late, late_got, step = [], [], 256
-        tok_n, dy_n, tok_xn = flip(tok_y, ["data"]), flip(dy_y, ["data"]), flip(tok_yx, ["data"])
-        groups = [(rows, (tok_y, tok_n, dy_y, dy_n)), (rows, (tok_yx, tok_xn, dy_yx, flip(dy_yx, ["data"])))]
-        for size, blocks in groups:
-            blk = [pl.BlockSpec((size, d_model), lambda j: (0, 0), pipeline_mode=once)] * 4
+        late, late_got = [], []
+        for x_blk, x_near, dy_blk, dy_near in ((tok_y, tok_n, dy_y, dy_n), (tok_yx, tok_xn, dy_yx, flip(dy_yx, ["data"]))):
+            a, b, x_t = gate_up(x_blk, x_near)
             outs = pl.pallas_call(
                 functools.partial(late_kernel, part),
                 grid=(ff // step,),
-                in_specs=blk + w_specs(step, lambda j: j),
-                out_specs=[pl.BlockSpec((step, 2 * size), lambda j: (j, 0))] + [pl.BlockSpec((2 * size, step), lambda j: (0, j))] * 2 + [pl.BlockSpec((part, 2 * size), lambda j: (0, 0)), pl.BlockSpec((2 * size, part), lambda j: (0, 0))] * 2,
-                out_shape=[jax.ShapeDtypeStruct((ff, 2 * size), bf16)] + [jax.ShapeDtypeStruct((2 * size, ff), bf16)] * 2 + [jax.ShapeDtypeStruct((part, 2 * size), bf16), jax.ShapeDtypeStruct((2 * size, part), bf16)] * 2,
-                scratch_shapes=[pltpu.VMEM((2 * size, d_model), bf16)] * 2,
-                compiler_params=params,
-                cost_estimate=cost(6 * 2 * size * d_model * ff),
-            )(*blocks, *w_all)
+                in_specs=blk + every[2:] + [ab_block] * 2 + [pl.BlockSpec((part, 2 * rows), fixed, pipeline_mode=once)],
+                out_specs=[pl.BlockSpec((step, 2 * rows), lambda j: (j, 0))] + [ab_block] * 2 + [pl.BlockSpec((part, 2 * rows), fixed), pl.BlockSpec((2 * rows, part), fixed)] * 2,
+                out_shape=[jax.ShapeDtypeStruct((ff, 2 * rows), bf16)] + [jax.ShapeDtypeStruct((2 * rows, ff), bf16)] * 2 + [jax.ShapeDtypeStruct((part, 2 * rows), bf16), jax.ShapeDtypeStruct((2 * rows, part), bf16)] * 2,
+                scratch_shapes=[pltpu.VMEM((2 * rows, d_model), bf16)],
+                compiler_params=params,
+                cost_estimate=cost(2 * 2 * rows * d_model * ff),
+            )(dy_blk, dy_near, w_all[2], a, b, x_t)
             late.append(outs)
             late_got.append([flip(v, ["data"]) for v in outs[:3]])
+        groups = [rows, rows]
         count = len(groups)
 
         finals = ()
@@ -312,7 +369,7 @@
         stages = [(grads[:3], core, [[*late[k][3:5], *late[k][:3]] for k in range(count)]), (got, 1 - core, [[*late[k][5:7], *late_got[k]] for k in range(count)])]
         for before, side, parts in stages:
             late_specs = []
-            for size, _ in groups:
+            for size in groups:
                 late_specs += [pl.BlockSpec((part, 2 * size), lambda j, c: (0, 0), pipeline_mode=once), pl.BlockSpec((2 * size, part), lambda j, c: (0, 0), pipeline_mode=once), pl.BlockSpec((unit, 2 * size), lambda j, c: (j, 0))] + [pl.BlockSpec((2 * size, unit), lambda j, c: (0, j))] * 2
             place_at = lambda j, c: c[0] * units + j
             finals = pl.pallas_call(

time: 751 us -> 755 us (level)
  Pallas kernels: 380 us -> 390 us
    pallas_call x0 -> x4, Pallas kernels: none -> 77.4 us  [the longest x2 46.3 us: gate_up(): pl.pallas_call(gate_up_kernel, grid=(ff // step,), in_specs=blk + every[:...]
    pallas_call x8 -> x4, Pallas kernels: 105 us -> 71.4 us  [sums(): pl.pallas_call(functools.partial(sum_kernel, down, before is not None), g...]
    pallas_call x2, Pallas kernels: 73 us -> 40.3 us  [local_step(): pl.pallas_call(functools.partial(late_kernel, part), grid=(ff // step,),...]
  transfers between devices with their start and end apart: 39 -> 39, of which waited for: 9 -> 9; matrix products, arithmetic and copies ran while one was open for 2% -> 2% of each run, Pallas kernels for 48% -> 49%
where the time goes in v3:
time: 755 us; the launch traced here: 751 us
  Pallas kernels  390 us (52%)
  waiting for transfers between devices  316 us (42%)
  starting transfers between devices  22.3 us (3%)
  other arithmetic  12.6 us (2%)
  local copies, waits for them, and re-layouts  8.88 us (1%)
    ppermute x39, waiting for transfers between devices, flip(): return lax.ppermute(value, AXES, [(i, i ^ mask) for i in range(8)])  316 us
    pallas_call x4, Pallas kernels, local_step(): pl.pallas_call(functools.partial(own_kernel, half), grid=(own_count // TI...  119 us
    pallas_call x4, Pallas kernels, sums(): pl.pallas_call(functools.partial(sum_kernel, down, before is not None), g...  71.4 us
    pallas_call x2, Pallas kernels, gate_up(): pl.pallas_call(gate_up_kernel, grid=(ff // step,), in_specs=blk + every[:...  46.3 us
    pallas_call x2, Pallas kernels, local_step(): pl.pallas_call(functools.partial(last_kernel, count), grid_spec=pltpu.Pre...  46.2 us
    pallas_call x2, Pallas kernels, local_step(): pl.pallas_call(functools.partial(late_kernel, part), grid=(ff // step,),...  40.3 us
    pallas_call x2, Pallas kernels, close(): pl.pallas_call(close_kernel, grid=(2 * rows // TILE,), in_specs=[act] * 3...  31.1 us
    ppermute x39, starting transfers between devices, flip(): return lax.ppermute(value, AXES, [(i, i ^ mask) for i in range(8)])  22.3 us
  transfers between devices with their start and end apart: 39, of which 9 were waited for; matrix products, arithmetic and copies ran while one was open for 2% of the time, Pallas kernels for 49%

profile of v3, /device:TPU:0, one launch (start us, length us, event | category | flops | bytes accessed | tf_op | source)
XLA Modules:
  0.0 751.0 jit_solution(17133259020704442569)
XLA Ops:
  0.7 2.5 constant_dynamic-slice_fusion.27
  3.4 1.8 pad_maximum_fusion.refs_0_.residual
  5.2 3.3 collective-permute-start.3
  8.6 46.6 %collective-permute-done.3.refs_1_ = bf16[512,2048]{1,0:T(8,128)(2,1)} collective-permute-done((bf16[512,2048]{1,0:T(8,128)(2,1)S(1)}, bf16[512,2048]{1,0:T(8,128)(2,1)}, u32[]{:S(2)}, u32[]{:S(2)}) %collective-permute-start.3) | collective-permute-done | bytes 2097184 | tf_op jit(solution)/shard_map/ppermute | solution.py:178
  55.6 3.6 constant_dynamic-slice_fusion.2
  59.2 1.5 copy-done.3
  60.8 1.3 constant_dynamic-slice_fusion
  62.1 37.1 %collective-permute-done.refs_1_ = bf16[512,2048]{1,0:T(8,128)(2,1)} collective-permute-done((bf16[512,2048]{1,0:T(8,128)(2,1)}, bf16[512,2048]{1,0:T(8,128)(2,1)}, u32[]{:S(2)}, u32[]{:S(2)}) %collective-permute-start) | collective-permute-done | bytes 2097184 | tf_op jit(solution)/shard_map/ppermute | solution.py:178
  99.2 2.3 pad_maximum_fusion.9
  102.0 1.3 pad_maximum_fusion.8.refs_2_
  103.3 1.4 collective-permute-start.17
  106.4 1.3 pad_maximum_fusion.6.refs_2_
  107.6 1.3 pad_maximum_fusion.4.refs_2_
  111.5 7.6 %shard_map.93 = bf16[4,512,2048]{2,1,0:T(8,128)(2,1)} custom-call(bf16[512,2048]{1,0:T(8,128)(2,1)} %copy-done, bf16[512,2048]{1,0:T(8,128)(2,1)} %collective-permute-done.3.refs_1_, bf16[512,2048]{1,0:T(8,128)(2,1)} %collective-permute-done.4.refs_2_, bf16[512,2048]{1,0:T(8,128)(2,1)} %collective-permute-done.5.refs_3_), custom_call_target="tpu_custom_call" | custom-call | flops 1000000 | bytes 16777216 | tf_op jit(solution)/shard_map/pallas_call | solution.py:164
  119.2 1.6 collective-permute-start.14
  120.9 7.0 shard_map.92
  128.0 46.4 %collective-permute-done.16.refs_4_ = bf16[1536,512]{1,0:T(8,128)(2,1)} collective-permute-done((bf16[1536,512]{1,0:T(8,128)(2,1)}, bf16[1536,512]{1,0:T(8,128)(2,1)}, u32[]{:S(2)}, u32[]{:S(2)}) %collective-permute-start.16) | collective-permute-done | bytes 1572896 | tf_op jit(solution)/shard_map/ppermute | solution.py:178
  174.4 1.6 collective-permute-start.13
  176.0 29.6 %shard_map.94 = (bf16[2048,2048]{1,0:T(8,128)(2,1)}, bf16[2048,2048]{1,0:T(8,128)(2,1)}, bf16[2048,2048]{1,0:T(8,128)(2,1)}, bf16[2048,2048]{1,0:T(8,128)(2,1)},...) custom-call(bf16[2048,2048]{1,0:T(8,128)(2,1)} %bitcast.8, ...), custom_call_target="tpu_custom_call" | custom-call | flops 19327352832 | bytes 52428800 | tf_op jit(solution)/shard_map/pallas_call | solution.py:257
  205.9 69.3 %collective-permute-done.13.refs_4_ = bf16[1536,512]{1,0:T(8,128)(2,1)} collective-permute-done((bf16[1536,512]{1,0:T(8,128)(2,1)}, bf16[1536,512]{1,0:T(8,128)(2,1)}, u32[]{:S(2)}, u32[]{:S(2)}) %collective-permute-start.13) | collective-permute-done | bytes 1572896 | tf_op jit(solution)/shard_map/ppermute | solution.py:178
  275.1 1.3 collective-permute-start.8
  276.9 29.8 %shard_map.95 = (bf16[2048,2048]{1,0:T(8,128)(2,1)}, bf16[2048,2048]{1,0:T(8,128)(2,1)}, bf16[2048,2048]{1,0:T(8,128)(2,1)}, bf16[2048,2048]{1,0:T(8,128)(2,1)},...) custom-call(bf16[2048,2048]{1,0:T(8,128)(2,1)} %bitcast.9, ...), custom_call_target="tpu_custom_call", output_to_operand_aliasing={{0}: (6, {}), {1}: (7, {}), {2}: (8, {}), {3}: (9, {}), {4}... | custom-call | flops 19327352832 | bytes 52428800 | tf_op jit(solution)/shard_map/pallas_call | solution.py:257
  306.7 14.1 %shard_map.98.refs_2_ = f32[2048,2048]{1,0:T(8,128)} custom-call(bf16[2048,2048]{1,0:T(8,128)(2,1)} %get-tuple-element.99.refs_6_.refs_0_, bf16[2048,2048]{1,0:T(8,128)(2,1)} %get-tuple-element.104.refs_11_.refs_1_), custom_call_target="tpu_custom_call" | custom-call | flops 8589934592 | bytes 52428800 | tf_op jit(solution)/shard_map/pallas_call | solution.py:238
  320.8 24.2 %shard_map.100.refs_4_ = f32[2048,2048]{1,0:T(8,128)} custom-call(bf16[2048,2048]{1,0:T(8,128)(2,1)} %get-tuple-element.100.refs_7_.refs_0_, bf16[2048,2048]{1,0:T(8,128)(2,1)} %get-tuple-element.101.refs_8_.refs_1_, bf16[2048,2048]{1,0:T(8,128)(2,1)} %get-tuple-element.102.refs_9_.refs_2_, bf16[2048,2048]{1,0:T(8,128)(2,1)} %get-tuple-element.103.refs_10_.refs_3_), custom_call_target="tpu_custom_call" | custom-call | flops 17179869184 | bytes 52428800 | tf_op jit(solution)/shard_map/pallas_call | solution.py:238
  345.9 1.8 collective-permute-start.24
  347.9 1.8 collective-permute-start.7
  349.7 29.8 %shard_map.96 = (bf16[2048,2048]{1,0:T(8,128)(2,1)}, bf16[2048,2048]{1,0:T(8,128)(2,1)}, bf16[2048,2048]{1,0:T(8,128)(2,1)}, bf16[2048,2048]{1,0:T(8,128)(2,1)},...) custom-call(bf16[2048,2048]{1,0:T(8,128)(2,1)} %bitcast.10, ...), custom_call_target="tpu_custom_call", output_to_operand_aliasing={{0}: (6, {}), {1}: (7, {}), {2}: (8, {}), {3}: (9, {}), {4}... | custom-call | flops 19327352832 | bytes 52428800 | tf_op jit(solution)/shard_map/pallas_call | solution.py:257
  379.5 14.2 %shard_map.99.y_old = f32[2048,2048]{1,0:T(8,128)} custom-call(bf16[2048,2048]{1,0:T(8,128)(2,1)} %get-tuple-element.111.refs_6_.refs_0_, bf16[2048,2048]{1,0:T(8,128)(2,1)} %get-tuple-element.116.refs_11_.refs_1_, f32[2048,2048]{1,0:T(8,128)} %shard_map.98.refs_2_), custom_call_target="tpu_custom_call" | custom-call | flops 4294967296 | bytes 52428800 | tf_op jit(solution)/shard_map/pallas_call | solution.py:238
  393.6 19.0 %shard_map.101.dx_old = f32[2048,2048]{1,0:T(8,128)} custom-call(bf16[2048,2048]{1,0:T(8,128)(2,1)} %get-tuple-element.112.refs_7_.refs_0_, bf16[2048,2048]{1,0:T(8,128)(2,1)} %get-tuple-element.113.refs_8_.refs_1_, bf16[2048,2048]{1,0:T(8,128)(2,1)} %get-tuple-element.114.refs_9_.refs_2_, bf16[2048,2048]{1,0:T(8,128)(2,1)} %get-tuple-element.115.refs_10_.refs_3_, ...), custom_call_target="tpu_custom_call" | custom-call | flops 8589934592 | bytes 52428800 | tf_op jit(solution)/shard_map/pallas_call | solution.py:238
  412.9 1.7 collective-permute-start.31
  414.6 58.7 %collective-permute-done.7.refs_4_ = bf16[1536,512]{1,0:T(8,128)(2,1)} collective-permute-done((bf16[1536,512]{1,0:T(8,128)(2,1)S(1)}, bf16[1536,512]{1,0:T(8,128)(2,1)}, u32[]{:S(2)}, u32[]{:S(2)}) %collective-permute-start.7) | collective-permute-done | bytes 1572896 | tf_op jit(solution)/shard_map/ppermute | solution.py:178
  473.8 29.9 %shard_map.97 = (bf16[2048,2048]{1,0:T(8,128)(2,1)}, bf16[2048,2048]{1,0:T(8,128)(2,1)}, bf16[2048,2048]{1,0:T(8,128)(2,1)}, bf16[2048,2048]{1,0:T(8,128)(2,1)},...) custom-call(bf16[2048,2048]{1,0:T(8,128)(2,1)} %bitcast.11, ...), custom_call_target="tpu_custom_call", output_to_operand_aliasing={{0}: (6, {}), {1}: (7, {}), {2}: (8, {}), {3}: (9, {}), {4}... | custom-call | flops 19327352832 | bytes 52428800 | tf_op jit(solution)/shard_map/pallas_call | solution.py:257
  503.7 15.6 %shard_map.103 = (bf16[1024,2048]{1,0:T(8,128)(2,1)}, bf16[1024,2048]{1,0:T(8,128)(2,1)}) custom-call(bf16[2048,2048]{1,0:T(8,128)(2,1)} %get-tuple-element.123.h, bf16[2048,2048]{1,0:T(8,128)(2,1)} %get-tuple-element.124.da, bf16[2048,2048]{1,0:T(8,128)(2,1)} %get-tuple-element.125.db, bf16[2048,2048]{1,0:T(8,128)(2,1)} %get-tuple-element.126.wg, ...), custom_call_target="tpu_custom_call" | custom-call | flops 6442450944 | bytes 52428800 | tf_op jit(solution)/shard_map/pallas_call | solution.py:278
  519.9 23.1 %shard_map.108 = (bf16[1024,2048]{1,0:T(8,128)(2,1)}, bf16[1024,2048]{1,0:T(8,128)(2,1)}, bf16[1024,1024]{1,0:T(8,128)(2,1)}) custom-call(bf16[512,2048]{1,0:T(8,128)(2,1)} %collective-permute-done.24.xd, bf16[512,2048]{1,0:T(8,128)(2,1)} %collective-permute-done.25.xp, bf16[2048,2048]{1,0:T(8,128)(2,1)} %get-tuple-element.126.wg, ...), custom_call_target="tpu_custom_call" | custom-call | flops 17179869184 | bytes 52428800 | tf_op jit(solution)/shard_map/pallas_call | solution.py:336
  543.0 20.2 %shard_map.109 = (bf16[2048,1024]{1,0:T(8,128)(2,1)}, bf16[1024,2048]{1,0:T(8,128)(2,1)}, bf16[1024,2048]{1,0:T(8,128)(2,1)}, bf16[512,1024]{1,0:T(8,128)(2,1)},...) custom-call(bf16[512,2048]{1,0:T(8,128)(2,1)} %collective-permute-done.22.dyd, ...), custom_call_target="tpu_custom_call" | custom-call | flops 8589934592 | bytes 52428800 | tf_op jit(solution)/shard_map/pallas_call | solution.py:351
  563.8 9.9 %collective-permute-done.32.xp = bf16[512,2048]{1,0:T(8,128)(2,1)} collective-permute-done((bf16[512,2048]{1,0:T(8,128)(2,1)}, bf16[512,2048]{1,0:T(8,128)(2,1)}, u32[]{:S(2)}, u32[]{:S(2)}) %collective-permute-start.32) | collective-permute-done | bytes 2097184 | tf_op jit(solution)/shard_map/ppermute | solution.py:178
  574.4 15.4 %shard_map.102 = (bf16[1024,2048]{1,0:T(8,128)(2,1)}, bf16[1024,2048]{1,0:T(8,128)(2,1)}) custom-call(bf16[2048,2048]{1,0:T(8,128)(2,1)} %get-tuple-element.123.h, bf16[2048,2048]{1,0:T(8,128)(2,1)} %get-tuple-element.124.da, bf16[2048,2048]{1,0:T(8,128)(2,1)} %get-tuple-element.125.db, bf16[2048,2048]{1,0:T(8,128)(2,1)} %get-tuple-element.126.wg, ...), custom_call_target="tpu_custom_call" | custom-call | flops 6442450944 | bytes 52428800 | tf_op jit(solution)/shard_map/pallas_call | solution.py:278
  589.8 4.3 shard_map.106
  594.2 4.3 shard_map.104
  598.5 1.7 collective-permute-start.21
  600.5 23.1 %shard_map.110 = (bf16[1024,2048]{1,0:T(8,128)(2,1)}, bf16[1024,2048]{1,0:T(8,128)(2,1)}, bf16[1024,1024]{1,0:T(8,128)(2,1)}) custom-call(bf16[512,2048]{1,0:T(8,128)(2,1)} %collective-permute-done.31.xd, bf16[512,2048]{1,0:T(8,128)(2,1)} %collective-permute-done.32.xp, bf16[2048,2048]{1,0:T(8,128)(2,1)} %get-tuple-element.126.wg, ...), custom_call_target="tpu_custom_call" | custom-call | flops 17179869184 | bytes 52428800 | tf_op jit(solution)/shard_map/pallas_call | solution.py:336
  623.7 20.1 %shard_map.111 = (bf16[2048,1024]{1,0:T(8,128)(2,1)}, bf16[1024,2048]{1,0:T(8,128)(2,1)}, bf16[1024,2048]{1,0:T(8,128)(2,1)}, bf16[512,1024]{1,0:T(8,128)(2,1)},...) custom-call(bf16[512,2048]{1,0:T(8,128)(2,1)} %collective-permute-done.29.dyd, ...), custom_call_target="tpu_custom_call" | custom-call | flops 8589934592 | bytes 52428800 | tf_op jit(solution)/shard_map/pallas_call | solution.py:351
  644.3 3.0 collective-permute-done.21.far
  647.3 44.3 %collective-permute-done.19.far = bf16[512,2048]{1,0:T(8,128)(2,1)} collective-permute-done((bf16[512,2048]{1,0:T(8,128)(2,1)}, bf16[512,2048]{1,0:T(8,128)(2,1)}, u32[]{:S(2)}, u32[]{:S(2)}) %collective-permute-start.19) | collective-permute-done | bytes 2097184 | tf_op jit(solution)/shard_map/ppermute | solution.py:178
  692.2 23.1 %shard_map.112 = (f32[512,4096]{1,0:T(8,128)}, f32[512,4096]{1,0:T(8,128)}, f32[4096,512]{1,0:T(8,128)}) custom-call(s32[1]{0:T(128)} %bitcast.3.where, bf16[512,1024]{1,0:T(8,128)(2,1)} %get-tuple-element.152.refs_0_, bf16[1024,512]{1,0:T(8,128)(2,1)} %get-tuple-element.153.refs_1_, bf16[2048,1024]{1,0:T(8,128)(2,1)} %get-tuple-element.138.refs_2_, ...), custom_call_target="tpu_custom_call" | custom-call | flops 12884901888 | bytes 52428800 | tf_op jit(solution)/shard_map/pallas_call | solution.py:375
  715.2 6.2 shard_map.107
  721.4 6.2 shard_map.105
  727.7 23.1 %shard_map.113 = (f32[512,4096]{1,0:T(8,128)}, f32[512,4096]{1,0:T(8,128)}, f32[4096,512]{1,0:T(8,128)}) custom-call(s32[1]{0:T(128)} %bitcast.2.where, bf16[512,1024]{1,0:T(8,128)(2,1)} %get-tuple-element.136.refs_0_, bf16[1024,512]{1,0:T(8,128)(2,1)} %get-tuple-element.137.refs_1_, ...), custom_call_target="tpu_custom_call", output_to_operand_aliasing={{0}: (14, {}), {1}: (15, {}), {2}: (16, {})} | custom-call | flops 12884901888 | bytes 52428800 | tf_op jit(solution)/shard_map/pallas_call | solution.py:375
  (76 shorter events, 11.6 us)
Async XLA Ops:
  3.4 55.8 %copy-start = (bf16[512,2048]{1,0:T(8,128)(2,1)}, bf16[512,2048]{1,0:T(8,128)(2,1)S(1)}, u32[]{:S(2)}) copy-start(bf16[512,2048]{1,0:T(8,128)(2,1)S(1)} %pad_maximum_fusion.1.refs_0_.residual) | copy-start | bytes 6291460
  5.2 49.9 %collective-permute-start.3 = (bf16[512,2048]{1,0:T(8,128)(2,1)S(1)}, bf16[512,2048]{1,0:T(8,128)(2,1)}, u32[]{:S(2)}, u32[]{:S(2)}) collective-permute-start(bf16[512,2048]{1,0:T(8,128)(2,1)S(1)} %pad_maximum_fusion.1.refs_0_.residual), channel_id=1, source_target_pairs={{0,2},{1,3},{2,0},{3,1},{4,6},{5,7},{6,4},{7,5}} | collective-permute-start | bytes 6291464 | tf_op jit(solution)/shard_map/ppermute | solution.py:178
  8.5 90.7 %collective-permute-start = (bf16[512,2048]{1,0:T(8,128)(2,1)}, bf16[512,2048]{1,0:T(8,128)(2,1)}, u32[]{:S(2)}, u32[]{:S(2)}) collective-permute-start(bf16[512,2048]{1,0:T(8,128)(2,1)} %pad_maximum_fusion.refs_0_.residual), channel_id=1, source_target_pairs={{0,2},{1,3},{2,0},{3,1},{4,6},{5,7},{6,4},{7,5}} | collective-permute-start | bytes 6291464 | tf_op jit(solution)/shard_map/ppermute | solution.py:178
  8.6 94.7 %collective-permute-start.4 = (bf16[512,2048]{1,0:T(8,128)(2,1)S(1)}, bf16[512,2048]{1,0:T(8,128)(2,1)}, u32[]{:S(2)}, u32[]{:S(2)}) collective-permute-start(bf16[512,2048]{1,0:T(8,128)(2,1)S(1)} %pad_maximum_fusion.1.refs_0_.residual), channel_id=1, source_target_pairs={{0,1},{1,0},{2,3},{3,2},{4,5},{5,4},{6,7},{7,6}} | collective-permute-start | bytes 6291464 | tf_op jit(solution)/shard_map/ppermute | solution.py:178
  55.1 49.6 %collective-permute-start.5 = (bf16[512,2048]{1,0:T(8,128)(2,1)}, bf16[512,2048]{1,0:T(8,128)(2,1)}, u32[]{:S(2)}, u32[]{:S(2)}) collective-permute-start(bf16[512,2048]{1,0:T(8,128)(2,1)} %collective-permute-done.3.refs_1_), channel_id=1, source_target_pairs={{0,1},{1,0},{2,3},{3,2},{4,5},{5,4},{6,7},{7,6}} | collective-permute-start | bytes 6291464 | tf_op jit(solution)/shard_map/ppermute | solution.py:178
  55.1 64.0 %collective-permute-start.1 = (bf16[512,2048]{1,0:T(8,128)(2,1)}, bf16[512,2048]{1,0:T(8,128)(2,1)}, u32[]{:S(2)}, u32[]{:S(2)}) collective-permute-start(bf16[512,2048]{1,0:T(8,128)(2,1)} %pad_maximum_fusion.refs_0_.residual), channel_id=1, source_target_pairs={{0,1},{1,0},{2,3},{3,2},{4,5},{5,4},{6,7},{7,6}} | collective-permute-start | bytes 6291464 | tf_op jit(solution)/shard_map/ppermute | solution.py:178
  55.6 3.6 copy-start.2
  55.6 5.1 copy-start.3
  62.1 40.0 %copy-start.4 = (bf16[512,512]{1,0:T(8,128)(2,1)S(1)}, bf16[512,512]{1,0:T(8,128)(2,1)}, u32[]{:S(2)}) copy-start(bf16[512,512]{1,0:T(8,128)(2,1)} %get-tuple-element.172) | copy-start | bytes 1572868
  99.2 20.0 %collective-permute-start.2 = (bf16[512,2048]{1,0:T(8,128)(2,1)}, bf16[512,2048]{1,0:T(8,128)(2,1)}, u32[]{:S(2)}, u32[]{:S(2)}) collective-permute-start(bf16[512,2048]{1,0:T(8,128)(2,1)} %collective-permute-done.refs_1_), channel_id=1, source_target_pairs={{0,1},{1,0},{2,3},{3,2},{4,5},{5,4},{6,7},{7,6}} | collective-permute-start | bytes 6291464 | tf_op jit(solution)/shard_map/ppermute | solution.py:178
  101.5 26.4 %collective-permute-start.15 = (bf16[1536,512]{1,0:T(8,128)(2,1)}, bf16[1536,512]{1,0:T(8,128)(2,1)}, u32[]{:S(2)}, u32[]{:S(2)}) collective-permute-start(bf16[1536,512]{1,0:T(8,128)(2,1)} %pad_maximum_fusion.9), channel_id=1, source_target_pairs={{0,1},{1,0},{2,3},{3,2},{4,5},{5,4},{6,7},{7,6}} | collective-permute-start | bytes 4718600 | tf_op jit(solution)/shard_map/ppermute | solution.py:178
  103.3 71.0 %collective-permute-start.17 = (bf16[1536,512]{1,0:T(8,128)(2,1)}, bf16[1536,512]{1,0:T(8,128)(2,1)}, u32[]{:S(2)}, u32[]{:S(2)}) collective-permute-start(bf16[1536,512]{1,0:T(8,128)(2,1)} %pad_maximum_fusion.9), channel_id=1, source_target_pairs={{0,5},{1,4},{2,7},{3,6},{4,1},{5,0},{6,3},{7,2}} | collective-permute-start | bytes 4718600 | tf_op jit(solution)/shard_map/ppermute | solution.py:178
  104.7 69.7 %collective-permute-start.16 = (bf16[1536,512]{1,0:T(8,128)(2,1)}, bf16[1536,512]{1,0:T(8,128)(2,1)}, u32[]{:S(2)}, u32[]{:S(2)}) collective-permute-start(bf16[1536,512]{1,0:T(8,128)(2,1)} %pad_maximum_fusion.8.refs_2_), channel_id=1, source_target_pairs={{0,4},{1,5},{2,6},{3,7},{4,0},{5,1},{6,2},{7,3}} | collective-permute-start | bytes 4718600 | tf_op jit(solution)/shard_map/ppermute | solution.py:178
  111.5 236.4 %copy-start.1 = (bf16[1536,512]{1,0:T(8,128)(2,1)}, bf16[1536,512]{1,0:T(8,128)(2,1)S(1)}, u32[]{:S(2)}) copy-start(bf16[1536,512]{1,0:T(8,128)(2,1)S(1)} %pad_maximum_fusion.2.refs_2_) | copy-start | bytes 4718596
  119.1 86.5 %collective-permute-start.12 = (bf16[1536,512]{1,0:T(8,128)(2,1)}, bf16[1536,512]{1,0:T(8,128)(2,1)}, u32[]{:S(2)}, u32[]{:S(2)}) collective-permute-start(bf16[1536,512]{1,0:T(8,128)(2,1)} %pad_maximum_fusion.7), channel_id=1, source_target_pairs={{0,1},{1,0},{2,3},{3,2},{4,5},{5,4},{6,7},{7,6}} | collective-permute-start | bytes 4718600 | tf_op jit(solution)/shard_map/ppermute | solution.py:178
  119.2 157.2 %collective-permute-start.14 = (bf16[1536,512]{1,0:T(8,128)(2,1)}, bf16[1536,512]{1,0:T(8,128)(2,1)}, u32[]{:S(2)}, u32[]{:S(2)}) collective-permute-start(bf16[1536,512]{1,0:T(8,128)(2,1)} %pad_maximum_fusion.7), channel_id=1, source_target_pairs={{0,5},{1,4},{2,7},{3,6},{4,1},{5,0},{6,3},{7,2}} | collective-permute-start | bytes 4718600 | tf_op jit(solution)/shard_map/ppermute | solution.py:178
  127.9 219.8 %collective-permute-start.11 = (bf16[1536,512]{1,0:T(8,128)(2,1)}, bf16[1536,512]{1,0:T(8,128)(2,1)}, u32[]{:S(2)}, u32[]{:S(2)}) collective-permute-start(bf16[1536,512]{1,0:T(8,128)(2,1)} %pad_maximum_fusion.5), channel_id=1, source_target_pairs={{0,5},{1,4},{2,7},{3,6},{4,1},{5,0},{6,3},{7,2}} | collective-permute-start | bytes 4718600 | tf_op jit(solution)/shard_map/ppermute | solution.py:178
  174.4 173.5 %collective-permute-start.9 = (bf16[1536,512]{1,0:T(8,128)(2,1)}, bf16[1536,512]{1,0:T(8,128)(2,1)}, u32[]{:S(2)}, u32[]{:S(2)}) collective-permute-start(bf16[1536,512]{1,0:T(8,128)(2,1)} %pad_maximum_fusion.5), channel_id=1, source_target_pairs={{0,1},{1,0},{2,3},{3,2},{4,5},{5,4},{6,7},{7,6}} | collective-permute-start | bytes 4718600 | tf_op jit(solution)/shard_map/ppermute | solution.py:178
  174.4 100.8 %collective-permute-start.13 = (bf16[1536,512]{1,0:T(8,128)(2,1)}, bf16[1536,512]{1,0:T(8,128)(2,1)}, u32[]{:S(2)}, u32[]{:S(2)}) collective-permute-start(bf16[1536,512]{1,0:T(8,128)(2,1)} %pad_maximum_fusion.6.refs_2_), channel_id=1, source_target_pairs={{0,4},{1,5},{2,6},{3,7},{4,0},{5,1},{6,2},{7,3}} | collective-permute-start | bytes 4718600 | tf_op jit(solution)/shard_map/ppermute | solution.py:178
  205.6 207.0 %collective-permute-start.6 = (bf16[1536,512]{1,0:T(8,128)(2,1)}, bf16[1536,512]{1,0:T(8,128)(2,1)}, u32[]{:S(2)}, u32[]{:S(2)}) collective-permute-start(bf16[1536,512]{1,0:T(8,128)(2,1)} %pad_maximum_fusion.3), channel_id=1, source_target_pairs={{0,1},{1,0},{2,3},{3,2},{4,5},{5,4},{6,7},{7,6}} | collective-permute-start | bytes 4718600 | tf_op jit(solution)/shard_map/ppermute | solution.py:178
  275.1 198.7 %collective-permute-start.8 = (bf16[1536,512]{1,0:T(8,128)(2,1)}, bf16[1536,512]{1,0:T(8,128)(2,1)}, u32[]{:S(2)}, u32[]{:S(2)}) collective-permute-start(bf16[1536,512]{1,0:T(8,128)(2,1)} %pad_maximum_fusion.3), channel_id=1, source_target_pairs={{0,5},{1,4},{2,7},{3,6},{4,1},{5,0},{6,3},{7,2}} | collective-permute-start | bytes 4718600 | tf_op jit(solution)/shard_map/ppermute | solution.py:178
  276.5 69.4 %collective-permute-start.10 = (bf16[1536,512]{1,0:T(8,128)(2,1)}, bf16[1536,512]{1,0:T(8,128)(2,1)}, u32[]{:S(2)}, u32[]{:S(2)}) collective-permute-start(bf16[1536,512]{1,0:T(8,128)(2,1)} %pad_maximum_fusion.4.refs_2_), channel_id=1, source_target_pairs={{0,4},{1,5},{2,6},{3,7},{4,0},{5,1},{6,2},{7,3}} | collective-permute-start | bytes 4718600 | tf_op jit(solution)/shard_map/ppermute | solution.py:178
  345.9 67.0 %collective-permute-start.24 = (bf16[512,2048]{1,0:T(8,128)(2,1)}, bf16[512,2048]{1,0:T(8,128)(2,1)}, u32[]{:S(2)}, u32[]{:S(2)}) collective-permute-start(bf16[512,2048]{1,0:T(8,128)(2,1)} %pad_maximum_fusion.refs_0_.residual), channel_id=1, source_target_pairs={{0,4},{1,5},{2,6},{3,7},{4,0},{5,1},{6,2},{7,3}} | collective-permute-start | bytes 6291464 | tf_op jit(solution)/shard_map/ppermute | solution.py:178
  347.6 125.7 %collective-permute-start.22 = (bf16[512,2048]{1,0:T(8,128)(2,1)}, bf16[512,2048]{1,0:T(8,128)(2,1)}, u32[]{:S(2)}, u32[]{:S(2)}) collective-permute-start(bf16[512,2048]{1,0:T(8,128)(2,1)} %copy-done), channel_id=1, source_target_pairs={{0,4},{1,5},{2,6},{3,7},{4,0},{5,1},{6,2},{7,3}} | collective-permute-start | bytes 6291464 | tf_op jit(solution)/shard_map/ppermute | solution.py:178
  347.9 125.4 %collective-permute-start.7 = (bf16[1536,512]{1,0:T(8,128)(2,1)S(1)}, bf16[1536,512]{1,0:T(8,128)(2,1)}, u32[]{:S(2)}, u32[]{:S(2)}) collective-permute-start(bf16[1536,512]{1,0:T(8,128)(2,1)S(1)} %pad_maximum_fusion.2.refs_2_), channel_id=1, source_target_pairs={{0,4},{1,5},{2,6},{3,7},{4,0},{5,1},{6,2},{7,3}} | collective-permute-start | bytes 4718600 | tf_op jit(solution)/shard_map/ppermute | solution.py:178
  412.6 151.1 %collective-permute-start.29 = (bf16[512,2048]{1,0:T(8,128)(2,1)}, bf16[512,2048]{1,0:T(8,128)(2,1)}, u32[]{:S(2)}, u32[]{:S(2)}) collective-permute-start(bf16[512,2048]{1,0:T(8,128)(2,1)} %collective-permute-done.3.refs_1_), channel_id=1, source_target_pairs={{0,4},{1,5},{2,6},{3,7},{4,0},{5,1},{6,2},{7,3}} | collective-permute-start | bytes 6291464 | tf_op jit(solution)/shard_map/ppermute | solution.py:178
  412.9 150.4 %collective-permute-start.31 = (bf16[512,2048]{1,0:T(8,128)(2,1)}, bf16[512,2048]{1,0:T(8,128)(2,1)}, u32[]{:S(2)}, u32[]{:S(2)}) collective-permute-start(bf16[512,2048]{1,0:T(8,128)(2,1)} %collective-permute-done.24.xd), channel_id=1, source_target_pairs={{0,2},{1,3},{2,0},{3,1},{4,6},{5,7},{6,4},{7,5}} | collective-permute-start | bytes 6291464 | tf_op jit(solution)/shard_map/ppermute | solution.py:178
  473.3 46.1 %collective-permute-start.25 = (bf16[512,2048]{1,0:T(8,128)(2,1)}, bf16[512,2048]{1,0:T(8,128)(2,1)}, u32[]{:S(2)}, u32[]{:S(2)}) collective-permute-start(bf16[512,2048]{1,0:T(8,128)(2,1)} %collective-permute-done.24.xd), channel_id=1, source_target_pairs={{0,1},{1,0},{2,3},{3,2},{4,5},{5,4},{6,7},{7,6}} | collective-permute-start | bytes 6291464 | tf_op jit(solution)/shard_map/ppermute | solution.py:178
  473.3 69.7 %collective-permute-start.23 = (bf16[512,2048]{1,0:T(8,128)(2,1)}, bf16[512,2048]{1,0:T(8,128)(2,1)}, u32[]{:S(2)}, u32[]{:S(2)}) collective-permute-start(bf16[512,2048]{1,0:T(8,128)(2,1)} %collective-permute-done.22.dyd), channel_id=1, source_target_pairs={{0,1},{1,0},{2,3},{3,2},{4,5},{5,4},{6,7},{7,6}} | collective-permute-start | bytes 6291464 | tf_op jit(solution)/shard_map/ppermute | solution.py:178
  519.3 54.5 %collective-permute-start.20 = (bf16[1024,2048]{1,0:T(8,128)(2,1)}, bf16[1024,2048]{1,0:T(8,128)(2,1)}, u32[]{:S(2)}, u32[]{:S(2)}) collective-permute-start(bf16[1024,2048]{1,0:T(8,128)(2,1)} %get-tuple-element.132), channel_id=1, source_target_pairs={{0,1},{1,0},{2,3},{3,2},{4,5},{5,4},{6,7},{7,6}} | collective-permute-start | bytes 12582920 | tf_op jit(solution)/shard_map/ppermute | solution.py:178
  519.4 54.9 %collective-permute-start.18 = (bf16[1024,2048]{1,0:T(8,128)(2,1)}, bf16[1024,2048]{1,0:T(8,128)(2,1)}, u32[]{:S(2)}, u32[]{:S(2)}) collective-permute-start(bf16[1024,2048]{1,0:T(8,128)(2,1)} %get-tuple-element.130), channel_id=1, source_target_pairs={{0,1},{1,0},{2,3},{3,2},{4,5},{5,4},{6,7},{7,6}} | collective-permute-start | bytes 12582920 | tf_op jit(solution)/shard_map/ppermute | solution.py:178
  563.2 37.0 %collective-permute-start.26 = (bf16[2048,1024]{1,0:T(8,128)(2,1)}, bf16[2048,1024]{1,0:T(8,128)(2,1)}, u32[]{:S(2)}, u32[]{:S(2)}) collective-permute-start(bf16[2048,1024]{1,0:T(8,128)(2,1)} %get-tuple-element.138.refs_2_), channel_id=1, source_target_pairs={{0,1},{1,0},{2,3},{3,2},{4,5},{5,4},{6,7},{7,6}} | collective-permute-start | bytes 12582920 | tf_op jit(solution)/shard_map/ppermute | solution.py:178
  563.3 10.5 %collective-permute-start.32 = (bf16[512,2048]{1,0:T(8,128)(2,1)}, bf16[512,2048]{1,0:T(8,128)(2,1)}, u32[]{:S(2)}, u32[]{:S(2)}) collective-permute-start(bf16[512,2048]{1,0:T(8,128)(2,1)} %collective-permute-done.31.xd), channel_id=1, source_target_pairs={{0,1},{1,0},{2,3},{3,2},{4,5},{5,4},{6,7},{7,6}} | collective-permute-start | bytes 6291464 | tf_op jit(solution)/shard_map/ppermute | solution.py:178
  563.8 34.7 %collective-permute-start.30 = (bf16[512,2048]{1,0:T(8,128)(2,1)}, bf16[512,2048]{1,0:T(8,128)(2,1)}, u32[]{:S(2)}, u32[]{:S(2)}) collective-permute-start(bf16[512,2048]{1,0:T(8,128)(2,1)} %collective-permute-done.29.dyd), channel_id=1, source_target_pairs={{0,1},{1,0},{2,3},{3,2},{4,5},{5,4},{6,7},{7,6}} | collective-permute-start | bytes 6291464 | tf_op jit(solution)/shard_map/ppermute | solution.py:178
  573.7 70.0 %collective-permute-start.27 = (bf16[1024,2048]{1,0:T(8,128)(2,1)}, bf16[1024,2048]{1,0:T(8,128)(2,1)}, u32[]{:S(2)}, u32[]{:S(2)}) collective-permute-start(bf16[1024,2048]{1,0:T(8,128)(2,1)} %get-tuple-element.139.refs_3_), channel_id=1, source_target_pairs={{0,1},{1,0},{2,3},{3,2},{4,5},{5,4},{6,7},{7,6}} | collective-permute-start | bytes 12582920 | tf_op jit(solution)/shard_map/ppermute | solution.py:178
  573.9 69.9 %collective-permute-start.28 = (bf16[1024,2048]{1,0:T(8,128)(2,1)}, bf16[1024,2048]{1,0:T(8,128)(2,1)}, u32[]{:S(2)}, u32[]{:S(2)}) collective-permute-start(bf16[1024,2048]{1,0:T(8,128)(2,1)} %get-tuple-element.140.refs_4_), channel_id=1, source_target_pairs={{0,1},{1,0},{2,3},{3,2},{4,5},{5,4},{6,7},{7,6}} | collective-permute-start | bytes 12582920 | tf_op jit(solution)/shard_map/ppermute | solution.py:178
  574.3 70.0 %collective-permute-start.36 = (f32[512,2048]{1,0:T(8,128)}, f32[512,2048]{1,0:T(8,128)}, u32[]{:S(2)}, u32[]{:S(2)}) collective-permute-start(f32[512,2048]{1,0:T(8,128)} %get-tuple-element.149), channel_id=1, source_target_pairs={{0,1},{1,0},{2,3},{3,2},{4,5},{5,4},{6,7},{7,6}} | collective-permute-start | bytes 12582920 | tf_op jit(solution)/shard_map/ppermute | solution.py:178
  598.5 48.8 %collective-permute-start.21 = (bf16[512,2048]{1,0:T(8,128)(2,1)}, bf16[512,2048]{1,0:T(8,128)(2,1)}, u32[]{:S(2)}, u32[]{:S(2)}) collective-permute-start(bf16[512,2048]{1,0:T(8,128)(2,1)} %shard_map.106), channel_id=1, source_target_pairs={{0,2},{1,3},{2,0},{3,1},{4,6},{5,7},{6,4},{7,5}} | collective-permute-start | bytes 6291464 | tf_op jit(solution)/shard_map/ppermute | solution.py:178
  600.2 91.4 %collective-permute-start.19 = (bf16[512,2048]{1,0:T(8,128)(2,1)}, bf16[512,2048]{1,0:T(8,128)(2,1)}, u32[]{:S(2)}, u32[]{:S(2)}) collective-permute-start(bf16[512,2048]{1,0:T(8,128)(2,1)} %shard_map.104), channel_id=1, source_target_pairs={{0,2},{1,3},{2,0},{3,1},{4,6},{5,7},{6,4},{7,5}} | collective-permute-start | bytes 6291464 | tf_op jit(solution)/shard_map/ppermute | solution.py:178
  643.7 83.9 %collective-permute-start.37 = (f32[512,2048]{1,0:T(8,128)}, f32[512,2048]{1,0:T(8,128)}, u32[]{:S(2)}, u32[]{:S(2)}) collective-permute-start(f32[512,2048]{1,0:T(8,128)} %get-tuple-element.150), channel_id=1, source_target_pairs={{0,1},{1,0},{2,3},{3,2},{4,5},{5,4},{6,7},{7,6}} | collective-permute-start | bytes 12582920 | tf_op jit(solution)/shard_map/ppermute | solution.py:178
  643.8 83.9 %collective-permute-start.38 = (f32[2048,512]{1,0:T(8,128)}, f32[2048,512]{1,0:T(8,128)}, u32[]{:S(2)}, u32[]{:S(2)}) collective-permute-start(f32[2048,512]{1,0:T(8,128)} %get-tuple-element.151), channel_id=1, source_target_pairs={{0,1},{1,0},{2,3},{3,2},{4,5},{5,4},{6,7},{7,6}} | collective-permute-start | bytes 12582920 | tf_op jit(solution)/shard_map/ppermute | solution.py:178
  644.3 83.4 %collective-permute-start.33 = (bf16[2048,1024]{1,0:T(8,128)(2,1)}, bf16[2048,1024]{1,0:T(8,128)(2,1)}, u32[]{:S(2)}, u32[]{:S(2)}) collective-permute-start(bf16[2048,1024]{1,0:T(8,128)(2,1)} %get-tuple-element.146.refs_7_), channel_id=1, source_target_pairs={{0,1},{1,0},{2,3},{3,2},{4,5},{5,4},{6,7},{7,6}} | collective-permute-start | bytes 12582920 | tf_op jit(solution)/shard_map/ppermute | solution.py:178
  647.3 80.4 %collective-permute-start.34 = (bf16[1024,2048]{1,0:T(8,128)(2,1)}, bf16[1024,2048]{1,0:T(8,128)(2,1)}, u32[]{:S(2)}, u32[]{:S(2)}) collective-permute-start(bf16[1024,2048]{1,0:T(8,128)(2,1)} %get-tuple-element.147.refs_8_), channel_id=1, source_target_pairs={{0,1},{1,0},{2,3},{3,2},{4,5},{5,4},{6,7},{7,6}} | collective-permute-start | bytes 12582920 | tf_op jit(solution)/shard_map/ppermute | solution.py:178
  691.6 36.0 %collective-permute-start.35 = (bf16[1024,2048]{1,0:T(8,128)(2,1)}, bf16[1024,2048]{1,0:T(8,128)(2,1)}, u32[]{:S(2)}, u32[]{:S(2)}) collective-permute-start(bf16[1024,2048]{1,0:T(8,128)(2,1)} %get-tuple-element.148.refs_9_), channel_id=1, source_target_pairs={{0,1},{1,0},{2,3},{3,2},{4,5},{5,4},{6,7},{7,6}} | collective-permute-start | bytes 12582920 | tf_op jit(solution)/shard_map/ppermute | solution.py:178

commit v4 on v3

--- a/solution.py
+++ b/solution.py
@@ -123,7 +123,7 @@
             dy_sw[swapped, :] = dys[rows, :part]
 
     h, da, db = gated(a[...], b[...], mm(dys[...], wd[...], 1, 1))
-    h_out[...] = h.T
+    h_out[...] = h
     da_out[...] = da
     db_out[...] = db
 
@@ -136,7 +136,7 @@
         x, dy, h, da, db = (ref[...] for ref in refs[5 * n:5 * n + 5])
         dg += mm(x, da)
         du += mm(x, db)
-        dd += mm(h, dy)
+        dd += mm(h, dy, 0, 0)
     gate[...] = dg
     up[...] = du
     down[...] = dd
@@ -352,8 +352,8 @@
                 functools.partial(late_kernel, part),
                 grid=(ff // step,),
                 in_specs=blk + every[2:] + [ab_block] * 2 + [pl.BlockSpec((part, 2 * rows), fixed, pipeline_mode=once)],
-                out_specs=[pl.BlockSpec((step, 2 * rows), lambda j: (j, 0))] + [ab_block] * 2 + [pl.BlockSpec((part, 2 * rows), fixed), pl.BlockSpec((2 * rows, part), fixed)] * 2,
-                out_shape=[jax.ShapeDtypeStruct((ff, 2 * rows), bf16)] + [jax.ShapeDtypeStruct((2 * rows, ff), bf16)] * 2 + [jax.ShapeDtypeStruct((part, 2 * rows), bf16), jax.ShapeDtypeStruct((2 * rows, part), bf16)] * 2,
+                out_specs=[ab_block] * 3 + [pl.BlockSpec((part, 2 * rows), fixed), pl.BlockSpec((2 * rows, part), fixed)] * 2,
+                out_shape=[jax.ShapeDtypeStruct((2 * rows, ff), bf16)] * 3 + [jax.ShapeDtypeStruct((part, 2 * rows), bf16), jax.ShapeDtypeStruct((2 * rows, part), bf16)] * 2,
                 scratch_shapes=[pltpu.VMEM((2 * rows, d_model), bf16)],
                 compiler_params=params,
                 cost_estimate=cost(2 * 2 * rows * d_model * ff),
@@ -370,7 +370,7 @@
         for before, side, parts in stages:
             late_specs = []
             for size in groups:
-                late_specs += [pl.BlockSpec((part, 2 * size), lambda j, c: (0, 0), pipeline_mode=once), pl.BlockSpec((2 * size, part), lambda j, c: (0, 0), pipeline_mode=once), pl.BlockSpec((unit, 2 * size), lambda j, c: (j, 0))] + [pl.BlockSpec((2 * size, unit), lambda j, c: (0, j))] * 2
+                late_specs += [pl.BlockSpec((part, 2 * size), lambda j, c: (0, 0), pipeline_mode=once), pl.BlockSpec((2 * size, part), lambda j, c: (0, 0), pipeline_mode=once), pl.BlockSpec((2 * size, unit), lambda j, c: (0, j))] + [pl.BlockSpec((2 * size, unit), lambda j, c: (0, j))] * 2
             place_at = lambda j, c: c[0] * units + j
             finals = pl.pallas_call(
                 functools.partial(last_kernel, count),

time: 755 us -> 755 us (level)
  no operation moved by 1% of the time
where the time goes in v4:
time: 755 us; the launch traced here: 751 us
  Pallas kernels  390 us (52%)
  waiting for transfers between devices  316 us (42%)
  starting transfers between devices  22.3 us (3%)
  other arithmetic  12.6 us (2%)
  local copies, waits for them, and re-layouts  8.88 us (1%)
    ppermute x39, waiting for transfers between devices, flip(): return lax.ppermute(value, AXES, [(i, i ^ mask) for i in range(8)])  316 us
    pallas_call x4, Pallas kernels, local_step(): pl.pallas_call(functools.partial(own_kernel, half), grid=(own_count // TI...  119 us
    pallas_call x4, Pallas kernels, sums(): pl.pallas_call(functools.partial(sum_kernel, down, before is not None), g...  71.4 us
    pallas_call x2, Pallas kernels, local_step(): pl.pallas_call(functools.partial(last_kernel, count), grid_spec=pltpu.Pre...  46.6 us
    pallas_call x2, Pallas kernels, gate_up(): pl.pallas_call(gate_up_kernel, grid=(ff // step,), in_specs=blk + every[:...  46.3 us
    pallas_call x2, Pallas kernels, local_step(): pl.pallas_call(functools.partial(late_kernel, part), grid=(ff // step,),...  39.8 us
    pallas_call x2, Pallas kernels, close(): pl.pallas_call(close_kernel, grid=(2 * rows // TILE,), in_specs=[act] * 3...  31.1 us
    ppermute x39, starting transfers between devices, flip(): return lax.ppermute(value, AXES, [(i, i ^ mask) for i in range(8)])  22.3 us
  transfers between devices with their start and end apart: 39, of which 9 were waited for; matrix products, arithmetic and copies ran while one was open for 2% of the time, Pallas kernels for 49%

profile of v4, /device:TPU:0, one launch (start us, length us, event | category | flops | bytes accessed | tf_op | source)
XLA Modules:
  0.0 751.2 jit_solution(17042439806580553012)
XLA Ops:
  0.7 2.5 constant_dynamic-slice_fusion.27
  3.4 1.8 pad_maximum_fusion.refs_0_.residual
  5.2 3.3 collective-permute-start.3
  8.6 46.6 %collective-permute-done.3.refs_1_ = bf16[512,2048]{1,0:T(8,128)(2,1)} collective-permute-done((bf16[512,2048]{1,0:T(8,128)(2,1)S(1)}, bf16[512,2048]{1,0:T(8,128)(2,1)}, u32[]{:S(2)}, u32[]{:S(2)}) %collective-permute-start.3) | collective-permute-done | bytes 2097184 | tf_op jit(solution)/shard_map/ppermute | solution.py:178
  55.6 3.6 constant_dynamic-slice_fusion.2
  59.2 1.5 copy-done.3
  60.8 1.3 constant_dynamic-slice_fusion
  62.1 37.1 %collective-permute-done.refs_1_ = bf16[512,2048]{1,0:T(8,128)(2,1)} collective-permute-done((bf16[512,2048]{1,0:T(8,128)(2,1)}, bf16[512,2048]{1,0:T(8,128)(2,1)}, u32[]{:S(2)}, u32[]{:S(2)}) %collective-permute-start) | collective-permute-done | bytes 2097184 | tf_op jit(solution)/shard_map/ppermute | solution.py:178
  99.2 2.3 pad_maximum_fusion.9
  102.0 1.3 pad_maximum_fusion.8.refs_2_
  103.3 1.4 collective-permute-start.17
  106.4 1.3 pad_maximum_fusion.6.refs_2_
  107.6 1.3 pad_maximum_fusion.4.refs_2_
  111.5 7.6 %shard_map.93 = bf16[4,512,2048]{2,1,0:T(8,128)(2,1)} custom-call(bf16[512,2048]{1,0:T(8,128)(2,1)} %copy-done, bf16[512,2048]{1,0:T(8,128)(2,1)} %collective-permute-done.3.refs_1_, bf16[512,2048]{1,0:T(8,128)(2,1)} %collective-permute-done.4.refs_2_, bf16[512,2048]{1,0:T(8,128)(2,1)} %collective-permute-done.5.refs_3_), custom_call_target="tpu_custom_call" | custom-call | flops 1000000 | bytes 16777216 | tf_op jit(solution)/shard_map/pallas_call | solution.py:164
  119.2 1.6 collective-permute-start.14
  120.9 7.0 shard_map.92
  128.0 46.4 %collective-permute-done.16.refs_4_ = bf16[1536,512]{1,0:T(8,128)(2,1)} collective-permute-done((bf16[1536,512]{1,0:T(8,128)(2,1)}, bf16[1536,512]{1,0:T(8,128)(2,1)}, u32[]{:S(2)}, u32[]{:S(2)}) %collective-permute-start.16) | collective-permute-done | bytes 1572896 | tf_op jit(solution)/shard_map/ppermute | solution.py:178
  174.4 1.6 collective-permute-start.13
  176.0 29.6 %shard_map.94 = (bf16[2048,2048]{1,0:T(8,128)(2,1)}, bf16[2048,2048]{1,0:T(8,128)(2,1)}, bf16[2048,2048]{1,0:T(8,128)(2,1)}, bf16[2048,2048]{1,0:T(8,128)(2,1)},...) custom-call(bf16[2048,2048]{1,0:T(8,128)(2,1)} %bitcast.8, ...), custom_call_target="tpu_custom_call" | custom-call | flops 19327352832 | bytes 52428800 | tf_op jit(solution)/shard_map/pallas_call | solution.py:257
  205.9 69.3 %collective-permute-done.13.refs_4_ = bf16[1536,512]{1,0:T(8,128)(2,1)} collective-permute-done((bf16[1536,512]{1,0:T(8,128)(2,1)}, bf16[1536,512]{1,0:T(8,128)(2,1)}, u32[]{:S(2)}, u32[]{:S(2)}) %collective-permute-start.13) | collective-permute-done | bytes 1572896 | tf_op jit(solution)/shard_map/ppermute | solution.py:178
  275.1 1.3 collective-permute-start.8
  276.9 29.8 %shard_map.95 = (bf16[2048,2048]{1,0:T(8,128)(2,1)}, bf16[2048,2048]{1,0:T(8,128)(2,1)}, bf16[2048,2048]{1,0:T(8,128)(2,1)}, bf16[2048,2048]{1,0:T(8,128)(2,1)},...) custom-call(bf16[2048,2048]{1,0:T(8,128)(2,1)} %bitcast.9, ...), custom_call_target="tpu_custom_call", output_to_operand_aliasing={{0}: (6, {}), {1}: (7, {}), {2}: (8, {}), {3}: (9, {}), {4}... | custom-call | flops 19327352832 | bytes 52428800 | tf_op jit(solution)/shard_map/pallas_call | solution.py:257
  306.7 14.1 %shard_map.98.refs_2_ = f32[2048,2048]{1,0:T(8,128)} custom-call(bf16[2048,2048]{1,0:T(8,128)(2,1)} %get-tuple-element.99.refs_6_.refs_0_, bf16[2048,2048]{1,0:T(8,128)(2,1)} %get-tuple-element.104.refs_11_.refs_1_), custom_call_target="tpu_custom_call" | custom-call | flops 8589934592 | bytes 52428800 | tf_op jit(solution)/shard_map/pallas_call | solution.py:238
  320.8 24.2 %shard_map.100.refs_4_ = f32[2048,2048]{1,0:T(8,128)} custom-call(bf16[2048,2048]{1,0:T(8,128)(2,1)} %get-tuple-element.100.refs_7_.refs_0_, bf16[2048,2048]{1,0:T(8,128)(2,1)} %get-tuple-element.101.refs_8_.refs_1_, bf16[2048,2048]{1,0:T(8,128)(2,1)} %get-tuple-element.102.refs_9_.refs_2_, bf16[2048,2048]{1,0:T(8,128)(2,1)} %get-tuple-element.103.refs_10_.refs_3_), custom_call_target="tpu_custom_call" | custom-call | flops 17179869184 | bytes 52428800 | tf_op jit(solution)/shard_map/pallas_call | solution.py:238
  345.9 1.8 collective-permute-start.24
  347.9 1.8 collective-permute-start.7
  349.7 29.8 %shard_map.96 = (bf16[2048,2048]{1,0:T(8,128)(2,1)}, bf16[2048,2048]{1,0:T(8,128)(2,1)}, bf16[2048,2048]{1,0:T(8,128)(2,1)}, bf16[2048,2048]{1,0:T(8,128)(2,1)},...) custom-call(bf16[2048,2048]{1,0:T(8,128)(2,1)} %bitcast.10, ...), custom_call_target="tpu_custom_call", output_to_operand_aliasing={{0}: (6, {}), {1}: (7, {}), {2}: (8, {}), {3}: (9, {}), {4}... | custom-call | flops 19327352832 | bytes 52428800 | tf_op jit(solution)/shard_map/pallas_call | solution.py:257
  379.5 14.2 %shard_map.99.y_old = f32[2048,2048]{1,0:T(8,128)} custom-call(bf16[2048,2048]{1,0:T(8,128)(2,1)} %get-tuple-element.111.refs_6_.refs_0_, bf16[2048,2048]{1,0:T(8,128)(2,1)} %get-tuple-element.116.refs_11_.refs_1_, f32[2048,2048]{1,0:T(8,128)} %shard_map.98.refs_2_), custom_call_target="tpu_custom_call" | custom-call | flops 4294967296 | bytes 52428800 | tf_op jit(solution)/shard_map/pallas_call | solution.py:238
  393.6 19.0 %shard_map.101.dx_old = f32[2048,2048]{1,0:T(8,128)} custom-call(bf16[2048,2048]{1,0:T(8,128)(2,1)} %get-tuple-element.112.refs_7_.refs_0_, bf16[2048,2048]{1,0:T(8,128)(2,1)} %get-tuple-element.113.refs_8_.refs_1_, bf16[2048,2048]{1,0:T(8,128)(2,1)} %get-tuple-element.114.refs_9_.refs_2_, bf16[2048,2048]{1,0:T(8,128)(2,1)} %get-tuple-element.115.refs_10_.refs_3_, ...), custom_call_target="tpu_custom_call" | custom-call | flops 8589934592 | bytes 52428800 | tf_op jit(solution)/shard_map/pallas_call | solution.py:238
  412.9 1.7 collective-permute-start.31
  414.6 58.7 %collective-permute-done.7.refs_4_ = bf16[1536,512]{1,0:T(8,128)(2,1)} collective-permute-done((bf16[1536,512]{1,0:T(8,128)(2,1)S(1)}, bf16[1536,512]{1,0:T(8,128)(2,1)}, u32[]{:S(2)}, u32[]{:S(2)}) %collective-permute-start.7) | collective-permute-done | bytes 1572896 | tf_op jit(solution)/shard_map/ppermute | solution.py:178
  473.8 29.9 %shard_map.97 = (bf16[2048,2048]{1,0:T(8,128)(2,1)}, bf16[2048,2048]{1,0:T(8,128)(2,1)}, bf16[2048,2048]{1,0:T(8,128)(2,1)}, bf16[2048,2048]{1,0:T(8,128)(2,1)},...) custom-call(bf16[2048,2048]{1,0:T(8,128)(2,1)} %bitcast.11, ...), custom_call_target="tpu_custom_call", output_to_operand_aliasing={{0}: (6, {}), {1}: (7, {}), {2}: (8, {}), {3}: (9, {}), {4}... | custom-call | flops 19327352832 | bytes 52428800 | tf_op jit(solution)/shard_map/pallas_call | solution.py:257
  503.7 15.6 %shard_map.103 = (bf16[1024,2048]{1,0:T(8,128)(2,1)}, bf16[1024,2048]{1,0:T(8,128)(2,1)}) custom-call(bf16[2048,2048]{1,0:T(8,128)(2,1)} %get-tuple-element.123.h, bf16[2048,2048]{1,0:T(8,128)(2,1)} %get-tuple-element.124.da, bf16[2048,2048]{1,0:T(8,128)(2,1)} %get-tuple-element.125.db, bf16[2048,2048]{1,0:T(8,128)(2,1)} %get-tuple-element.126.wg, ...), custom_call_target="tpu_custom_call" | custom-call | flops 6442450944 | bytes 52428800 | tf_op jit(solution)/shard_map/pallas_call | solution.py:278
  519.9 23.1 %shard_map.108 = (bf16[1024,2048]{1,0:T(8,128)(2,1)}, bf16[1024,2048]{1,0:T(8,128)(2,1)}, bf16[1024,1024]{1,0:T(8,128)(2,1)}) custom-call(bf16[512,2048]{1,0:T(8,128)(2,1)} %collective-permute-done.24.xd, bf16[512,2048]{1,0:T(8,128)(2,1)} %collective-permute-done.25.xp, bf16[2048,2048]{1,0:T(8,128)(2,1)} %get-tuple-element.126.wg, ...), custom_call_target="tpu_custom_call" | custom-call | flops 17179869184 | bytes 52428800 | tf_op jit(solution)/shard_map/pallas_call | solution.py:336
  543.0 20.0 %shard_map.109 = (bf16[1024,2048]{1,0:T(8,128)(2,1)}, bf16[1024,2048]{1,0:T(8,128)(2,1)}, bf16[1024,2048]{1,0:T(8,128)(2,1)}, bf16[512,1024]{1,0:T(8,128)(2,1)},...) custom-call(bf16[512,2048]{1,0:T(8,128)(2,1)} %collective-permute-done.22.dyd, ...), custom_call_target="tpu_custom_call" | custom-call | flops 8589934592 | bytes 52428800 | tf_op jit(solution)/shard_map/pallas_call | solution.py:351
  563.6 9.9 %collective-permute-done.32.xp = bf16[512,2048]{1,0:T(8,128)(2,1)} collective-permute-done((bf16[512,2048]{1,0:T(8,128)(2,1)}, bf16[512,2048]{1,0:T(8,128)(2,1)}, u32[]{:S(2)}, u32[]{:S(2)}) %collective-permute-start.32) | collective-permute-done | bytes 2097184 | tf_op jit(solution)/shard_map/ppermute | solution.py:178
  574.2 15.4 %shard_map.102 = (bf16[1024,2048]{1,0:T(8,128)(2,1)}, bf16[1024,2048]{1,0:T(8,128)(2,1)}) custom-call(bf16[2048,2048]{1,0:T(8,128)(2,1)} %get-tuple-element.123.h, bf16[2048,2048]{1,0:T(8,128)(2,1)} %get-tuple-element.124.da, bf16[2048,2048]{1,0:T(8,128)(2,1)} %get-tuple-element.125.db, bf16[2048,2048]{1,0:T(8,128)(2,1)} %get-tuple-element.126.wg, ...), custom_call_target="tpu_custom_call" | custom-call | flops 6442450944 | bytes 52428800 | tf_op jit(solution)/shard_map/pallas_call | solution.py:278
  589.6 4.3 shard_map.106
  593.9 4.3 shard_map.104
  598.2 1.7 collective-permute-start.21
  600.3 23.1 %shard_map.110 = (bf16[1024,2048]{1,0:T(8,128)(2,1)}, bf16[1024,2048]{1,0:T(8,128)(2,1)}, bf16[1024,1024]{1,0:T(8,128)(2,1)}) custom-call(bf16[512,2048]{1,0:T(8,128)(2,1)} %collective-permute-done.31.xd, bf16[512,2048]{1,0:T(8,128)(2,1)} %collective-permute-done.32.xp, bf16[2048,2048]{1,0:T(8,128)(2,1)} %get-tuple-element.126.wg, ...), custom_call_target="tpu_custom_call" | custom-call | flops 17179869184 | bytes 52428800 | tf_op jit(solution)/shard_map/pallas_call | solution.py:336
  623.4 19.9 %shard_map.111 = (bf16[1024,2048]{1,0:T(8,128)(2,1)}, bf16[1024,2048]{1,0:T(8,128)(2,1)}, bf16[1024,2048]{1,0:T(8,128)(2,1)}, bf16[512,1024]{1,0:T(8,128)(2,1)},...) custom-call(bf16[512,2048]{1,0:T(8,128)(2,1)} %collective-permute-done.29.dyd, ...), custom_call_target="tpu_custom_call" | custom-call | flops 8589934592 | bytes 52428800 | tf_op jit(solution)/shard_map/pallas_call | solution.py:351
  643.9 3.2 collective-permute-done.21.far
  647.1 44.3 %collective-permute-done.19.far = bf16[512,2048]{1,0:T(8,128)(2,1)} collective-permute-done((bf16[512,2048]{1,0:T(8,128)(2,1)}, bf16[512,2048]{1,0:T(8,128)(2,1)}, u32[]{:S(2)}, u32[]{:S(2)}) %collective-permute-start.19) | collective-permute-done | bytes 2097184 | tf_op jit(solution)/shard_map/ppermute | solution.py:178
  691.9 23.3 %shard_map.112 = (f32[512,4096]{1,0:T(8,128)}, f32[512,4096]{1,0:T(8,128)}, f32[4096,512]{1,0:T(8,128)}) custom-call(s32[1]{0:T(128)} %bitcast.3.where, bf16[512,1024]{1,0:T(8,128)(2,1)} %get-tuple-element.152.refs_0_, bf16[1024,512]{1,0:T(8,128)(2,1)} %get-tuple-element.153.refs_1_, bf16[1024,2048]{1,0:T(8,128)(2,1)} %get-tuple-element.138.refs_2_, ...), custom_call_target="tpu_custom_call" | custom-call | flops 12884901888 | bytes 52428800 | tf_op jit(solution)/shard_map/pallas_call | solution.py:375
  715.2 6.2 shard_map.107
  721.4 6.2 shard_map.105
  727.6 23.3 %shard_map.113 = (f32[512,4096]{1,0:T(8,128)}, f32[512,4096]{1,0:T(8,128)}, f32[4096,512]{1,0:T(8,128)}) custom-call(s32[1]{0:T(128)} %bitcast.2.where, bf16[512,1024]{1,0:T(8,128)(2,1)} %get-tuple-element.136.refs_0_, bf16[1024,512]{1,0:T(8,128)(2,1)} %get-tuple-element.137.refs_1_, ...), custom_call_target="tpu_custom_call", output_to_operand_aliasing={{0}: (14, {}), {1}: (15, {}), {2}: (16, {})} | custom-call | flops 12884901888 | bytes 52428800 | tf_op jit(solution)/shard_map/pallas_call | solution.py:375
  (76 shorter events, 11.6 us)
Async XLA Ops:
  3.4 55.8 %copy-start = (bf16[512,2048]{1,0:T(8,128)(2,1)}, bf16[512,2048]{1,0:T(8,128)(2,1)S(1)}, u32[]{:S(2)}) copy-start(bf16[512,2048]{1,0:T(8,128)(2,1)S(1)} %pad_maximum_fusion.1.refs_0_.residual) | copy-start | bytes 6291460
  5.2 49.9 %collective-permute-start.3 = (bf16[512,2048]{1,0:T(8,128)(2,1)S(1)}, bf16[512,2048]{1,0:T(8,128)(2,1)}, u32[]{:S(2)}, u32[]{:S(2)}) collective-permute-start(bf16[512,2048]{1,0:T(8,128)(2,1)S(1)} %pad_maximum_fusion.1.refs_0_.residual), channel_id=1, source_target_pairs={{0,2},{1,3},{2,0},{3,1},{4,6},{5,7},{6,4},{7,5}} | collective-permute-start | bytes 6291464 | tf_op jit(solution)/shard_map/ppermute | solution.py:178
  8.5 90.7 %collective-permute-start = (bf16[512,2048]{1,0:T(8,128)(2,1)}, bf16[512,2048]{1,0:T(8,128)(2,1)}, u32[]{:S(2)}, u32[]{:S(2)}) collective-permute-start(bf16[512,2048]{1,0:T(8,128)(2,1)} %pad_maximum_fusion.refs_0_.residual), channel_id=1, source_target_pairs={{0,2},{1,3},{2,0},{3,1},{4,6},{5,7},{6,4},{7,5}} | collective-permute-start | bytes 6291464 | tf_op jit(solution)/shard_map/ppermute | solution.py:178
  8.6 94.7 %collective-permute-start.4 = (bf16[512,2048]{1,0:T(8,128)(2,1)S(1)}, bf16[512,2048]{1,0:T(8,128)(2,1)}, u32[]{:S(2)}, u32[]{:S(2)}) collective-permute-start(bf16[512,2048]{1,0:T(8,128)(2,1)S(1)} %pad_maximum_fusion.1.refs_0_.residual), channel_id=1, source_target_pairs={{0,1},{1,0},{2,3},{3,2},{4,5},{5,4},{6,7},{7,6}} | collective-permute-start | bytes 6291464 | tf_op jit(solution)/shard_map/ppermute | solution.py:178
  55.1 49.6 %collective-permute-start.5 = (bf16[512,2048]{1,0:T(8,128)(2,1)}, bf16[512,2048]{1,0:T(8,128)(2,1)}, u32[]{:S(2)}, u32[]{:S(2)}) collective-permute-start(bf16[512,2048]{1,0:T(8,128)(2,1)} %collective-permute-done.3.refs_1_), channel_id=1, source_target_pairs={{0,1},{1,0},{2,3},{3,2},{4,5},{5,4},{6,7},{7,6}} | collective-permute-start | bytes 6291464 | tf_op jit(solution)/shard_map/ppermute | solution.py:178
  55.1 64.0 %collective-permute-start.1 = (bf16[512,2048]{1,0:T(8,128)(2,1)}, bf16[512,2048]{1,0:T(8,128)(2,1)}, u32[]{:S(2)}, u32[]{:S(2)}) collective-permute-start(bf16[512,2048]{1,0:T(8,128)(2,1)} %pad_maximum_fusion.refs_0_.residual), channel_id=1, source_target_pairs={{0,1},{1,0},{2,3},{3,2},{4,5},{5,4},{6,7},{7,6}} | collective-permute-start | bytes 6291464 | tf_op jit(solution)/shard_map/ppermute | solution.py:178
  55.6 3.6 copy-start.2
  55.6 5.1 copy-start.3
  62.1 40.0 %copy-start.4 = (bf16[512,512]{1,0:T(8,128)(2,1)S(1)}, bf16[512,512]{1,0:T(8,128)(2,1)}, u32[]{:S(2)}) copy-start(bf16[512,512]{1,0:T(8,128)(2,1)} %get-tuple-element.172) | copy-start | bytes 1572868
  99.2 20.0 %collective-permute-start.2 = (bf16[512,2048]{1,0:T(8,128)(2,1)}, bf16[512,2048]{1,0:T(8,128)(2,1)}, u32[]{:S(2)}, u32[]{:S(2)}) collective-permute-start(bf16[512,2048]{1,0:T(8,128)(2,1)} %collective-permute-done.refs_1_), channel_id=1, source_target_pairs={{0,1},{1,0},{2,3},{3,2},{4,5},{5,4},{6,7},{7,6}} | collective-permute-start | bytes 6291464 | tf_op jit(solution)/shard_map/ppermute | solution.py:178
  101.5 26.4 %collective-permute-start.15 = (bf16[1536,512]{1,0:T(8,128)(2,1)}, bf16[1536,512]{1,0:T(8,128)(2,1)}, u32[]{:S(2)}, u32[]{:S(2)}) collective-permute-start(bf16[1536,512]{1,0:T(8,128)(2,1)} %pad_maximum_fusion.9), channel_id=1, source_target_pairs={{0,1},{1,0},{2,3},{3,2},{4,5},{5,4},{6,7},{7,6}} | collective-permute-start | bytes 4718600 | tf_op jit(solution)/shard_map/ppermute | solution.py:178
  103.3 71.0 %collective-permute-start.17 = (bf16[1536,512]{1,0:T(8,128)(2,1)}, bf16[1536,512]{1,0:T(8,128)(2,1)}, u32[]{:S(2)}, u32[]{:S(2)}) collective-permute-start(bf16[1536,512]{1,0:T(8,128)(2,1)} %pad_maximum_fusion.9), channel_id=1, source_target_pairs={{0,5},{1,4},{2,7},{3,6},{4,1},{5,0},{6,3},{7,2}} | collective-permute-start | bytes 4718600 | tf_op jit(solution)/shard_map/ppermute | solution.py:178
  104.7 69.7 %collective-permute-start.16 = (bf16[1536,512]{1,0:T(8,128)(2,1)}, bf16[1536,512]{1,0:T(8,128)(2,1)}, u32[]{:S(2)}, u32[]{:S(2)}) collective-permute-start(bf16[1536,512]{1,0:T(8,128)(2,1)} %pad_maximum_fusion.8.refs_2_), channel_id=1, source_target_pairs={{0,4},{1,5},{2,6},{3,7},{4,0},{5,1},{6,2},{7,3}} | collective-permute-start | bytes 4718600 | tf_op jit(solution)/shard_map/ppermute | solution.py:178
  111.5 236.4 %copy-start.1 = (bf16[1536,512]{1,0:T(8,128)(2,1)}, bf16[1536,512]{1,0:T(8,128)(2,1)S(1)}, u32[]{:S(2)}) copy-start(bf16[1536,512]{1,0:T(8,128)(2,1)S(1)} %pad_maximum_fusion.2.refs_2_) | copy-start | bytes 4718596
  119.1 86.5 %collective-permute-start.12 = (bf16[1536,512]{1,0:T(8,128)(2,1)}, bf16[1536,512]{1,0:T(8,128)(2,1)}, u32[]{:S(2)}, u32[]{:S(2)}) collective-permute-start(bf16[1536,512]{1,0:T(8,128)(2,1)} %pad_maximum_fusion.7), channel_id=1, source_target_pairs={{0,1},{1,0},{2,3},{3,2},{4,5},{5,4},{6,7},{7,6}} | collective-permute-start | bytes 4718600 | tf_op jit(solution)/shard_map/ppermute | solution.py:178
  119.2 157.2 %collective-permute-start.14 = (bf16[1536,512]{1,0:T(8,128)(2,1)}, bf16[1536,512]{1,0:T(8,128)(2,1)}, u32[]{:S(2)}, u32[]{:S(2)}) collective-permute-start(bf16[1536,512]{1,0:T(8,128)(2,1)} %pad_maximum_fusion.7), channel_id=1, source_target_pairs={{0,5},{1,4},{2,7},{3,6},{4,1},{5,0},{6,3},{7,2}} | collective-permute-start | bytes 4718600 | tf_op jit(solution)/shard_map/ppermute | solution.py:178
  127.9 219.8 %collective-permute-start.11 = (bf16[1536,512]{1,0:T(8,128)(2,1)}, bf16[1536,512]{1,0:T(8,128)(2,1)}, u32[]{:S(2)}, u32[]{:S(2)}) collective-permute-start(bf16[1536,512]{1,0:T(8,128)(2,1)} %pad_maximum_fusion.5), channel_id=1, source_target_pairs={{0,5},{1,4},{2,7},{3,6},{4,1},{5,0},{6,3},{7,2}} | collective-permute-start | bytes 4718600 | tf_op jit(solution)/shard_map/ppermute | solution.py:178
  174.4 173.5 %collective-permute-start.9 = (bf16[1536,512]{1,0:T(8,128)(2,1)}, bf16[1536,512]{1,0:T(8,128)(2,1)}, u32[]{:S(2)}, u32[]{:S(2)}) collective-permute-start(bf16[1536,512]{1,0:T(8,128)(2,1)} %pad_maximum_fusion.5), channel_id=1, source_target_pairs={{0,1},{1,0},{2,3},{3,2},{4,5},{5,4},{6,7},{7,6}} | collective-permute-start | bytes 4718600 | tf_op jit(solution)/shard_map/ppermute | solution.py:178
  174.4 100.8 %collective-permute-start.13 = (bf16[1536,512]{1,0:T(8,128)(2,1)}, bf16[1536,512]{1,0:T(8,128)(2,1)}, u32[]{:S(2)}, u32[]{:S(2)}) collective-permute-start(bf16[1536,512]{1,0:T(8,128)(2,1)} %pad_maximum_fusion.6.refs_2_), channel_id=1, source_target_pairs={{0,4},{1,5},{2,6},{3,7},{4,0},{5,1},{6,2},{7,3}} | collective-permute-start | bytes 4718600 | tf_op jit(solution)/shard_map/ppermute | solution.py:178
  205.6 207.0 %collective-permute-start.6 = (bf16[1536,512]{1,0:T(8,128)(2,1)}, bf16[1536,512]{1,0:T(8,128)(2,1)}, u32[]{:S(2)}, u32[]{:S(2)}) collective-permute-start(bf16[1536,512]{1,0:T(8,128)(2,1)} %pad_maximum_fusion.3), channel_id=1, source_target_pairs={{0,1},{1,0},{2,3},{3,2},{4,5},{5,4},{6,7},{7,6}} | collective-permute-start | bytes 4718600 | tf_op jit(solution)/shard_map/ppermute | solution.py:178
  275.1 198.7 %collective-permute-start.8 = (bf16[1536,512]{1,0:T(8,128)(2,1)}, bf16[1536,512]{1,0:T(8,128)(2,1)}, u32[]{:S(2)}, u32[]{:S(2)}) collective-permute-start(bf16[1536,512]{1,0:T(8,128)(2,1)} %pad_maximum_fusion.3), channel_id=1, source_target_pairs={{0,5},{1,4},{2,7},{3,6},{4,1},{5,0},{6,3},{7,2}} | collective-permute-start | bytes 4718600 | tf_op jit(solution)/shard_map/ppermute | solution.py:178
  276.5 69.4 %collective-permute-start.10 = (bf16[1536,512]{1,0:T(8,128)(2,1)}, bf16[1536,512]{1,0:T(8,128)(2,1)}, u32[]{:S(2)}, u32[]{:S(2)}) collective-permute-start(bf16[1536,512]{1,0:T(8,128)(2,1)} %pad_maximum_fusion.4.refs_2_), channel_id=1, source_target_pairs={{0,4},{1,5},{2,6},{3,7},{4,0},{5,1},{6,2},{7,3}} | collective-permute-start | bytes 4718600 | tf_op jit(solution)/shard_map/ppermute | solution.py:178
  345.9 67.0 %collective-permute-start.24 = (bf16[512,2048]{1,0:T(8,128)(2,1)}, bf16[512,2048]{1,0:T(8,128)(2,1)}, u32[]{:S(2)}, u32[]{:S(2)}) collective-permute-start(bf16[512,2048]{1,0:T(8,128)(2,1)} %pad_maximum_fusion.refs_0_.residual), channel_id=1, source_target_pairs={{0,4},{1,5},{2,6},{3,7},{4,0},{5,1},{6,2},{7,3}} | collective-permute-start | bytes 6291464 | tf_op jit(solution)/shard_map/ppermute | solution.py:178
  347.6 125.7 %collective-permute-start.22 = (bf16[512,2048]{1,0:T(8,128)(2,1)}, bf16[512,2048]{1,0:T(8,128)(2,1)}, u32[]{:S(2)}, u32[]{:S(2)}) collective-permute-start(bf16[512,2048]{1,0:T(8,128)(2,1)} %copy-done), channel_id=1, source_target_pairs={{0,4},{1,5},{2,6},{3,7},{4,0},{5,1},{6,2},{7,3}} | collective-permute-start | bytes 6291464 | tf_op jit(solution)/shard_map/ppermute | solution.py:178
  347.9 125.4 %collective-permute-start.7 = (bf16[1536,512]{1,0:T(8,128)(2,1)S(1)}, bf16[1536,512]{1,0:T(8,128)(2,1)}, u32[]{:S(2)}, u32[]{:S(2)}) collective-permute-start(bf16[1536,512]{1,0:T(8,128)(2,1)S(1)} %pad_maximum_fusion.2.refs_2_), channel_id=1, source_target_pairs={{0,4},{1,5},{2,6},{3,7},{4,0},{5,1},{6,2},{7,3}} | collective-permute-start | bytes 4718600 | tf_op jit(solution)/shard_map/ppermute | solution.py:178
  412.6 150.9 %collective-permute-start.29 = (bf16[512,2048]{1,0:T(8,128)(2,1)}, bf16[512,2048]{1,0:T(8,128)(2,1)}, u32[]{:S(2)}, u32[]{:S(2)}) collective-permute-start(bf16[512,2048]{1,0:T(8,128)(2,1)} %collective-permute-done.3.refs_1_), channel_id=1, source_target_pairs={{0,4},{1,5},{2,6},{3,7},{4,0},{5,1},{6,2},{7,3}} | collective-permute-start | bytes 6291464 | tf_op jit(solution)/shard_map/ppermute | solution.py:178
  412.9 150.2 %collective-permute-start.31 = (bf16[512,2048]{1,0:T(8,128)(2,1)}, bf16[512,2048]{1,0:T(8,128)(2,1)}, u32[]{:S(2)}, u32[]{:S(2)}) collective-permute-start(bf16[512,2048]{1,0:T(8,128)(2,1)} %collective-permute-done.24.xd), channel_id=1, source_target_pairs={{0,2},{1,3},{2,0},{3,1},{4,6},{5,7},{6,4},{7,5}} | collective-permute-start | bytes 6291464 | tf_op jit(solution)/shard_map/ppermute | solution.py:178
  473.3 46.1 %collective-permute-start.25 = (bf16[512,2048]{1,0:T(8,128)(2,1)}, bf16[512,2048]{1,0:T(8,128)(2,1)}, u32[]{:S(2)}, u32[]{:S(2)}) collective-permute-start(bf16[512,2048]{1,0:T(8,128)(2,1)} %collective-permute-done.24.xd), channel_id=1, source_target_pairs={{0,1},{1,0},{2,3},{3,2},{4,5},{5,4},{6,7},{7,6}} | collective-permute-start | bytes 6291464 | tf_op jit(solution)/shard_map/ppermute | solution.py:178
  473.3 69.7 %collective-permute-start.23 = (bf16[512,2048]{1,0:T(8,128)(2,1)}, bf16[512,2048]{1,0:T(8,128)(2,1)}, u32[]{:S(2)}, u32[]{:S(2)}) collective-permute-start(bf16[512,2048]{1,0:T(8,128)(2,1)} %collective-permute-done.22.dyd), channel_id=1, source_target_pairs={{0,1},{1,0},{2,3},{3,2},{4,5},{5,4},{6,7},{7,6}} | collective-permute-start | bytes 6291464 | tf_op jit(solution)/shard_map/ppermute | solution.py:178
  519.3 54.3 %collective-permute-start.20 = (bf16[1024,2048]{1,0:T(8,128)(2,1)}, bf16[1024,2048]{1,0:T(8,128)(2,1)}, u32[]{:S(2)}, u32[]{:S(2)}) collective-permute-start(bf16[1024,2048]{1,0:T(8,128)(2,1)} %get-tuple-element.132), channel_id=1, source_target_pairs={{0,1},{1,0},{2,3},{3,2},{4,5},{5,4},{6,7},{7,6}} | collective-permute-start | bytes 12582920 | tf_op jit(solution)/shard_map/ppermute | solution.py:178
  519.4 54.6 %collective-permute-start.18 = (bf16[1024,2048]{1,0:T(8,128)(2,1)}, bf16[1024,2048]{1,0:T(8,128)(2,1)}, u32[]{:S(2)}, u32[]{:S(2)}) collective-permute-start(bf16[1024,2048]{1,0:T(8,128)(2,1)} %get-tuple-element.130), channel_id=1, source_target_pairs={{0,1},{1,0},{2,3},{3,2},{4,5},{5,4},{6,7},{7,6}} | collective-permute-start | bytes 12582920 | tf_op jit(solution)/shard_map/ppermute | solution.py:178
  563.0 37.0 %collective-permute-start.26 = (bf16[1024,2048]{1,0:T(8,128)(2,1)}, bf16[1024,2048]{1,0:T(8,128)(2,1)}, u32[]{:S(2)}, u32[]{:S(2)}) collective-permute-start(bf16[1024,2048]{1,0:T(8,128)(2,1)} %get-tuple-element.138.refs_2_), channel_id=1, source_target_pairs={{0,1},{1,0},{2,3},{3,2},{4,5},{5,4},{6,7},{7,6}} | collective-permute-start | bytes 12582920 | tf_op jit(solution)/shard_map/ppermute | solution.py:178
  563.1 10.5 %collective-permute-start.32 = (bf16[512,2048]{1,0:T(8,128)(2,1)}, bf16[512,2048]{1,0:T(8,128)(2,1)}, u32[]{:S(2)}, u32[]{:S(2)}) collective-permute-start(bf16[512,2048]{1,0:T(8,128)(2,1)} %collective-permute-done.31.xd), channel_id=1, source_target_pairs={{0,1},{1,0},{2,3},{3,2},{4,5},{5,4},{6,7},{7,6}} | collective-permute-start | bytes 6291464 | tf_op jit(solution)/shard_map/ppermute | solution.py:178
  563.5 34.7 %collective-permute-start.30 = (bf16[512,2048]{1,0:T(8,128)(2,1)}, bf16[512,2048]{1,0:T(8,128)(2,1)}, u32[]{:S(2)}, u32[]{:S(2)}) collective-permute-start(bf16[512,2048]{1,0:T(8,128)(2,1)} %collective-permute-done.29.dyd), channel_id=1, source_target_pairs={{0,1},{1,0},{2,3},{3,2},{4,5},{5,4},{6,7},{7,6}} | collective-permute-start | bytes 6291464 | tf_op jit(solution)/shard_map/ppermute | solution.py:178
  573.5 69.8 %collective-permute-start.27 = (bf16[1024,2048]{1,0:T(8,128)(2,1)}, bf16[1024,2048]{1,0:T(8,128)(2,1)}, u32[]{:S(2)}, u32[]{:S(2)}) collective-permute-start(bf16[1024,2048]{1,0:T(8,128)(2,1)} %get-tuple-element.139.refs_3_), channel_id=1, source_target_pairs={{0,1},{1,0},{2,3},{3,2},{4,5},{5,4},{6,7},{7,6}} | collective-permute-start | bytes 12582920 | tf_op jit(solution)/shard_map/ppermute | solution.py:178
  573.6 69.7 %collective-permute-start.28 = (bf16[1024,2048]{1,0:T(8,128)(2,1)}, bf16[1024,2048]{1,0:T(8,128)(2,1)}, u32[]{:S(2)}, u32[]{:S(2)}) collective-permute-start(bf16[1024,2048]{1,0:T(8,128)(2,1)} %get-tuple-element.140.refs_4_), channel_id=1, source_target_pairs={{0,1},{1,0},{2,3},{3,2},{4,5},{5,4},{6,7},{7,6}} | collective-permute-start | bytes 12582920 | tf_op jit(solution)/shard_map/ppermute | solution.py:178
  574.0 69.8 %collective-permute-start.36 = (f32[512,2048]{1,0:T(8,128)}, f32[512,2048]{1,0:T(8,128)}, u32[]{:S(2)}, u32[]{:S(2)}) collective-permute-start(f32[512,2048]{1,0:T(8,128)} %get-tuple-element.149), channel_id=1, source_target_pairs={{0,1},{1,0},{2,3},{3,2},{4,5},{5,4},{6,7},{7,6}} | collective-permute-start | bytes 12582920 | tf_op jit(solution)/shard_map/ppermute | solution.py:178
  598.2 48.8 %collective-permute-start.21 = (bf16[512,2048]{1,0:T(8,128)(2,1)}, bf16[512,2048]{1,0:T(8,128)(2,1)}, u32[]{:S(2)}, u32[]{:S(2)}) collective-permute-start(bf16[512,2048]{1,0:T(8,128)(2,1)} %shard_map.106), channel_id=1, source_target_pairs={{0,2},{1,3},{2,0},{3,1},{4,6},{5,7},{6,4},{7,5}} | collective-permute-start | bytes 6291464 | tf_op jit(solution)/shard_map/ppermute | solution.py:178
  600.0 91.4 %collective-permute-start.19 = (bf16[512,2048]{1,0:T(8,128)(2,1)}, bf16[512,2048]{1,0:T(8,128)(2,1)}, u32[]{:S(2)}, u32[]{:S(2)}) collective-permute-start(bf16[512,2048]{1,0:T(8,128)(2,1)} %shard_map.104), channel_id=1, source_target_pairs={{0,2},{1,3},{2,0},{3,1},{4,6},{5,7},{6,4},{7,5}} | collective-permute-start | bytes 6291464 | tf_op jit(solution)/shard_map/ppermute | solution.py:178
  643.3 84.3 %collective-permute-start.37 = (f32[512,2048]{1,0:T(8,128)}, f32[512,2048]{1,0:T(8,128)}, u32[]{:S(2)}, u32[]{:S(2)}) collective-permute-start(f32[512,2048]{1,0:T(8,128)} %get-tuple-element.150), channel_id=1, source_target_pairs={{0,1},{1,0},{2,3},{3,2},{4,5},{5,4},{6,7},{7,6}} | collective-permute-start | bytes 12582920 | tf_op jit(solution)/shard_map/ppermute | solution.py:178
  643.3 84.3 %collective-permute-start.38 = (f32[2048,512]{1,0:T(8,128)}, f32[2048,512]{1,0:T(8,128)}, u32[]{:S(2)}, u32[]{:S(2)}) collective-permute-start(f32[2048,512]{1,0:T(8,128)} %get-tuple-element.151), channel_id=1, source_target_pairs={{0,1},{1,0},{2,3},{3,2},{4,5},{5,4},{6,7},{7,6}} | collective-permute-start | bytes 12582920 | tf_op jit(solution)/shard_map/ppermute | solution.py:178
  643.8 83.8 %collective-permute-start.33 = (bf16[1024,2048]{1,0:T(8,128)(2,1)}, bf16[1024,2048]{1,0:T(8,128)(2,1)}, u32[]{:S(2)}, u32[]{:S(2)}) collective-permute-start(bf16[1024,2048]{1,0:T(8,128)(2,1)} %get-tuple-element.146.refs_7_), channel_id=1, source_target_pairs={{0,1},{1,0},{2,3},{3,2},{4,5},{5,4},{6,7},{7,6}} | collective-permute-start | bytes 12582920 | tf_op jit(solution)/shard_map/ppermute | solution.py:178
  647.1 80.6 %collective-permute-start.34 = (bf16[1024,2048]{1,0:T(8,128)(2,1)}, bf16[1024,2048]{1,0:T(8,128)(2,1)}, u32[]{:S(2)}, u32[]{:S(2)}) collective-permute-start(bf16[1024,2048]{1,0:T(8,128)(2,1)} %get-tuple-element.147.refs_8_), channel_id=1, source_target_pairs={{0,1},{1,0},{2,3},{3,2},{4,5},{5,4},{6,7},{7,6}} | collective-permute-start | bytes 12582920 | tf_op jit(solution)/shard_map/ppermute | solution.py:178
  691.4 36.2 %collective-permute-start.35 = (bf16[1024,2048]{1,0:T(8,128)(2,1)}, bf16[1024,2048]{1,0:T(8,128)(2,1)}, u32[]{:S(2)}, u32[]{:S(2)}) collective-permute-start(bf16[1024,2048]{1,0:T(8,128)(2,1)} %get-tuple-element.148.refs_9_), channel_id=1, source_target_pairs={{0,1},{1,0},{2,3},{3,2},{4,5},{5,4},{6,7},{7,6}} | collective-permute-start | bytes 12582920 | tf_op jit(solution)/shard_map/ppermute | solution.py:178
